TPU v7x, 32 devices: a whole 2x2x4 slice. The times are simulated.
32 devices in a mesh: dp: 8 (over y, x, core), opt: 4 (over z).
Axes of the slice: x: 2, y: 2, z: 4, core: 2. Of those that a mesh axis runs over, the one named last changes fastest.
Arguments:
- images: bfloat16 [256, 14, 14, 512], P(('dp', 'opt')), may hold values from -6 to 6
- cotangent: bfloat16 [256, 14, 14, 512], P(('dp', 'opt')), may hold values from -6 to 6
- counts: int32 [32], P(('dp', 'opt')), may hold values from 1 to 8, as said below
- rel_index: int32 [49, 49], replicated, may hold values from 0 to 168, as said below
- params: float32 [3158016], P('opt'), may hold values from -3 to 250
- moment1: float32 [3158016], P('opt'), may hold values from -3840 to 3840
- moment2: float32 [3158016], P('opt'), may hold values from 0 to 6400
- rates: float32 [15], replicated, may hold values from 0 to 1
Outputs:
- block_out: bfloat16 [256, 14, 14, 512], P(('dp', 'opt'))
- input_grad: float32 [256, 14, 14, 512], P(('dp', 'opt'))
- param_grad: float32 [3158016], P('opt')
- new_params: float32 [3158016], P('opt')
- new_moment1: float32 [3158016], P('opt')
- new_moment2: float32 [3158016], P('opt')
Inputs may be any that keep to these rules, and one draw needn't show every extreme that they name: `counts`: some device has 8 live images and another one in every draw. `rel_index`: two pairs of cells share a bucket exactly when their offsets within the window are equal.
All inputs are finite; a program needn't handle non-finite values.
Results may differ from a plain program's by a relative error of at most 0.02.
Values may be sent and summed in bfloat16 or wider, within the bound.
A program may use at most 256 MiB of HBM per device.

v0:
```python
import jax
import jax.numpy as jnp
from jax import lax
from jax.sharding import PartitionSpec as P

D = 512
HEADS = 16
HEAD_DIM = 32
HID = 2048
SIDE = 14
WIN = 7
SHIFT = 3
STEP = 2
TAB = 169


HIGH = lax.Precision.HIGHEST
DECAY = [0.0, 0.0, 0.05, 0.0, 0.0, 0.0, 0.05, 0.0, 0.0, 0.0, 0.05, 0.0, 0.05, 0.0, 0.0]


def group_starts():
    lengths = [D, D, 3 * D * D, D, D, TAB * HEADS, D * D, D, D, D, D * HID, HID, HID * D, D]
    starts = [0]
    for length in lengths:
        starts.append(starts[-1] + length)
    return starts


def region_map():
    cells = lax.iota(jnp.int32, SIDE)
    band = (cells >= SIDE - WIN).astype(jnp.int32) + (cells >= SIDE - SHIFT).astype(jnp.int32)
    return band[:, None] * 3 + band[None, :]


def layer_norm(field, gain, shift):
    center = jnp.mean(field, -1, keepdims=True)
    deviation = field - center
    spread = jnp.mean(deviation * deviation, -1, keepdims=True)
    return deviation * lax.rsqrt(spread + 1e-05) * gain + shift


def gelu_exact(value):
    return jax.nn.gelu(value, approximate=False)


def to_windows(field):
    count, side, width = (field.shape[0], field.shape[1], field.shape[-1])
    blocks = side // WIN
    field = field.reshape(count, blocks, WIN, blocks, WIN, width).transpose(0, 1, 3, 2, 4, 5)
    return field.reshape(count * blocks * blocks * WIN * WIN, width)


def from_windows(rows, count, side):
    blocks = side // WIN
    width = rows.shape[-1]
    field = rows.reshape(count, blocks, blocks, WIN, WIN, width).transpose(0, 1, 3, 2, 4, 5)
    return field.reshape(count, side, side, width)


def split_heads(rows, groups, span):
    return rows.reshape(groups, span, HEADS, HEAD_DIM).transpose(0, 2, 1, 3)


def join_heads(field):
    groups, span = (field.shape[0], field.shape[2])
    return field.transpose(0, 2, 1, 3).reshape(groups * span, D)


def adam_update(weights, first, second, grad, rates, start):
    index = start + lax.iota(jnp.int32, weights.shape[0])
    starts = group_starts()
    rate = jnp.zeros_like(weights) + rates[0]
    decay = jnp.zeros_like(weights)
    for group in range(1, len(starts)):
        after = index >= starts[group]
        rate = jnp.where(after, rates[group], rate)
        decay = jnp.where(after, DECAY[group], decay)
    first_new = 0.9 * first + 0.1 * grad
    second_new = 0.999 * second + 0.001 * grad * grad
    first_hat = first_new / (1.0 - 0.9**STEP)
    second_hat = second_new / (1.0 - 0.999**STEP)
    weights_new = weights - rate * (first_hat / (jnp.sqrt(second_hat) + 1e-08) + decay * weights)
    return (weights_new, first_new, second_new)


def local(images, cotangent, counts, rel_index, params, moment1, moment2, rates):
    f32 = jnp.float32
    bf16 = jnp.bfloat16
    shard_len = params.shape[0]
    opt_count = lax.axis_size("opt")
    total_len = shard_len * opt_count
    working = lax.all_gather(params.astype(bf16), "opt", axis=0, tiled=True)
    starts = group_starts()
    pieces = [working[starts[g] : starts[g + 1]] for g in range(14)]
    gain_one, bias_one, w_qkv, query_bias, value_bias, table, w_proj, proj_bias = pieces[:8]
    gain_two, bias_two, w_fc1, fc1_bias, w_fc2, fc2_bias = pieces[8:]
    w_qkv = w_qkv.reshape(D, 3 * D)
    w_query = w_qkv[:, :D]
    w_keys = w_qkv[:, D : 2 * D]
    w_values = w_qkv[:, 2 * D :]
    w_proj = w_proj.reshape(D, D)
    w_fc1 = w_fc1.reshape(D, HID)
    w_fc2 = w_fc2.reshape(HID, D)
    table = table.reshape(TAB, HEADS)
    count, side = (images.shape[0], images.shape[1])
    blocks = side // WIN
    windows = blocks * blocks
    span = WIN * WIN
    groups = count * windows
    rows_all = count * side * side
    scale = HEAD_DIM ** (-0.5)
    inputs = images.astype(f32).reshape(rows_all, D)
    norm_one, norm_one_back = jax.vjp(
        layer_norm, inputs, gain_one.astype(f32), bias_one.astype(f32)
    )
    normed = norm_one.astype(bf16).reshape(count, side, side, D)
    shifted = to_windows(jnp.roll(normed, (-SHIFT, -SHIFT), (1, 2)))
    query_rows = (
        jnp.dot(shifted, w_query, preferred_element_type=f32) + query_bias.astype(f32)
    ) * scale
    key_rows = jnp.dot(shifted, w_keys, preferred_element_type=f32)
    value_rows = jnp.dot(shifted, w_values, preferred_element_type=f32) + value_bias.astype(f32)
    query = split_heads(query_rows.astype(bf16), groups, span)
    keys = split_heads(key_rows.astype(bf16), groups, span)
    values = split_heads(value_rows.astype(bf16), groups, span)
    onehot = rel_index.reshape(-1)[:, None] == lax.iota(jnp.int32, TAB)[None, :]
    position = jnp.dot(onehot.astype(bf16), table, preferred_element_type=f32)
    position = position.reshape(span, span, HEADS).transpose(2, 0, 1)
    region_rows = to_windows(region_map().reshape(1, side, side, 1)).reshape(windows, span)
    masking = jnp.where(region_rows[:, :, None] == region_rows[:, None, :], 0.0, -100.0).astype(f32)
    offsets = position[None] + masking[:, None]

    def scores_of(query_part, key_part):
        raw = jnp.einsum("ghqd,ghkd->ghqk", query_part, key_part, preferred_element_type=f32)
        raw = raw.reshape(count, windows, HEADS, span, span) + offsets[None]
        return raw.reshape(groups, HEADS, span, span)

    scores = scores_of(query, keys)
    top = jnp.max(scores, -1, keepdims=True)
    expo = jnp.exp(scores - top)
    total = jnp.sum(expo, -1, keepdims=True)
    logsum = top + jnp.log(total)
    probs = (expo / total).astype(bf16)
    attended = jnp.einsum("ghqk,ghkd->ghqd", probs, values, preferred_element_type=f32)
    attended = join_heads(attended.astype(bf16))
    projected = jnp.dot(attended, w_proj, preferred_element_type=f32) + proj_bias.astype(f32)
    branch = jnp.roll(from_windows(projected, count, side), (SHIFT, SHIFT), (1, 2)).reshape(
        rows_all, D
    )
    middle = inputs + branch
    norm_two, norm_two_back = jax.vjp(
        layer_norm, middle, gain_two.astype(f32), bias_two.astype(f32)
    )
    hidden_in = norm_two.astype(bf16)
    pre = jnp.dot(hidden_in, w_fc1, preferred_element_type=f32) + fc1_bias.astype(f32)
    act, act_back = jax.vjp(gelu_exact, pre)
    act_low = act.astype(bf16)
    out_rows = middle + jnp.dot(act_low, w_fc2, preferred_element_type=f32) + fc2_bias.astype(f32)
    block_out = out_rows.astype(bf16).reshape(images.shape)
    live = (lax.iota(jnp.int32, count) < counts[0]).astype(bf16)
    upstream = (cotangent * live[:, None, None, None]).reshape(rows_all, D)
    upstream_f = upstream.astype(f32)
    grad_fc2 = jnp.einsum("rh,rd->hd", act_low, upstream, preferred_element_type=f32)
    grad_fc2_bias = jnp.sum(upstream_f, 0)
    grad_act = jnp.einsum("rd,hd->rh", upstream, w_fc2, preferred_element_type=f32)
    grad_pre = act_back(grad_act)[0].astype(bf16)
    grad_fc1 = jnp.einsum("rd,rh->dh", hidden_in, grad_pre, preferred_element_type=f32)
    grad_fc1_bias = jnp.sum(grad_pre.astype(f32), 0)
    grad_norm_two = jnp.einsum("rh,dh->rd", grad_pre, w_fc1, preferred_element_type=f32)
    grad_mid_part, grad_gain_two, grad_bias_two = norm_two_back(grad_norm_two)
    grad_middle = upstream_f + grad_mid_part
    branch_grad = to_windows(
        jnp.roll(grad_middle.astype(bf16).reshape(count, side, side, D), (-SHIFT, -SHIFT), (1, 2))
    )
    grad_proj = jnp.einsum("rc,rd->cd", attended, branch_grad, preferred_element_type=f32)
    grad_proj_bias = jnp.sum(branch_grad.astype(f32), 0)
    grad_att = jnp.einsum("rd,cd->rc", branch_grad, w_proj, preferred_element_type=f32)
    grad_att = split_heads(grad_att.astype(bf16), groups, span)
    again = scores_of(query, keys)
    weights_f = jnp.exp(again - logsum)
    grad_probs = jnp.einsum("ghqd,ghkd->ghqk", grad_att, values, preferred_element_type=f32)
    grad_scores = weights_f * (grad_probs - jnp.sum(weights_f * grad_probs, -1, keepdims=True))
    grad_scores = grad_scores.astype(bf16)
    grad_query = (
        jnp.einsum("ghqk,ghkd->ghqd", grad_scores, keys, preferred_element_type=f32) * scale
    )
    grad_keys = jnp.einsum("ghqk,ghqd->ghkd", grad_scores, query, preferred_element_type=f32)
    grad_values = jnp.einsum(
        "ghqk,ghqd->ghkd", weights_f.astype(bf16), grad_att, preferred_element_type=f32
    )
    grad_query = join_heads(grad_query.astype(bf16))
    grad_keys = join_heads(grad_keys.astype(bf16))
    grad_values = join_heads(grad_values.astype(bf16))
    grad_qkv = jnp.concatenate([grad_query, grad_keys, grad_values], 1)
    grad_wqkv = jnp.einsum("rc,rj->cj", shifted, grad_qkv, preferred_element_type=f32)
    grad_query_bias = jnp.sum(grad_query.astype(f32), 0)
    grad_value_bias = jnp.sum(grad_values.astype(f32), 0)
    score_sum = jnp.sum(grad_scores.astype(f32), 0).reshape(HEADS, span * span)
    grad_table = jnp.dot(score_sum, onehot.astype(f32), precision=HIGH).T.reshape(-1)
    grad_norm_one = jnp.einsum("rj,cj->rc", grad_qkv, w_qkv, preferred_element_type=f32)
    grad_norm_one = jnp.roll(
        from_windows(grad_norm_one, count, side), (SHIFT, SHIFT), (1, 2)
    ).reshape(rows_all, D)
    grad_in_part, grad_gain_one, grad_bias_one = norm_one_back(grad_norm_one)
    input_grad = (grad_middle + grad_in_part).reshape(images.shape)
    padding = total_len - starts[-1]
    local_grad = jnp.concatenate(
        [
            grad_gain_one,
            grad_bias_one,
            grad_wqkv.reshape(-1),
            grad_query_bias,
            grad_value_bias,
            grad_table,
            grad_proj.reshape(-1),
            grad_proj_bias,
            grad_gain_two,
            grad_bias_two,
            grad_fc1.reshape(-1),
            grad_fc1_bias,
            grad_fc2.reshape(-1),
            grad_fc2_bias,
            jnp.zeros((padding,), f32),
        ]
    )
    summed = lax.psum(local_grad.astype(jnp.bfloat16), "dp")
    grad_shard = lax.psum_scatter(summed, "opt", scatter_dimension=0, tiled=True).astype(
        jnp.float32
    )
    start = lax.axis_index("opt") * shard_len
    new_params, new_first, new_second = adam_update(
        params, moment1, moment2, grad_shard, rates, start
    )
    return (block_out, input_grad, grad_shard, new_params, new_first, new_second)


def solution(mesh):
    return jax.shard_map(
        local,
        mesh=mesh,
        in_specs=(
            P(("dp", "opt"), None, None, None),
            P(("dp", "opt"), None, None, None),
            P(("dp", "opt")),
            P(),
            P("opt"),
            P("opt"),
            P("opt"),
            P(),
        ),
        out_specs=(
            P(("dp", "opt"), None, None, None),
            P(("dp", "opt"), None, None, None),
            P("opt"),
            P("opt"),
            P("opt"),
            P("opt"),
        ),
        check_vma=False,
    )
```

profile of v0, /device:TPU:0, one launch (start us, length us, event | category | flops | bytes accessed | tf_op | source)
XLA Modules:
  0.0 1061.0 jit_solution(6383839707523604842)
XLA Ops:
  25.0 104.2 %all-gather.2.cloned.1.call-done = bf16[3158016]{0:T(1024)(128)(2,1)} async-done(((bf16[789504]{0:T(1024)(128)(2,1)}), bf16[3158016]{0:T(1024)(128)(2,1)}) %all-gather.2.cloned.1.call-update) | async-done | bytes 6316048 | tf_op jit(solution)/shard_map/all_gather | solution.py:92
  158.2 14.4 %reshape.407 = bf16[32,49,16,32]{1,0,3,2:T(8,128)(2,1)} reshape(bf16[1568,512]{0,1:T(8,128)(2,1)} %copy.126) | data formatting | bytes 3211264 | tf_op jit(solution)/shard_map/reshape | solution.py:61
  172.6 13.6 %reshape.408 = bf16[32,49,16,32]{1,0,3,2:T(8,128)(2,1)} reshape(bf16[1568,512]{0,1:T(8,128)(2,1)S(1)} %copy.127) | data formatting | bytes 3211264 | tf_op jit(solution)/shard_map/reshape | solution.py:61
  187.4 20.8 %fusion.7 = (f32[32,16,49]{2,1,0:T(8,128)}, f32[32,16,49,49]{2,3,1,0:T(8,128)}) fusion(f32[4,16,49,49]{2,3,1,0:T(8,128)S(1)} %broadcast_add_fusion, bf16[32,16,49,32]{2,0,3,1:T(8,128)(2,1)} %bitcast.148, bf16[32,16,49,32]{2,0,3,1:T(8,128)(2,1)} %bitcast.146), kind=kOutput, calls=%fused_computation.25 | convolution fusion | flops 81109504 | bytes 8843520 | tf_op jit(solution)/shard_map/ghqd,ghkd->ghqk/dot_general | solution.py:134
  208.2 10.6 fusion
  220.6 9.8 divide_convert_fusion
  239.2 13.8 %reshape.409 = bf16[32,49,16,32]{1,0,3,2:T(8,128)(2,1)} reshape(bf16[1568,512]{0,1:T(8,128)(2,1)S(1)} %copy.132) | data formatting | bytes 3211264 | tf_op jit(solution)/shard_map/reshape | solution.py:61
  253.0 10.9 %convert_bitcast_fusion.2 = bf16[32,49,16,32]{1,3,2,0:T(8,128)(2,1)} fusion(bf16[32,16,49,49]{2,3,1,0:T(8,128)(2,1)} %divide_convert_fusion, bf16[32,16,49,32]{2,0,3,1:T(8,128)(2,1)} %bitcast.144), kind=kOutput, calls=%fused_computation.47 | convolution fusion | flops 79478784 | bytes 5669888 | tf_op jit(solution)/shard_map/ghqk,ghkd->ghqd/dot_general | solution.py:144
  270.7 7.7 reshape.410
  329.9 32.9 %multiply_convert_fusion.1 = (bf16[1568,2048]{1,0:T(8,128)(2,1)}, f32[1568,2048]{1,0:T(8,128)}, f32[1568,2048]{1,0:T(8,128)}) fusion(f32[2048]{0:T(1024)S(1)} %slice_convert_fusion, bf16[1568,512]{1,0:T(8,128)(2,1)S(1)} %copy-done.25, bf16[512,2048]{1,0:T(8,128)(2,1)} %reshape.415), kind=kOutput, calls=%fused_computation.11 | convolution fusion | flops 3500277760 | bytes 35823616 | tf_op jit(solution)/shard_map/dot_general | solution.py:155
  362.9 14.9 %fusion.112 = (bf16[2048]{0:T(1024)(128)(2,1)S(1)}, bf16[1568,2048]{1,0:T(8,128)(2,1)}) fusion(f32[1568,2048]{1,0:T(8,128)} %get-tuple-element.55, bf16[1568,512]{1,0:T(8,128)(2,1)S(1)} %copy-done.8, bf16[2048,512]{1,0:T(8,128)(2,1)S(1)} %copy-done.18, f32[1568,2048]{1,0:T(8,128)} %get-tuple-element.93, f32[2048]{0:T(1024)S(1)} %slice_convert_fusion), kind=kOutput, calls=%fused_computation.190 | convolution fusion | flops 3339712512 | bytes 35827712 | tf_op jit(solution)/shard_map/rd,hd->rh/dot_general | solution.py:165
  377.8 10.2 multiply_reduce_fusion.1
  415.1 14.6 %reshape.422 = bf16[32,49,16,32]{1,0,3,2:T(8,128)(2,1)} reshape(bf16[1568,512]{0,1:T(8,128)(2,1)} %copy.144) | data formatting | bytes 3211264 | tf_op jit(solution)/shard_map/reshape | solution.py:61
  429.6 17.5 %multiply_reduce_fusion = (f32[32,16,49]{2,1,0:T(8,128)S(1)}, f32[32,16,49,49]{2,3,1,0:T(8,128)}) fusion(f32[32,16,49,49]{2,3,1,0:T(8,128)} %get-tuple-element.92, f32[32,16,49]{2,1,0:T(8,128)} %log_add_fusion, f32[4,16,49,49]{2,3,1,0:T(8,128)S(1)} %copy-done.3, bf16[32,16,49,32]{2,0,3,1:T(8,128)(2,1)} %bitcast.145, bf16[32,16,49,32]{2,0,3,1:T(8,128)(2,1)} %bitcast.142), kind=kOutput, calls=%fused_computation.4 | convolution fusion | flops 83568128 | bytes 13861120 | tf_op jit(solution)/shard_map/ghqd,ghkd->ghqk/dot_general | solution.py:181
  447.1 16.9 %convert_reduce_fusion = (f32[16,49,49]{1,2,0:T(8,128)}, bf16[32,16,49,49]{2,3,1,0:T(8,128)(2,1)}, bf16[32,16,49,49]{2,3,1,0:T(8,128)(2,1)}) fusion(f32[32,16,49,49]{2,3,1,0:T(8,128)} %get-tuple-element.96, f32[32,16,49]{2,1,0:T(8,128)S(1)} %get-tuple-element.95, f32[32,16,49]{2,1,0:T(8,128)S(1)} %copy-done.17, f32[32,16,49,49]{2,3,1,0:T(8,128)} %get-tuple-element.92, ...), kind=kLoop, calls=%fused_computation.2 | loop fusion | flops 9796080 | bytes 15720768 | tf_op jit(solution)/shard_map/reduce_sum | solution.py:198
  464.0 10.8 %convert_bitcast_fusion.1 = bf16[32,49,16,32]{1,3,2,0:T(8,128)(2,1)} fusion(bf16[32,16,49,49]{2,3,1,0:T(8,128)(2,1)} %get-tuple-element.46, bf16[32,16,49,32]{2,0,3,1:T(8,128)(2,1)} %bitcast.147), kind=kOutput, calls=%fused_computation.46 | convolution fusion | flops 79478784 | bytes 5669888 | tf_op jit(solution)/shard_map/ghqk,ghqd->ghkd/dot_general | solution.py:187
  474.9 11.4 %fusion.110 = (bf16[16,32]{1,0:T(8,128)(2,1)S(1)}, bf16[32,49,16,32]{1,3,2,0:T(8,128)(2,1)}) fusion(bf16[32,16,49,49]{2,3,1,0:T(8,128)(2,1)} %get-tuple-element.46, bf16[32,16,49,32]{2,0,3,1:T(8,128)(2,1)} %bitcast.149), kind=kOutput, calls=%fused_computation.188 | convolution fusion | flops 81083904 | bytes 5670912 | tf_op jit(solution)/shard_map/ghqk,ghkd->ghqd/dot_general | solution.py:185
  493.5 12.5 %copy.149 = bf16[32,49,16,32]{3,2,0,1:T(8,128)(2,1)} copy(bf16[32,49,16,32]{1,3,2,0:T(8,128)(2,1)} %get-tuple-element.98) | data formatting | bytes 3211264 | tf_op jit(solution)/shard_map/convert_element_type | solution.py:191
  506.0 11.3 %fusion.111 = (bf16[16,32]{1,0:T(8,128)(2,1)S(1)}, bf16[32,49,16,32]{1,3,2,0:T(8,128)(2,1)}) fusion(bf16[32,16,49,49]{2,3,1,0:T(8,128)(2,1)} %get-tuple-element.56, bf16[32,16,49,32]{2,0,3,1:T(8,128)(2,1)} %bitcast.143), kind=kOutput, calls=%fused_computation.189 | convolution fusion | flops 80281088 | bytes 5670912 | tf_op jit(solution)/shard_map/ghqk,ghqd->ghkd/dot_general | solution.py:188
  524.2 12.7 %copy.155 = bf16[32,49,16,32]{3,2,0,1:T(8,128)(2,1)} copy(bf16[32,49,16,32]{1,3,2,0:T(8,128)(2,1)} %get-tuple-element.100) | data formatting | bytes 3211264 | tf_op jit(solution)/shard_map/convert_element_type | solution.py:193
  543.8 12.5 %copy.152 = bf16[32,49,16,32]{3,2,0,1:T(8,128)(2,1)} copy(bf16[32,49,16,32]{1,3,2,0:T(8,128)(2,1)} %convert_bitcast_fusion.1) | data formatting | bytes 3211264 | tf_op jit(solution)/shard_map/convert_element_type | solution.py:192
  556.3 8.9 concatenate.50
  566.7 8.9 concatenate.52
  577.1 8.9 concatenate.51
  608.5 7.7 reshape.426
  616.2 7.7 reshape.428
  624.0 8.8 reshape.427
  649.0 100.5 %concatenate.57 = bf16[3158016]{0:T(1024)(128)(2,1)} concatenate(bf16[512]{0:T(512)(128)(2,1)} %get-tuple-element.32, bf16[512]{0:T(512)(128)(2,1)S(1)} %add_convert_fusion.6, bf16[786432]{0:T(1024)(128)(2,1)S(1)} %reshape.429, bf16[512]{0:T(512)(128)(2,1)} %reduce_sum.242, bf16[512]{0:T(512)(128)(2,1)} %reduce_sum.244, bf16[2704]{0:T(1024)(128)(2,1)S(1)} %reshape.431, ...), dimensions={0} | concatenate | bytes 12632064 | tf_op jit(solution)/shard_map/concatenate | solution.py:207
  752.8 8.8 add_convert_fusion.2
  777.9 193.7 %all-reduce.6.cloned.1.call-done = bf16[3158016]{0:T(1024)(128)(2,1)} async-done(((bf16[3158016]{0:T(1024)(128)(2,1)}), bf16[3158016]{0:T(1024)(128)(2,1)}) %all-reduce.6.cloned.1.call-update) | async-done | bytes 6316048
  990.6 42.8 %all-reduce.4.cloned.1.call-done = bf16[789504]{0:T(1024)(128)(2,1)} async-done(((bf16[789504]{0:T(1024)(128)(2,1)}), bf16[789504]{0:T(1024)(128)(2,1)}) %all-reduce.4.cloned.1.call-update) | async-done | bytes 1579024 | tf_op jit(solution)/shard_map/psum | solution.py:226
  1033.4 20.8 %multiply_subtract_fusion = (f32[789504]{0:T(1024)}, f32[789504]{0:T(1024)}, f32[789504]{0:T(1024)}, f32[789504]{0:T(1024)}) fusion(f32[789504]{0:T(1024)S(1)} %copy-done.12, f32[]{:T(128)} %bitcast.36, f32[]{:T(128)} %bitcast.35, f32[]{:T(128)} %bitcast.34, f32[]{:T(128)} %bitcast.33, f32[]{:T(128)} %bitcast.32, f32[]{:T(128)} %bitcast.31, f32[]{:T(128)} %bitcast.30, ...), kind=kLoop, calls=%fused_computation.85 | loop fusion | flops 45791232 | bytes 23685184 | tf_op jit(solution)/shard_map/sub | solution.py:82
  (246 shorter events, 243.1 us)
Async XLA Ops:
  7.2 4.1 copy-start.37
  7.2 5.6 copy-start.23
  7.2 122.0 %all-gather.2.cloned.1.call-start = ((), (), s32[]{:S(2)}) async-start(), calls=%async_computation | async-start | bytes 7895040 | tf_op jit(solution)/shard_map/all_gather | solution.py:92
  10.6 961.1 %all-reduce.6.cloned.1.call-start = ((), (), s32[]{:S(2)}) async-start(), calls=%async_computation.2 | async-start | bytes 12632064
  18.4 5.1 copy-start.39
  23.6 113.9 %copy-start.14 = (f32[8,14,14]{0,2,1:T(8,128)}, f32[8,14,14]{0,2,1:T(8,128)S(1)}, u32[]{:S(2)}) copy-start(f32[8,14,14]{0,2,1:T(8,128)S(1)} %broadcast_multiply_fusion.2) | copy-start | bytes 18820
  25.0 112.5 %copy-start.27 = (f32[8,14,14]{0,2,1:T(8,128)}, f32[8,14,14]{0,2,1:T(8,128)S(1)}, u32[]{:S(2)}) copy-start(f32[8,14,14]{0,2,1:T(8,128)S(1)} %get-tuple-element.71) | copy-start | bytes 18820
  187.4 33.2 %copy-start.2 = (f32[4,16,49,49]{2,3,1,0:T(8,128)}, f32[4,16,49,49]{2,3,1,0:T(8,128)S(1)}, u32[]{:S(2)}) copy-start(f32[4,16,49,49]{2,3,1,0:T(8,128)S(1)} %broadcast_add_fusion) | copy-start | bytes 1843972
  220.6 12.3 %copy-start.47 = (f32[512]{0:T(512)S(1)}, f32[512]{0:T(512)}, u32[]{:S(2)}) copy-start(f32[512]{0:T(512)} %get-tuple-element.61) | copy-start | bytes 6148
  270.7 7.8 copy-start.46
  278.5 4.2 copy-start.22
  308.4 4.6 copy-start.40
  308.4 4.7 copy-start.42
  315.3 5.4 copy-start.11
  324.4 5.5 copy-start.25
  329.9 32.9 %copy-start.8 = (bf16[1568,512]{1,0:T(8,128)(2,1)S(1)}, bf16[1568,512]{1,0:T(8,128)(2,1)}, u32[]{:S(2)}) copy-start(bf16[1568,512]{1,0:T(8,128)(2,1)} %reshape.418) | copy-start | bytes 4816900
  329.9 32.9 %copy-start.18 = (bf16[2048,512]{1,0:T(8,128)(2,1)S(1)}, bf16[2048,512]{1,0:T(8,128)(2,1)}, u32[]{:S(2)}) copy-start(bf16[2048,512]{1,0:T(8,128)(2,1)} %reshape.416) | copy-start | bytes 6291460
  362.9 14.9 %copy-start.9 = (f32[1568,512]{1,0:T(8,128)S(1)}, f32[1568,512]{1,0:T(8,128)}, u32[]{:S(2)}) copy-start(f32[1568,512]{1,0:T(8,128)} %reshape.403) | copy-start | bytes 9633796
  377.8 10.2 copy-start.50
  388.0 5.7 copy-start.16
  407.7 4.0 copy-start.26
  407.7 4.0 copy-start.31
  415.1 14.6 %copy-start.3 = (f32[4,16,49,49]{2,3,1,0:T(8,128)S(1)}, f32[4,16,49,49]{2,3,1,0:T(8,128)}, u32[]{:S(2)}) copy-start(f32[4,16,49,49]{2,3,1,0:T(8,128)} %copy-done.2) | copy-start | bytes 1843972
  429.6 17.5 %copy-start.17 = (f32[32,16,49]{2,1,0:T(8,128)S(1)}, f32[32,16,49]{2,1,0:T(8,128)}, u32[]{:S(2)}) copy-start(f32[32,16,49]{2,1,0:T(8,128)} %log_add_fusion) | copy-start | bytes 301060
  592.1 3.9 slice-start.1
  600.2 4.4 copy-start.32
  602.6 4.7 copy-start.41
  632.8 9.7 copy-start.36
  749.5 283.9 %all-reduce.4.cloned.1.call-start = ((), (), s32[]{:S(2)}) async-start(), calls=%async_computation.1 | async-start | bytes 3158016 | tf_op jit(solution)/shard_map/psum | solution.py:226
  761.7 7.9 copy-start.10
  777.9 196.4 %copy-start.6 = (f32[1568,512]{1,0:T(8,128)S(1)}, f32[1568,512]{1,0:T(8,128)}, u32[]{:S(2)}) copy-start(f32[1568,512]{1,0:T(8,128)} %copy-done.5) | copy-start | bytes 9633796
  984.2 49.2 %copy-start.12 = (f32[789504]{0:T(1024)S(1)}, f32[789504]{0:T(1024)}, u32[]{:S(2)}) copy-start(f32[789504]{0:T(1024)} %param.12) | copy-start | bytes 9474052
  (24 other events, 62.7 us)
Sparse Core Ops, SparseCore 0:
  10.7 118.4 all-gather.1
  749.6 221.9 all-reduce.5
  975.5 57.8 all-reduce.3
where the time goes:
time: 1080 us; the launch traced here: 1060 us
  local copies, waits for them, and re-layouts  413 us (38%)
  waiting for transfers between devices  341 us (32%)
  matrix products  193 us (18%)
  other arithmetic  98 us (9%)
  between operations  16.2 us (2%)
    unnamed x4, waiting for transfers between devices  194 us
    all_gather x1, waiting for transfers between devices, local(): working = lax.all_gather(params.astype(bf16), 'opt', axis=0, tiled=True)  104 us
    concatenate x1, local copies, waits for them, and re-layouts, local(): jnp.concatenate([grad_gain_one, grad_bias_one, grad_wqkv.reshape(-1), gra...  101 us
    reshape x4, local copies, waits for them, and re-layouts, split_heads(): return rows.reshape(groups, span, HEADS, HEAD_DIM).transpose(0, 2, 1, 3)  56.4 us
    psum x1, waiting for transfers between devices, local(): summed = lax.psum(local_grad.astype(jnp.bfloat16), 'dp')  42.8 us
    dot_general x1, matrix products, local(): jnp.dot(hidden_in, w_fc1, preferred_element_type=f32) + fc1_bias.astype(f32)  32.9 us
    reshape x4, local copies, waits for them, and re-layouts, join_heads(): return field.transpose(0, 2, 1, 3).reshape(groups * span, D)  32 us
    concatenate x6, local copies, waits for them, and re-layouts, local(): grad_qkv = jnp.concatenate([grad_query, grad_keys, grad_values], 1)  30 us
  transfers between devices with their start and end apart: 3, of which 3 were waited for; matrix products, arithmetic and copies ran while one was open for 5% of the time, Pallas kernels for 0%

commit v1 on v0

v1 whole, which is shorter than its diff:
```python
import math
import jax
import jax.numpy as jnp
from jax import lax
from jax.experimental import pallas as pl
from jax.experimental.pallas import tpu as pltpu

D = 512
HEADS = 16
HEAD_DIM = 32
HID = 2048
SIDE = 14
WIN = 7
SHIFT = 3
TAB = 169
F32 = jnp.float32
BF16 = jnp.bfloat16

IMGS = 8
SPAN = WIN * WIN
WROWS = SPAN * IMGS
ROWS = 4 * WROWS
RS = ROWS + 64
BLK = 224
NBLK = ROWS // BLK
WB = 4 * IMGS
SCALE = HEAD_DIM ** -0.5

R_G1, R_B1, R_QKV, R_BQ, R_BV, R_TAB = 0, 4, 8, 6152, 6156, 6160
R_PROJ, R_BP, R_G2, R_B2, R_W1, R_C1, R_W2, R_C2, R_END = 6181, 8229, 8233, 8237, 8241, 16433, 16449, 24641, 24645
LANE = 16
BROW = 6176


def segments(w):
    if w == 0:
        return [(SHIFT, WIN, 0)]
    return [(WIN + SHIFT, WIN - SHIFT, 0), (0, SHIFT, WIN - SHIFT)]


def window_copies(hbm, vmem, sem, inward):
    out = []
    n = 0
    for wy in range(2):
        for wx in range(2):
            for ys, yl, yo in segments(wy):
                for xs, xl, xo in segments(wx):
                    a = hbm.at[pl.ds(ys, yl), pl.ds(xs, xl)]
                    b = vmem.at[pl.ds((2 * wy + wx) * WIN + yo, yl), pl.ds(xo, xl)]
                    out.append(pltpu.make_async_copy(a, b, sem.at[n]) if inward else pltpu.make_async_copy(b, a, sem.at[n]))
                    n += 1
    return out


NSEG = 9


def dot(a, b):
    return lax.dot_general(a, b, (((1,), (0,)), ((), ())), preferred_element_type=F32)


def dot_nt(a, b):
    return lax.dot_general(a, b, (((1,), (1,)), ((), ())), preferred_element_type=F32)


def dot_tn(a, b):
    return lax.dot_general(a, b, (((0,), (0,)), ((), ())), preferred_element_type=F32)


def norm_stats(x):
    mean = jnp.mean(x, -1, keepdims=True)
    dev = x - mean
    var = jnp.mean(dev * dev, -1, keepdims=True)
    r = lax.rsqrt(var + 1e-05)
    return dev * r, r


def unit_rows(ref3, unit, units):
    return ref3[pl.ds(unit, units)].astype(F32).reshape(units * 8, 128)


def vec_from(fs, row, width, shift):
    parts = []
    lane = lax.broadcasted_iota(jnp.int32, (1, 128), 1)
    for c in range(width // 128):
        a = fs[pl.ds(row + c, 1), :]
        if shift:
            b = fs[pl.ds(row + c + 1, 1), :]
            a = jnp.where(lane < 128 - LANE, pltpu.roll(a, 128 - LANE, 1), pltpu.roll(b, 128 - LANE, 1))
        parts.append(a)
    return jnp.concatenate(parts, 1)


def take_matrix(fs, row, dst, nrows, ncb, shift, step=128):
    lane = lax.broadcasted_iota(jnp.int32, (step, 128), 1)

    def body(t, _):
        base = row + t * (step * ncb)
        r0 = pl.multiple_of(t * step, step)
        for c in range(ncb):
            a = fs[pl.ds(base + c, step, stride=ncb), :]
            if shift:
                b = fs[pl.ds(base + c + 1, step, stride=ncb), :]
                a = jnp.where(lane < 128 - LANE, pltpu.roll(a, 128 - LANE, 1), pltpu.roll(b, 128 - LANE, 1))
            dst[pl.ds(r0, step), c * 128:(c + 1) * 128] = a.astype(BF16)
        return 0

    lax.fori_loop(0, nrows // step, body, 0)


def lane_head():
    return lax.broadcasted_iota(jnp.int32, (64, 128), 1) // HEAD_DIM


def block_diag(v, heads):
    zero = jnp.zeros_like(v)
    return jnp.concatenate([jnp.where(heads == h, v, zero) for h in range(4)], 0)


def diag_sum(r, heads):
    out = r[0:64]
    for h in range(1, 4):
        out = jnp.where(heads == h, r[64 * h:64 * h + 64], out)
    return out


def take_rows(fs, start):
    v = fs[pl.ds(start, 56, stride=IMGS), :]
    v = jnp.where(lax.broadcasted_iota(jnp.int32, (56, 128), 0) < SPAN, v, 0.0)
    return jnp.concatenate([v, jnp.zeros((8, 128), F32)], 0)


def put_rows(fs, start, v):
    fs[pl.ds(start, 48, stride=IMGS), :] = v[0:48]
    fs[pl.ds(start + 48 * IMGS, 1), :] = v[48:49]


def build_bias(tab3, rel_ref, big, bias):
    rel = rel_ref[...]
    row = lax.shift_right_arithmetic(rel, 3)
    low = rel & 7
    oh = (lax.broadcasted_iota(jnp.int32, (32, 4096), 0) == row).astype(F32).astype(BF16)
    tab = jnp.concatenate([tab3, jnp.zeros((8, 128), F32)], 0).astype(BF16)
    r = dot_tn(tab, oh)
    acc = jnp.zeros((16, 4096), F32)
    for j in range(8):
        acc = acc + jnp.where(low == j, r[16 * j:16 * j + 16], 0.0)
    for kk in range(32):
        big[kk * 16:kk * 16 + 16, :] = acc[:, kk * 128:kk * 128 + 128]
    k = lax.broadcasted_iota(jnp.int32, (64, 256), 0)
    q = lax.broadcasted_iota(jnp.int32, (64, 256), 1) & 63
    ki = lax.shift_right_arithmetic(k * 37, 8)
    kj = k - ki * 7
    qi = lax.shift_right_arithmetic(q * 37, 8)
    qj = q - qi * 7
    cut = WIN - SHIFT
    same_y = (ki < cut) == (qi < cut)
    same_x = (kj < cut) == (qj < cut)
    lane = lax.broadcasted_iota(jnp.int32, (32, 128), 1)
    for g in range(4):
        for pair in range(2):
            h = 4 * g + 2 * pair
            a = big[pl.ds(h, 32, stride=16), :]
            b = big[pl.ds(h + 1, 32, stride=16), :]
            even = jnp.where(lane < 64, a, pltpu.roll(b, 64, 1))
            odd = jnp.where(lane < 64, pltpu.roll(a, 64, 1), b)
            big[pl.ds(1024 + g * 256 + pair * 128, 32, stride=2), :] = even
            big[pl.ds(1024 + g * 256 + pair * 128 + 1, 32, stride=2), :] = odd
    for g in range(4):
        pos = jnp.concatenate([big[1024 + g * 256:1024 + g * 256 + 64, :], big[1024 + g * 256 + 128:1024 + g * 256 + 192, :]], 1)
        for w in range(4):
            keep = None
            if w == 1:
                keep = same_x
            elif w == 2:
                keep = same_y
            elif w == 3:
                keep = same_y & same_x
            val = pos if keep is None else pos + jnp.where(keep, 0.0, -100.0)
            bias[w * 4 + g] = jnp.where(k < SPAN, val, -1e30)


def kernel_a(x_hbm, flat_hbm, rel_ref,
             wqkv_o, wp_o, w1_o, w2_o, vec_o, hw_o, ob_o, qkv_o, p_o,
             x_v, flat_v, fs, os_, bias, wqkv, wp, w1, w2, vec, hw, ob, qkvb, pb, xsem, fsem, osem, wsem):
    cps = window_copies(x_hbm, x_v, xsem, True)
    for c in cps:
        c.start()
    fcp = pltpu.make_async_copy(flat_hbm, flat_v, fsem)
    fcp.start()
    fcp.wait()
    nA = BROW // 8
    def conv(t, _):
        fs[pl.ds(pl.multiple_of(t * 128, 128), 128), :] = unit_rows(flat_v, t * 16, 16)
        return 0
    lax.fori_loop(0, nA // 16, conv, 0)
    fs[(nA // 16) * 128:BROW + 8, :] = unit_rows(flat_v, (nA // 16) * 16, nA + 1 - (nA // 16) * 16)
    take_matrix(fs, R_QKV, wqkv, D, 12, False)
    vec[0:1, :] = vec_from(fs, R_G1, D, False)
    vec[1:2, :] = vec_from(fs, R_B1, D, False)
    vec[2:3, :] = vec_from(fs, R_BQ, D, False)
    vec[3:4, :] = vec_from(fs, R_BV, D, False)
    build_bias(fs[R_TAB:R_TAB + 24, :], rel_ref, os_, bias)
    for c in cps:
        c.wait()
    gain = vec[0:1, :]
    shift = vec[1:2, :]
    bq = vec[2:3, :]
    bv = vec[3:4, :]

    def rows(t, _):
        r0 = pl.multiple_of(t * BLK, BLK)
        x = x_v[pl.ds(4 * t, 4)].reshape(BLK, D).astype(F32)
        xhat, _r = norm_stats(x)
        h = (xhat * gain + shift).astype(BF16)
        hw[pl.ds(r0, BLK), :] = h
        for c in range(12):
            y = dot(h, wqkv[:, c * 128:(c + 1) * 128])
            if c < 4:
                y = (y + bq[:, c * 128:(c + 1) * 128]) * SCALE
            if c >= 8:
                y = y + bv[:, (c - 8) * 128:(c - 7) * 128]
            fs[pl.ds(c * RS + r0, BLK), :] = y
        return 0
    lax.fori_loop(0, NBLK, rows, 0)

    heads = lane_head()

    def attend(i, _):
        w = lax.shift_right_arithmetic(i, 3)
        b = i & 7
        base = w * WROWS + b
        for g in range(4):
            q = take_rows(fs, g * RS + base).astype(BF16)
            k = take_rows(fs, (4 + g) * RS + base).astype(BF16)
            v = take_rows(fs, (8 + g) * RS + base).astype(BF16)
            qkvb[i, g] = q
            qkvb[i, 4 + g] = k
            qkvb[i, 8 + g] = v
            s = dot_nt(k, block_diag(q, heads)) + bias[w * 4 + g]
            m = jnp.max(s, 0, keepdims=True)
            e = jnp.exp(s - m)
            p = (e * (1.0 / jnp.sum(e, 0, keepdims=True))).astype(BF16)
            pb[i, g] = p
            o = diag_sum(dot_tn(p, v), heads)
            put_rows(os_, g * RS + base, o)
        return 0
    lax.fori_loop(0, WB, attend, 0)

    def outs(t, _):
        r0 = pl.multiple_of(t * BLK, BLK)
        for g in range(4):
            ob[pl.ds(r0, BLK), g * 128:(g + 1) * 128] = os_[pl.ds(g * RS + r0, BLK), :].astype(BF16)
        return 0
    lax.fori_loop(0, NBLK, outs, 0)
    cos = [pltpu.make_async_copy(a, b, osem.at[n]) for n, (a, b) in enumerate([(hw, hw_o), (ob, ob_o), (qkvb, qkv_o), (pb, p_o)])]
    for c in cos:
        c.start()
    nB = flat_v.shape[0] - BROW // 8
    def conv2(t, _):
        fs[pl.ds(pl.multiple_of(t * 64, 64), 64), :] = unit_rows(flat_v, BROW // 8 + t * 8, 8)
        return 0
    lax.fori_loop(0, nB // 8, conv2, 0)
    take_matrix(fs, R_PROJ - BROW, wp, D, 4, True)
    take_matrix(fs, R_W1 - BROW, w1, D, 16, True)
    take_matrix(fs, R_W2 - BROW, w2, HID, 4, True)
    for n, r in enumerate((R_BP, R_G2, R_B2, R_C2)):
        vec[4 + n:5 + n, :] = vec_from(fs, r - BROW, D, True)
    for n in range(4):
        vec[8 + n:9 + n, :] = vec_from(fs, R_C1 - BROW + 4 * n, D, True)
    wos = [pltpu.make_async_copy(a, b, wsem.at[n]) for n, (a, b) in enumerate([(wqkv, wqkv_o), (wp, wp_o), (w1, w1_o), (w2, w2_o), (vec, vec_o)])]
    for c in wos:
        c.start()
    for c in cos + wos:
        c.wait()


def call_a(x, flat, rel):
    units = flat.shape[0]
    any_ = pl.BlockSpec(memory_space=pl.ANY)
    sds = jax.ShapeDtypeStruct
    outs = [sds((D, 3 * D), BF16), sds((D, D), BF16), sds((D, HID), BF16), sds((HID, D), BF16), sds((16, D), F32),
            sds((ROWS, D), BF16), sds((ROWS, D), BF16), sds((WB, 12, 64, 128), BF16), sds((WB, 4, 64, 256), BF16)]
    return pl.pallas_call(
        kernel_a,
        out_shape=outs,
        in_specs=[any_, any_, pl.BlockSpec(memory_space=pltpu.VMEM)],
        out_specs=[any_] * len(outs),
        scratch_shapes=[
            pltpu.VMEM((28, 7, 8, D), BF16), pltpu.VMEM((units, 8, 128), BF16), pltpu.VMEM((12 * RS, 128), F32), pltpu.VMEM((4 * RS, 128), F32),
            pltpu.VMEM((16, 64, 256), F32), pltpu.VMEM((D, 3 * D), BF16), pltpu.VMEM((D, D), BF16), pltpu.VMEM((D, HID), BF16), pltpu.VMEM((HID, D), BF16),
            pltpu.VMEM((16, D), F32), pltpu.VMEM((ROWS, D), BF16), pltpu.VMEM((ROWS, D), BF16), pltpu.VMEM((WB, 12, 64, 128), BF16), pltpu.VMEM((WB, 4, 64, 256), BF16),
            pltpu.SemaphoreType.DMA((NSEG,)), pltpu.SemaphoreType.DMA, pltpu.SemaphoreType.DMA((4,)), pltpu.SemaphoreType.DMA((5,)),
        ],
        compiler_params=pltpu.CompilerParams(vmem_limit_bytes=64000000),
        name="attend",
    )(x, flat, rel)


def rel_lanes(rel_index):
    t = jnp.full((64, 64), -1, jnp.int32).at[:SPAN, :SPAN].set(rel_index.T)
    return t.reshape(1, 4096)


CH = 512
INV_SQRT2 = 0.7071067811865476
INV_SQRT2PI = 0.3989422804014327


def gelu_parts(u):
    e = jnp.exp(u * u * -0.5)
    t = 1.0 / (1.0 + jnp.abs(u) * (0.3275911 * INV_SQRT2))
    half = t * (0.127414796 + t * (-0.142248368 + t * (0.7107068705 + t * (-0.7265760135 + t * 0.5307027145)))) * e
    cdf = jnp.where(u >= 0, 1.0 - half, half)
    return cdf, e * INV_SQRT2PI


def put_matrix(fs, row, get, nrows, ncb, step=128):
    lane = lax.broadcasted_iota(jnp.int32, (step, 128), 1)


def acc_rows(ref, i, v):
    ref[8 * i:8 * i + 8, 0:v.shape[1]] += jnp.sum(v.reshape(v.shape[0] // 8, 8, v.shape[1]), 0)


def kernel_b(x_hbm, cot_hbm, ob_hbm, wp, w1, w2, vec, counts,
             y_hbm, dx1_o, dwp_o, dw1_o, dw2_o, vg_o,
             x_v, dy_v, ob, yv, a, du, h2, dx1, e, acc, xsem, csem, ysem, osem):
    cps = window_copies(x_hbm, x_v, xsem, True) + window_copies(cot_hbm, dy_v, csem, True)
    cps.append(pltpu.make_async_copy(ob_hbm, ob, osem.at[0]))
    for c in cps:
        c.start()
    acc[...] = jnp.zeros_like(acc)
    for c in cps:
        c.wait()
    bp, g2, b2, c2 = (vec[n:n + 1, :] for n in range(4, 8))
    count = counts[0]

    def rows(t, _):
        r0 = pl.multiple_of(t * BLK, BLK)
        x = x_v[pl.ds(4 * t, 4)].reshape(BLK, D).astype(F32)
        alive = lax.broadcasted_iota(jnp.int32, (4, 7, 8, D), 2) < count
        dy = jnp.where(alive, dy_v[pl.ds(4 * t, 4)].astype(F32), 0.0)
        dyb = dy.astype(BF16)
        dy_v[pl.ds(4 * t, 4)] = dyb
        dy = dy.reshape(BLK, D)
        dyb = dyb.reshape(BLK, D)
        x1 = x + dot(ob[pl.ds(r0, BLK), :], wp[...]) + bp
        xhat, r = norm_stats(x1)
        h = (xhat * g2 + b2).astype(BF16)
        h2[pl.ds(r0, BLK), :] = h
        y = x1 + c2
        dh = jnp.zeros((BLK, D), F32)
        for j in range(HID // CH):
            cs = slice(j * CH, (j + 1) * CH)
            u = dot(h, w1[:, cs]) + vec[8 + j:9 + j, :]
            cdf, pdf = gelu_parts(u)
            av = (u * cdf).astype(BF16)
            a[pl.ds(r0, BLK), cs] = av
            y = y + dot(av, w2[cs, :])
            da = dot_nt(dyb, w2[cs, :])
            duv = da * (cdf + u * pdf)
            acc_rows(acc, 4 + j, duv)
            dub = duv.astype(BF16)
            du[pl.ds(r0, BLK), cs] = dub
            dh = dh + dot_nt(dub, w1[:, cs])
        yv[pl.ds(4 * t, 4)] = y.reshape(4, 7, 8, D).astype(BF16)
        acc_rows(acc, 0, dy)
        acc_rows(acc, 1, dh * xhat)
        acc_rows(acc, 2, dh)
        dg = dh * g2
        dt = r * (dg - jnp.mean(dg, -1, keepdims=True) - xhat * jnp.mean(dg * xhat, -1, keepdims=True))
        dxv = dy + dt
        acc_rows(acc, 3, dxv)
        dx1[pl.ds(r0, BLK), :] = dxv
        e[pl.ds(r0, BLK), :] = dxv.astype(BF16)
        return 0
    lax.fori_loop(0, NBLK, rows, 0)
    ycs = window_copies(y_hbm, yv, ysem, False)
    for c in ycs:
        c.start()
    dcp = pltpu.make_async_copy(dx1, dx1_o, osem.at[1])
    dcp.start()
    vg_o[...] = jnp.sum(acc[...].reshape(8, 8, D), 1)
    dyf = dy_v[...].reshape(ROWS, D)

    def w2rows(t, _):
        r0 = pl.multiple_of(t * 256, 256)
        dw2_o[pl.ds(r0, 256), :] = dot_tn(a[:, pl.ds(r0, 256)], dyf)
        return 0
    lax.fori_loop(0, HID // 256, w2rows, 0)

    def w1rows(t, _):
        r0 = pl.multiple_of(t * 256, 256)
        dw1_o[:, pl.ds(r0, 256)] = dot_tn(h2[...], du[:, pl.ds(r0, 256)])
        return 0
    lax.fori_loop(0, HID // 256, w1rows, 0)
    dwp_o[...] = dot_tn(ob[...], e[...])
    dcp.wait()
    for c in ycs:
        c.wait()


def call_b(x, cot, ob, wp, w1, w2, vec, counts):
    any_ = pl.BlockSpec(memory_space=pl.ANY)
    vm = pl.BlockSpec(memory_space=pltpu.VMEM)
    sds = jax.ShapeDtypeStruct
    outs = [sds((14, 14, 8, D), BF16), sds((ROWS, D), F32), sds((D, D), F32), sds((D, HID), F32), sds((HID, D), F32), sds((8, D), F32)]
    big = pltpu.VMEM((28, 7, 8, D), BF16)
    return pl.pallas_call(
        kernel_b,
        out_shape=outs,
        in_specs=[any_, any_, any_, vm, vm, vm, vm, pl.BlockSpec(memory_space=pltpu.SMEM)],
        out_specs=[any_, any_, vm, vm, vm, vm],
        scratch_shapes=[
            big, big, pltpu.VMEM((ROWS, D), BF16), big, pltpu.VMEM((ROWS, HID), BF16), pltpu.VMEM((ROWS, HID), BF16), pltpu.VMEM((ROWS, D), BF16),
            pltpu.VMEM((ROWS, D), F32), pltpu.VMEM((ROWS, D), BF16), pltpu.VMEM((64, D), F32),
            pltpu.SemaphoreType.DMA((NSEG,)), pltpu.SemaphoreType.DMA((NSEG,)), pltpu.SemaphoreType.DMA((NSEG,)), pltpu.SemaphoreType.DMA((2,)),
        ],
        compiler_params=pltpu.CompilerParams(vmem_limit_bytes=64000000),
        name="mlp",
    )(x, cot, ob, wp, w1, w2, vec, counts)


def kernel_c(x_hbm, dx1_hbm, hw_hbm, qkv_hbm, p_hbm, wqkv, wp, vec,
             dx_hbm, dwq_o, vg_o, dtab_o,
             x_v, dx1, hw, qkvb, pb, fs, os_, dq, dxv, dtab, acc, xsem, isem, psem, ysem):
    cps = window_copies(x_hbm, x_v, xsem, True)
    ins = [pltpu.make_async_copy(a, b, isem.at[n]) for n, (a, b) in enumerate([(dx1_hbm, dx1), (hw_hbm, hw), (qkv_hbm, qkvb), (p_hbm, pb)])]
    ins[0].start()
    ins[2].start()
    ins[3].start()
    ins[1].start()
    for c in cps:
        c.start()
    acc[...] = jnp.zeros_like(acc)
    dtab[...] = jnp.zeros_like(dtab)
    ins[0].wait()

    def rows0(t, _):
        r0 = pl.multiple_of(t * BLK, BLK)
        ev = dx1[pl.ds(r0, BLK), :].astype(BF16)
        for g in range(4):
            os_[pl.ds(g * RS + r0, BLK), :] = dot_nt(ev, wp[g * 128:(g + 1) * 128, :])
        return 0
    lax.fori_loop(0, NBLK, rows0, 0)
    ins[2].wait()
    ins[3].wait()
    heads = lane_head()

    def attend(i, _):
        w = lax.shift_right_arithmetic(i, 3)
        b = i & 7
        base = w * WROWS + b
        for g in range(4):
            do = take_rows(os_, g * RS + base).astype(BF16)
            q = qkvb[i, g]
            k = qkvb[i, 4 + g]
            v = qkvb[i, 8 + g]
            pbv = pb[i, g]
            p = pbv.astype(F32)
            dobd = block_diag(do, heads)
            dp = dot_nt(v, dobd)
            t = p * dp
            ds = t - p * jnp.sum(t, 0, keepdims=True)
            dtab[g] += ds
            dsb = ds.astype(BF16)
            put_rows(fs, (8 + g) * RS + base, dot(pbv, dobd))
            put_rows(fs, (4 + g) * RS + base, dot(dsb, block_diag(q, heads)))
            put_rows(fs, g * RS + base, diag_sum(dot_tn(dsb, k), heads) * SCALE)
        return 0
    lax.fori_loop(0, WB, attend, 0)
    for c in cps:
        c.wait()
    gain = vec[0:1, :]

    def rows1(t, _):
        r0 = pl.multiple_of(t * BLK, BLK)
        dn = jnp.zeros((BLK, D), F32)
        for c in range(12):
            v = fs[pl.ds(c * RS + r0, BLK), :]
            if c < 4 or c >= 8:
                i = 2 if c < 4 else 3
                acc[8 * i:8 * i + 8, (c % 4) * 128:(c % 4) * 128 + 128] += jnp.sum(v.reshape(BLK // 8, 8, 128), 0)
            dq[pl.ds(r0, BLK), c * 128:(c + 1) * 128] = v.astype(BF16)
        dn = dot_nt(dq[pl.ds(r0, BLK), :], wqkv[...])
        x = x_v[pl.ds(4 * t, 4)].reshape(BLK, D).astype(F32)
        xhat, r = norm_stats(x)
        acc_rows(acc, 0, dn * xhat)
        acc_rows(acc, 1, dn)
        dg = dn * gain
        dt = r * (dg - jnp.mean(dg, -1, keepdims=True) - xhat * jnp.mean(dg * xhat, -1, keepdims=True))
        dxv[pl.ds(4 * t, 4)] = (dx1[pl.ds(r0, BLK), :] + dt).reshape(4, 7, 8, D)
        return 0
    lax.fori_loop(0, NBLK, rows1, 0)
    ycs = window_copies(dx_hbm, dxv, ysem, False)
    for c in ycs:
        c.start()
    vg_o[...] = jnp.sum(acc[...].reshape(8, 8, D), 1)
    ins[1].wait()

    def wq(t, _):
        c0 = pl.multiple_of(t * 256, 256)
        dwq_o[:, pl.ds(c0, 256)] = dot_tn(hw[...], dq[:, pl.ds(c0, 256)])
        return 0
    lax.fori_loop(0, 6, wq, 0)
    dtab_o[...] = dtab[...]
    for c in ycs:
        c.wait()


def call_c(x, dx1, hw, qkv, p, wqkv, wp, vec):
    any_ = pl.BlockSpec(memory_space=pl.ANY)
    vm = pl.BlockSpec(memory_space=pltpu.VMEM)
    sds = jax.ShapeDtypeStruct
    outs = [sds((14, 14, 8, D), F32), sds((D, 3 * D), F32), sds((8, D), F32), sds((4, 64, 256), F32)]
    return pl.pallas_call(
        kernel_c,
        out_shape=outs,
        in_specs=[any_] * 5 + [vm] * 3,
        out_specs=[any_, vm, vm, vm],
        scratch_shapes=[
            pltpu.VMEM((28, 7, 8, D), BF16), pltpu.VMEM((ROWS, D), F32), pltpu.VMEM((ROWS, D), BF16), pltpu.VMEM((WB, 12, 64, 128), BF16), pltpu.VMEM((WB, 4, 64, 256), BF16),
            pltpu.VMEM((12 * RS, 128), F32), pltpu.VMEM((4 * RS, 128), F32), pltpu.VMEM((ROWS, 3 * D), BF16), pltpu.VMEM((28, 7, 8, D), F32),
            pltpu.VMEM((4, 64, 256), F32), pltpu.VMEM((64, D), F32),
            pltpu.SemaphoreType.DMA((NSEG,)), pltpu.SemaphoreType.DMA((4,)), pltpu.SemaphoreType.DMA, pltpu.SemaphoreType.DMA((NSEG,)),
        ],
        compiler_params=pltpu.CompilerParams(vmem_limit_bytes=64000000),
        name="attend_back",
    )(x, dx1, hw, qkv, p, wqkv, wp, vec)


from jax.sharding import PartitionSpec as P

STEP = 2
HIGH = lax.Precision.HIGHEST
DECAY = [0.0, 0.0, 0.05, 0.0, 0.0, 0.0, 0.05, 0.0, 0.0, 0.0, 0.05, 0.0, 0.05, 0.0, 0.0]


def group_starts():
    lengths = [D, D, 3 * D * D, D, D, TAB * HEADS, D * D, D, D, D, D * HID, HID, HID * D, D]
    starts = [0]
    for length in lengths:
        starts.append(starts[-1] + length)
    return starts


def adam_update(weights, first, second, grad, rates, start):
    index = start + lax.iota(jnp.int32, weights.shape[0])
    starts = group_starts()
    rate = jnp.zeros_like(weights) + rates[0]
    decay = jnp.zeros_like(weights)
    for group in range(1, len(starts)):
        after = index >= starts[group]
        rate = jnp.where(after, rates[group], rate)
        decay = jnp.where(after, DECAY[group], decay)
    first_new = 0.9 * first + 0.1 * grad
    second_new = 0.999 * second + 0.001 * grad * grad
    first_hat = first_new / (1.0 - 0.9**STEP)
    second_hat = second_new / (1.0 - 0.999**STEP)
    weights_new = weights - rate * (first_hat / (jnp.sqrt(second_hat) + 1e-08) + decay * weights)
    return (weights_new, first_new, second_new)


def local(images, cotangent, counts, rel_index, params, moment1, moment2, rates):
    shard_len = params.shape[0]
    total_len = shard_len * lax.axis_size("opt")
    working = lax.all_gather(params.astype(BF16), "opt", axis=0, tiled=True)
    starts = group_starts()
    xt = images.transpose(1, 2, 0, 3)
    ct = cotangent.transpose(1, 2, 0, 3)
    flat = working.reshape(-1, 8, 128)
    wqkv, wp, w1, w2, vec, hw, ob, qkv, p = call_a(xt, flat, rel_lanes(rel_index))
    y, dx1, dwp, dw1, dw2, vgb = call_b(xt, ct, ob, wp, w1, w2, vec, counts)
    dx, dwq, vga, dtab = call_c(xt, dx1, hw, qkv, p, wqkv, wp, vec)
    score = dtab.reshape(4, 64, 4, 64)[:, :SPAN, :, :SPAN].transpose(0, 2, 3, 1).reshape(HEADS, SPAN * SPAN)
    onehot = rel_index.reshape(-1)[:, None] == lax.iota(jnp.int32, TAB)[None, :]
    grad_table = jnp.dot(score, onehot.astype(F32), precision=HIGH).T.reshape(-1)
    local_grad = jnp.concatenate([
        vga[0], vga[1], dwq.reshape(-1), vga[2], vga[3], grad_table, dwp.reshape(-1), vgb[3], vgb[1], vgb[2],
        dw1.reshape(-1), vgb[4:8].reshape(-1), dw2.reshape(-1), vgb[0], jnp.zeros((total_len - starts[-1],), F32)])
    summed = lax.psum(local_grad.astype(BF16), "dp")
    grad_shard = lax.psum_scatter(summed, "opt", scatter_dimension=0, tiled=True).astype(F32)
    start = lax.axis_index("opt") * shard_len
    new_params, new_first, new_second = adam_update(params, moment1, moment2, grad_shard, rates, start)
    return (y.transpose(2, 0, 1, 3), dx.transpose(2, 0, 1, 3), grad_shard, new_params, new_first, new_second)


def solution(mesh):
    split = P(("dp", "opt"), None, None, None)
    return jax.shard_map(
        local, mesh=mesh,
        in_specs=(split, split, P(("dp", "opt")), P(), P("opt"), P("opt"), P("opt"), P()),
        out_specs=(split, split, P("opt"), P("opt"), P("opt"), P("opt")),
        check_vma=False)
```

time: 1080 us -> 705 us (0.65); the launches traced: 1060 us -> 698 us
  local copies, waits for them, and re-layouts: 413 us -> 107 us
  matrix products: 193 us -> 0.91 us
  Pallas kernels: 0 us -> 149 us
  other arithmetic: 98 us -> 30.2 us
  waiting for transfers between devices: 341 us -> 396 us
    dot_general x22 -> x1, matrix products: 193 us -> 0.91 us  [local(): jnp.dot(score, onehot.astype(F32), precision=HIGH).T.reshape(-1)]
    pallas_call x0 -> x3, Pallas kernels: none -> 149 us  [the longest x1 52.3 us: call_b(): pl.pallas_call(kernel_b, out_shape=outs, in_specs=[any_, any_, any_, vm,...]
    reshape x27 -> x5, local copies, waits for them, and re-layouts: 142 us -> 4.09 us  [the longest x1 2.93 us: local(): dwq.reshape(-1)]
    convert_element_type x14 -> x0, local copies, waits for them, and re-layouts: 84.6 us -> none  [the longest x2 19.7 us: local(): grad_query = join_heads(grad_query.astype(bf16))]
    concatenate x10 -> x1, local copies, waits for them, and re-layouts: 139 us -> 93.4 us  [local(): jnp.concatenate([vga[0], vga[1], dwq.reshape(-1), vga[2], vga[3], grad_ta...]
    reduce_sum x14 -> x0, other arithmetic: 45 us -> none  [the longest x1 16.9 us: local(): score_sum = jnp.sum(grad_scores.astype(f32), 0).reshape(HEADS, span * span)]
    unnamed x4, waiting for transfers between devices: 194 us -> 220 us
    convert_element_type x8 -> x1, other arithmetic: 19.9 us -> 3.19 us  [local(): working = lax.all_gather(params.astype(BF16), 'opt', axis=0, tiled=True)]
  transfers between devices with their start and end apart: 3 -> 3, of which waited for: 3 -> 3; matrix products, arithmetic and copies ran while one was open for 5% -> 0% of each run, Pallas kernels for 0% -> 0%
where the time goes in v1:
time: 705 us; the launch traced here: 698 us
  waiting for transfers between devices  396 us (56%)
  Pallas kernels  149 us (21%)
  local copies, waits for them, and re-layouts  107 us (15%)
  other arithmetic  30.2 us (4%)
  between operations  15.3 us (2%)
    unnamed x4, waiting for transfers between devices  220 us
    all_gather x1, waiting for transfers between devices, local(): working = lax.all_gather(params.astype(BF16), 'opt', axis=0, tiled=True)  117 us
    concatenate x1, local copies, waits for them, and re-layouts, local(): jnp.concatenate([vga[0], vga[1], dwq.reshape(-1), vga[2], vga[3], grad_ta...  93.4 us
    psum x1, waiting for transfers between devices, local(): summed = lax.psum(local_grad.astype(BF16), 'dp')  58.4 us
    pallas_call x1, Pallas kernels, call_b(): pl.pallas_call(kernel_b, out_shape=outs, in_specs=[any_, any_, any_, vm,...  52.3 us
    pallas_call x1, Pallas kernels, call_c(): pl.pallas_call(kernel_c, out_shape=outs, in_specs=[any_] * 5 + [vm] * 3,...  50.2 us
    pallas_call x1, Pallas kernels, call_a(): pl.pallas_call(kernel_a, out_shape=outs, in_specs=[any_, any_, pl.BlockSp...  46.3 us
    sub x1, other arithmetic, adam_update(): weights - rate * (first_hat / (jnp.sqrt(second_hat) + 1e-08) + decay * we...  21.1 us
  transfers between devices with their start and end apart: 3, of which 3 were waited for; matrix products, arithmetic and copies ran while one was open for 0% of the time, Pallas kernels for 0%

profile of v1, /device:TPU:0, one launch (start us, length us, event | category | flops | bytes accessed | tf_op | source)
XLA Modules:
  0.0 698.2 jit_solution(136709605671948153)
XLA Ops:
  7.2 3.2 convert_element_type.8
  10.5 0.1 eq.15
  10.6 0.1 copy.22
  10.7 0.7 reshape.81.rel_ref
  12.1 117.0 %all-gather.2.cloned.1.call-done = bf16[3158016]{0:T(1024)(128)(2,1)} async-done(((bf16[789504]{0:T(1024)(128)(2,1)}), bf16[3158016]{0:T(1024)(128)(2,1)}) %all-gather.2.cloned.1.call-update) | async-done | bytes 6316048 | tf_op jit(solution)/shard_map/all_gather | solution.py:568
  129.0 46.3 %attend.1 = (bf16[512,1536]{1,0:T(8,128)(2,1)}, bf16[512,512]{1,0:T(8,128)(2,1)}, bf16[512,2048]{1,0:T(8,128)(2,1)}, bf16[2048,512]{1,0:T(8,128)(2,1)}, f32[16,5...) custom-call(bf16[14,14,8,512]{3,2,1,0:T(8,128)(2,1)} %bitcast.38, ...), custom_call_target="tpu_custom_call" | custom-call | tf_op jit(solution)/shard_map/attend/pallas_call | solution.py:284
  175.4 52.3 %mlp.1 = (bf16[14,14,8,512]{3,2,1,0:T(8,128)(2,1)}, f32[1568,512]{1,0:T(8,128)}, f32[512,512]{1,0:T(8,128)}, f32[512,2048]{1,0:T(8,128)}, f32[2048,512]{1,0:T(8,128)}, /*index=5*/f32[8,512]{1,0:T(8,128)}) custom-call(bf16[14,14,8,512]{3,2,1,0:T(8,128)(2,1)} %bitcast.39, bf16[14,14,8,512]{3,2,1,0:T(8,128)(2,1)} %bitcast.46, ...), custom_call_target="tpu_custom_call" | custom-call | tf_op jit(solution)/shard_map/mlp/pallas_call | solution.py:410
  227.7 50.2 %attend_back.1 = (f32[14,14,8,512]{3,2,1,0:T(8,128)}, f32[512,1536]{1,0:T(8,128)}, f32[8,512]{1,0:T(8,128)}, f32[4,64,256]{2,1,0:T(8,128)}) custom-call(bf16[14,14,8,512]{3,2,1,0:T(8,128)(2,1)} %bitcast.40, f32[1568,512]{1,0:T(8,128)} %get-tuple-element.43.dx1_hbm, bf16[1568,512]{1,0:T(8,128)(2,1)} %get-tuple-element.44.hw_hbm, ...), custom_call_target="tpu_custom_call" | custom-call | tf_op jit(solution)/shard_map/attend_back/pallas_call | solution.py:517
  277.9 0.7 convert.53
  278.7 0.1 slice_reduce_fusion
  278.7 2.1 convert.54
  280.9 2.9 reshape.82
  283.8 0.2 copy.21
  284.0 0.2 reshape.84
  284.2 0.9 fusion.17
  285.1 0.1 copy.20
  285.2 0.1 reshape.85
  285.4 2.6 convert_bitcast_fusion.1
  287.9 0.6 copy.24
  288.6 1.6 copy-done.1
  290.1 0.5 convert_bitcast_fusion
  290.6 2.4 copy.26
  293.0 0.1 convert_bitcast_fusion.2
  293.1 0.2 copy.23
  293.3 93.4 %concatenate.6 = bf16[3158016]{0:T(1024)(128)(2,1)} concatenate(bf16[512]{0:T(512)(128)(2,1)S(1)} %get-tuple-element.83, bf16[512]{0:T(512)(128)(2,1)S(1)} %get-tuple-element.84, bf16[786432]{0:T(1024)(128)(2,1)} %reshape.82, bf16[512]{0:T(512)(128)(2,1)S(1)} %get-tuple-element.85, bf16[512]{0:T(512)(128)(2,1)S(1)} %get-tuple-element.86, bf16[2704]{0:T(1024)(128)(2,1)S(1)} %reshape.85, ...), dimensions={0} | concatenate | bytes 12632064 | tf_op jit(solution)/shard_map/concatenate | solution.py:579
  386.9 0.6 copy-done.7
  387.4 0.6 dynamic-slice.8
  388.7 220.2 %all-reduce.7.cloned.1.call-done = bf16[3158016]{0:T(1024)(128)(2,1)} async-done(((bf16[3158016]{0:T(1024)(128)(2,1)}), bf16[3158016]{0:T(1024)(128)(2,1)}) %all-reduce.7.cloned.1.call-update) | async-done | bytes 6316048
  608.9 2.7 dynamic-slice.9
  611.6 0.7 fusion.19
  612.3 58.4 %all-reduce.5.cloned.1.call-done = bf16[789504]{0:T(1024)(128)(2,1)} async-done(((bf16[789504]{0:T(1024)(128)(2,1)}), bf16[789504]{0:T(1024)(128)(2,1)}) %all-reduce.5.cloned.1.call-update) | async-done | bytes 1579024 | tf_op jit(solution)/shard_map/psum | solution.py:582
  670.6 21.1 %multiply_subtract_fusion = (f32[789504]{0:T(1024)}, f32[789504]{0:T(1024)}, f32[789504]{0:T(1024)}, f32[789504]{0:T(1024)}) fusion(f32[789504]{0:T(1024)S(1)} %copy-done, f32[]{:T(128)} %bitcast.22, f32[]{:T(128)} %bitcast.21, f32[]{:T(128)} %bitcast.20, f32[]{:T(128)} %bitcast.19, f32[]{:T(128)} %bitcast.18, f32[]{:T(128)} %bitcast.17, f32[]{:T(128)} %bitcast.16, ...), kind=kLoop, calls=%fused_computation.2 | loop fusion | flops 45791232 | bytes 23685184 | tf_op jit(solution)/shard_map/sub | solution.py:561
  (26 shorter events, 0.3 us)
Async XLA Ops:
  7.2 3.3 copy-start.5
  7.2 121.9 %all-gather.2.cloned.1.call-start = ((), (), s32[]{:S(2)}) async-start(), calls=%async_computation | async-start | bytes 7895040 | tf_op jit(solution)/shard_map/all_gather | solution.py:568
  10.4 598.4 %all-reduce.7.cloned.1.call-start = ((), (), s32[]{:S(2)}) async-start(), calls=%async_computation.2 | async-start | bytes 12632064
  227.7 51.0 %copy-start.6 = (f32[8,512]{1,0:T(8,128)S(1)}, f32[8,512]{1,0:T(8,128)}, u32[]{:S(2)}) copy-start(f32[8,512]{1,0:T(8,128)} %get-tuple-element.53) | copy-start | bytes 49156
  278.7 5.1 copy-start.3
  287.9 2.2 copy-start.1
  290.6 2.4 copy-start.2
  386.8 0.7 copy-start.7
  386.8 224.8 %copy-start.4 = (f32[15]{0:T(128)S(1)}, f32[15]{0:T(128)}, u32[]{:S(2)}) copy-start(f32[15]{0:T(128)} %param.17) | copy-start | bytes 184
  386.8 283.8 %copy-start = (f32[789504]{0:T(1024)S(1)}, f32[789504]{0:T(1024)}, u32[]{:S(2)}) copy-start(f32[789504]{0:T(1024)} %param.14) | copy-start | bytes 9474052
  386.8 283.8 %all-reduce.5.cloned.1.call-start = ((), (), s32[]{:S(2)}) async-start(), calls=%async_computation.1 | async-start | bytes 3158016 | tf_op jit(solution)/shard_map/psum | solution.py:582
Sparse Core Ops, SparseCore 0:
  10.6 118.4 all-gather.1
  386.9 221.9 all-reduce.6
  612.7 57.8 all-reduce.4

commit v2 on v1

--- a/solution.py
+++ b/solution.py
@@ -1,4 +1,4 @@
-import math
+import functools
 import jax
 import jax.numpy as jnp
 from jax import lax
@@ -75,8 +75,12 @@
     return dev * r, r
 
 
-def unit_rows(ref3, unit, units):
-    return ref3[pl.ds(unit, units)].astype(F32).reshape(units * 8, 128)
+def pieces_to_rows(pn, wb, fs, shard, count, base):
+    def body(p, _):
+        row = pl.multiple_of((shard * pn.units - base + p * pn.pc) * 8, 8)
+        fs[pl.ds(row, pn.pc * 8), :] = wb[shard, p & 1, lax.shift_right_arithmetic(p, 1)].astype(F32).reshape(pn.pc * 8, 128)
+        return 0
+    lax.fori_loop(0, count, body, 0)
 
 
 def vec_from(fs, row, width, shift):
@@ -180,7 +184,7 @@
             bias[w * 4 + g] = jnp.where(k < SPAN, val, -1e30)
 
 
-def kernel_a(x_hbm, flat_hbm, rel_ref,
+def kernel_a(pn, x_hbm, flat_hbm, rel_ref,
              wqkv_o, wp_o, w1_o, w2_o, vec_o, hw_o, ob_o, qkv_o, p_o,
              x_v, flat_v, fs, os_, bias, wqkv, wp, w1, w2, vec, hw, ob, qkvb, pb, xsem, fsem, osem, wsem):
     cps = window_copies(x_hbm, x_v, xsem, True)
@@ -189,12 +193,9 @@
     fcp = pltpu.make_async_copy(flat_hbm, flat_v, fsem)
     fcp.start()
     fcp.wait()
-    nA = BROW // 8
-    def conv(t, _):
-        fs[pl.ds(pl.multiple_of(t * 128, 128), 128), :] = unit_rows(flat_v, t * 16, 16)
-        return 0
-    lax.fori_loop(0, nA // 16, conv, 0)
-    fs[(nA // 16) * 128:BROW + 8, :] = unit_rows(flat_v, (nA // 16) * 16, nA + 1 - (nA // 16) * 16)
+    for k in range(pn.ka):
+        pieces_to_rows(pn, flat_v, fs, k, pn.ndp, 0)
+    pieces_to_rows(pn, flat_v, fs, pn.ka, 1, 0)
     take_matrix(fs, R_QKV, wqkv, D, 12, False)
     vec[0:1, :] = vec_from(fs, R_G1, D, False)
     vec[1:2, :] = vec_from(fs, R_B1, D, False)
@@ -256,18 +257,16 @@
     cos = [pltpu.make_async_copy(a, b, osem.at[n]) for n, (a, b) in enumerate([(hw, hw_o), (ob, ob_o), (qkvb, qkv_o), (pb, p_o)])]
     for c in cos:
         c.start()
-    nB = flat_v.shape[0] - BROW // 8
-    def conv2(t, _):
-        fs[pl.ds(pl.multiple_of(t * 64, 64), 64), :] = unit_rows(flat_v, BROW // 8 + t * 8, 8)
-        return 0
-    lax.fori_loop(0, nB // 8, conv2, 0)
-    take_matrix(fs, R_PROJ - BROW, wp, D, 4, True)
-    take_matrix(fs, R_W1 - BROW, w1, D, 16, True)
-    take_matrix(fs, R_W2 - BROW, w2, HID, 4, True)
+    for k in range(pn.ka, pn.ns):
+        pieces_to_rows(pn, flat_v, fs, k, pn.ndp, pn.base)
+    first = pn.base * 8
+    take_matrix(fs, R_PROJ - first, wp, D, 4, True)
+    take_matrix(fs, R_W1 - first, w1, D, 16, True)
+    take_matrix(fs, R_W2 - first, w2, HID, 4, True)
     for n, r in enumerate((R_BP, R_G2, R_B2, R_C2)):
-        vec[4 + n:5 + n, :] = vec_from(fs, r - BROW, D, True)
+        vec[4 + n:5 + n, :] = vec_from(fs, r - first, D, True)
     for n in range(4):
-        vec[8 + n:9 + n, :] = vec_from(fs, R_C1 - BROW + 4 * n, D, True)
+        vec[8 + n:9 + n, :] = vec_from(fs, R_C1 - first + 4 * n, D, True)
     wos = [pltpu.make_async_copy(a, b, wsem.at[n]) for n, (a, b) in enumerate([(wqkv, wqkv_o), (wp, wp_o), (w1, w1_o), (w2, w2_o), (vec, vec_o)])]
     for c in wos:
         c.start()
@@ -275,19 +274,18 @@
         c.wait()
 
 
-def call_a(x, flat, rel):
-    units = flat.shape[0]
+def call_a(pn, x, flat, rel):
     any_ = pl.BlockSpec(memory_space=pl.ANY)
     sds = jax.ShapeDtypeStruct
     outs = [sds((D, 3 * D), BF16), sds((D, D), BF16), sds((D, HID), BF16), sds((HID, D), BF16), sds((16, D), F32),
             sds((ROWS, D), BF16), sds((ROWS, D), BF16), sds((WB, 12, 64, 128), BF16), sds((WB, 4, 64, 256), BF16)]
     return pl.pallas_call(
-        kernel_a,
+        functools.partial(kernel_a, pn),
         out_shape=outs,
         in_specs=[any_, any_, pl.BlockSpec(memory_space=pltpu.VMEM)],
         out_specs=[any_] * len(outs),
         scratch_shapes=[
-            pltpu.VMEM((28, 7, 8, D), BF16), pltpu.VMEM((units, 8, 128), BF16), pltpu.VMEM((12 * RS, 128), F32), pltpu.VMEM((4 * RS, 128), F32),
+            pltpu.VMEM((28, 7, 8, D), BF16), pltpu.VMEM(flat.shape, BF16), pltpu.VMEM((12 * RS, 128), F32), pltpu.VMEM((4 * RS, 128), F32),
             pltpu.VMEM((16, 64, 256), F32), pltpu.VMEM((D, 3 * D), BF16), pltpu.VMEM((D, D), BF16), pltpu.VMEM((D, HID), BF16), pltpu.VMEM((HID, D), BF16),
             pltpu.VMEM((16, D), F32), pltpu.VMEM((ROWS, D), BF16), pltpu.VMEM((ROWS, D), BF16), pltpu.VMEM((WB, 12, 64, 128), BF16), pltpu.VMEM((WB, 4, 64, 256), BF16),
             pltpu.SemaphoreType.DMA((NSEG,)), pltpu.SemaphoreType.DMA, pltpu.SemaphoreType.DMA((4,)), pltpu.SemaphoreType.DMA((5,)),
@@ -315,17 +313,28 @@
     return cdf, e * INV_SQRT2PI
 
 
-def put_matrix(fs, row, get, nrows, ncb, step=128):
-    lane = lax.broadcasted_iota(jnp.int32, (step, 128), 1)
+def put_block(fs, start, stride, v):
+    n = v.shape[0]
+    lane = lax.broadcasted_iota(jnp.int32, (n, 128), 1)
+    v = pltpu.roll(v, LANE, 1)
+    here = pl.ds(start, n, stride=stride) if n > 1 else pl.ds(start, 1)
+    fs[here, :] = jnp.where(lane >= LANE, v, fs[here, :])
+    here = pl.ds(start + 1, n, stride=stride) if n > 1 else pl.ds(start + 1, 1)
+    fs[here, :] = jnp.where(lane < LANE, v, fs[here, :])
+
+
+def put_vec(fs, row, v):
+    for c in range(v.shape[1] // 128):
+        put_block(fs, row + c, 1, v[:, c * 128:(c + 1) * 128])
 
 
 def acc_rows(ref, i, v):
     ref[8 * i:8 * i + 8, 0:v.shape[1]] += jnp.sum(v.reshape(v.shape[0] // 8, 8, v.shape[1]), 0)
 
 
-def kernel_b(x_hbm, cot_hbm, ob_hbm, wp, w1, w2, vec, counts,
-             y_hbm, dx1_o, dwp_o, dw1_o, dw2_o, vg_o,
-             x_v, dy_v, ob, yv, a, du, h2, dx1, e, acc, xsem, csem, ysem, osem):
+def kernel_b(pn, x_hbm, cot_hbm, ob_hbm, wp, w1, w2, vec, counts,
+             y_hbm, dx1_o, gb_o,
+             x_v, dy_v, ob, yv, a, du, h2, dx1, e, acc, fs, gflat, xsem, csem, ysem, osem, gsem):
     cps = window_copies(x_hbm, x_v, xsem, True) + window_copies(cot_hbm, dy_v, csem, True)
     cps.append(pltpu.make_async_copy(ob_hbm, ob, osem.at[0]))
     for c in cps:
@@ -381,49 +390,110 @@
         c.start()
     dcp = pltpu.make_async_copy(dx1, dx1_o, osem.at[1])
     dcp.start()
-    vg_o[...] = jnp.sum(acc[...].reshape(8, 8, D), 1)
+    vg = jnp.sum(acc[...].reshape(8, 8, D), 1)
     dyf = dy_v[...].reshape(ROWS, D)
+    first = pn.base * 8
+    nrow = pn.bunits * 8
+    lo = (R_PROJ // 8 + 1) * 8 - first
+    hi = R_END // 8 * 8 - first
+    fs[0:lo, :] = jnp.zeros((lo, 128), F32)
+    fs[hi:nrow, :] = jnp.zeros((nrow - hi, 128), F32)
 
     def w2rows(t, _):
         r0 = pl.multiple_of(t * 256, 256)
-        dw2_o[pl.ds(r0, 256), :] = dot_tn(a[:, pl.ds(r0, 256)], dyf)
+        v = dot_tn(a[:, pl.ds(r0, 256)], dyf)
+        for c in range(4):
+            put_block(fs, R_W2 - first + r0 * 4 + c, 4, v[:, c * 128:(c + 1) * 128])
         return 0
     lax.fori_loop(0, HID // 256, w2rows, 0)
 
     def w1rows(t, _):
         r0 = pl.multiple_of(t * 256, 256)
-        dw1_o[:, pl.ds(r0, 256)] = dot_tn(h2[...], du[:, pl.ds(r0, 256)])
+        v = dot_tn(h2[...], du[:, pl.ds(r0, 256)])
+        for c in range(2):
+            put_block(fs, R_W1 - first + 2 * t + c, 16, v[:, c * 128:(c + 1) * 128])
         return 0
     lax.fori_loop(0, HID // 256, w1rows, 0)
-    dwp_o[...] = dot_tn(ob[...], e[...])
+    v = dot_tn(ob[...], e[...])
+    for c in range(4):
+        put_block(fs, R_PROJ - first + c, 4, v[:, c * 128:(c + 1) * 128])
+    for row, n in ((R_BP, 3), (R_G2, 1), (R_B2, 2), (R_C2, 0)):
+        put_vec(fs, row - first, vg[n:n + 1])
+    for j in range(4):
+        put_vec(fs, R_C1 - first + 4 * j, vg[4 + j:5 + j])
+
+    def low(t, _):
+        gflat[pl.ds(t * 32, 32)] = fs[pl.ds(pl.multiple_of(t * 256, 256), 256), :].reshape(32, 8, 128).astype(BF16)
+        return 0
+    lax.fori_loop(0, pn.bunits // 32, low, 0)
+    n = pn.bunits % 32
+    if n:
+        gflat[pn.bunits - n:pn.bunits] = fs[nrow - 8 * n:nrow, :].reshape(n, 8, 128).astype(BF16)
+    gcs = []
+    for k in range(pn.nk):
+        for p in range(pn.ndp):
+            gcs.append(pltpu.make_async_copy(gflat.at[pl.ds(k * pn.units + p * pn.pc, pn.pc)], gb_o.at[p & 1, p >> 1, pl.ds(k * pn.pc, pn.pc)], gsem.at[k * pn.ndp + p]))
+    for cp in gcs:
+        cp.start()
+    for cp in gcs:
+        cp.wait()
     dcp.wait()
-    for c in ycs:
-        c.wait()
-
-
-def call_b(x, cot, ob, wp, w1, w2, vec, counts):
+    for cp in ycs:
+        cp.wait()
+
+
+def call_b(pn, x, cot, ob, wp, w1, w2, vec, counts):
     any_ = pl.BlockSpec(memory_space=pl.ANY)
     vm = pl.BlockSpec(memory_space=pltpu.VMEM)
     sds = jax.ShapeDtypeStruct
-    outs = [sds((14, 14, 8, D), BF16), sds((ROWS, D), F32), sds((D, D), F32), sds((D, HID), F32), sds((HID, D), F32), sds((8, D), F32)]
+    outs = [sds((14, 14, 8, D), BF16), sds((ROWS, D), F32), sds((2, pn.rest, pn.nk * pn.pc, 8, 128), BF16)]
     big = pltpu.VMEM((28, 7, 8, D), BF16)
     return pl.pallas_call(
-        kernel_b,
+        functools.partial(kernel_b, pn),
         out_shape=outs,
         in_specs=[any_, any_, any_, vm, vm, vm, vm, pl.BlockSpec(memory_space=pltpu.SMEM)],
-        out_specs=[any_, any_, vm, vm, vm, vm],
+        out_specs=[any_] * 3,
         scratch_shapes=[
             big, big, pltpu.VMEM((ROWS, D), BF16), big, pltpu.VMEM((ROWS, HID), BF16), pltpu.VMEM((ROWS, HID), BF16), pltpu.VMEM((ROWS, D), BF16),
             pltpu.VMEM((ROWS, D), F32), pltpu.VMEM((ROWS, D), BF16), pltpu.VMEM((64, D), F32),
+            pltpu.VMEM((pn.bunits * 8, 128), F32), pltpu.VMEM((pn.bunits, 8, 128), BF16),
             pltpu.SemaphoreType.DMA((NSEG,)), pltpu.SemaphoreType.DMA((NSEG,)), pltpu.SemaphoreType.DMA((NSEG,)), pltpu.SemaphoreType.DMA((2,)),
+            pltpu.SemaphoreType.DMA((pn.nk * pn.ndp,)),
         ],
         compiler_params=pltpu.CompilerParams(vmem_limit_bytes=64000000),
         name="mlp",
     )(x, cot, ob, wp, w1, w2, vec, counts)
 
 
-def kernel_c(x_hbm, dx1_hbm, hw_hbm, qkv_hbm, p_hbm, wqkv, wp, vec,
-             dx_hbm, dwq_o, vg_o, dtab_o,
+def table_grad(rel_ref, big, dtab):
+    lane = lax.broadcasted_iota(jnp.int32, (32, 128), 1)
+    for g in range(4):
+        for pair in range(2):
+            at = 1024 + g * 256 + pair * 128
+            big[at:at + 64, :] = dtab[g, :, pair * 128:pair * 128 + 128]
+    for g in range(4):
+        for pair in range(2):
+            at = 1024 + g * 256 + pair * 128
+            even = big[pl.ds(at, 32, stride=2), :]
+            odd = big[pl.ds(at + 1, 32, stride=2), :]
+            h = 4 * g + 2 * pair
+            big[pl.ds(h, 32, stride=16), :] = jnp.where(lane < 64, even, pltpu.roll(odd, 64, 1))
+            big[pl.ds(h + 1, 32, stride=16), :] = jnp.where(lane < 64, pltpu.roll(even, 64, 1), odd)
+    rel = rel_ref[...]
+    row = lax.shift_right_arithmetic(rel, 3)
+    low = rel & 7
+    oh = (lax.broadcasted_iota(jnp.int32, (32, 4096), 0) == row).astype(F32).astype(BF16)
+    grad = jnp.concatenate([big[kk * 16:kk * 16 + 16, :] for kk in range(32)], 1)
+    out = jnp.zeros((32, 128), F32)
+    high = grad.astype(BF16).astype(F32)
+    for part in (high, grad - high):
+        m = jnp.concatenate([jnp.where(low == j, part, 0.0) for j in range(8)], 0).astype(BF16)
+        out = out + dot_nt(oh, m)
+    return out
+
+
+def kernel_c(pn, x_hbm, dx1_hbm, hw_hbm, qkv_hbm, p_hbm, wqkv, wp, vec, rel_ref,
+             dx_hbm, gm, gs,
              x_v, dx1, hw, qkvb, pb, fs, os_, dq, dxv, dtab, acc, xsem, isem, psem, ysem):
     cps = window_copies(x_hbm, x_v, xsem, True)
     ins = [pltpu.make_async_copy(a, b, isem.at[n]) for n, (a, b) in enumerate([(dx1_hbm, dx1), (hw_hbm, hw), (qkv_hbm, qkvb), (p_hbm, pb)])]
@@ -496,29 +566,39 @@
     ycs = window_copies(dx_hbm, dxv, ysem, False)
     for c in ycs:
         c.start()
-    vg_o[...] = jnp.sum(acc[...].reshape(8, 8, D), 1)
+    vg = jnp.sum(acc[...].reshape(8, 8, D), 1)
+    tab = table_grad(rel_ref, os_, dtab)
+    small = [vg[n:n + 1, c * 128:(c + 1) * 128] for n in range(4) for c in range(4)]
+    small = [jnp.concatenate(small[:8], 0), jnp.concatenate(small[8:], 0), tab[0:8], tab[8:16], tab[16:24]]
+    gs[...] = jnp.zeros_like(gs)
+    for n, v in enumerate(small):
+        gs[n & 1, n >> 1, 0] = v.astype(BF16)
     ins[1].wait()
 
     def wq(t, _):
         c0 = pl.multiple_of(t * 256, 256)
-        dwq_o[:, pl.ds(c0, 256)] = dot_tn(hw[...], dq[:, pl.ds(c0, 256)])
+        v = dot_tn(hw[...], dq[:, pl.ds(c0, 256)])
+        mu = pn.mrow // 8
+        for i in range(2):
+            u = v[:, i * 128:(i + 1) * 128].reshape(D // 8, 8, 128).astype(BF16)
+            for p in range(pn.ndp):
+                gm[p & 1, p >> 1, pl.ds((2 * t + i) * mu, mu)] = u[p * mu:(p + 1) * mu]
         return 0
     lax.fori_loop(0, 6, wq, 0)
-    dtab_o[...] = dtab[...]
     for c in ycs:
         c.wait()
 
 
-def call_c(x, dx1, hw, qkv, p, wqkv, wp, vec):
+def call_c(pn, x, dx1, hw, qkv, p, wqkv, wp, vec, rel):
     any_ = pl.BlockSpec(memory_space=pl.ANY)
     vm = pl.BlockSpec(memory_space=pltpu.VMEM)
     sds = jax.ShapeDtypeStruct
-    outs = [sds((14, 14, 8, D), F32), sds((D, 3 * D), F32), sds((8, D), F32), sds((4, 64, 256), F32)]
+    outs = [sds((14, 14, 8, D), F32), sds((2, pn.rest, 12 * pn.mrow // 8, 8, 128), BF16), sds((2, pn.rest, 1, 8, 128), BF16)]
     return pl.pallas_call(
-        kernel_c,
+        functools.partial(kernel_c, pn),
         out_shape=outs,
-        in_specs=[any_] * 5 + [vm] * 3,
-        out_specs=[any_, vm, vm, vm],
+        in_specs=[any_] * 5 + [vm] * 4,
+        out_specs=[any_, vm, vm],
         scratch_shapes=[
             pltpu.VMEM((28, 7, 8, D), BF16), pltpu.VMEM((ROWS, D), F32), pltpu.VMEM((ROWS, D), BF16), pltpu.VMEM((WB, 12, 64, 128), BF16), pltpu.VMEM((WB, 4, 64, 256), BF16),
             pltpu.VMEM((12 * RS, 128), F32), pltpu.VMEM((4 * RS, 128), F32), pltpu.VMEM((ROWS, 3 * D), BF16), pltpu.VMEM((28, 7, 8, D), F32),
@@ -527,66 +607,375 @@
         ],
         compiler_params=pltpu.CompilerParams(vmem_limit_bytes=64000000),
         name="attend_back",
-    )(x, dx1, hw, qkv, p, wqkv, wp, vec)
+    )(x, dx1, hw, qkv, p, wqkv, wp, vec, rel)
+
+
+import functools
+
+MESH = pl.DeviceIdType.MESH
+NMAT = 768
+
+
+class Plan:
+    def __init__(self, mesh, shard_len):
+        self.ndp = mesh.shape["dp"]
+        self.ns = mesh.shape["opt"]
+        self.rest = self.ndp // 2
+        self.units = shard_len // 1024
+        self.pc = -(-self.units // self.ndp)
+        self.ka = (BROW // 8) // self.units
+        self.nk = self.ns - self.ka
+        self.base = self.ka * self.units
+        self.bunits = (self.nk - 1) * self.units + self.ndp * self.pc
+        self.mrow = D // self.ndp
+        self.gunits = max(BROW // 8 + 1, self.ndp * self.pc)
+
+
+def place():
+    me = lax.axis_index("dp")
+    return lax.shift_right_arithmetic(me, 1), me & 1, lax.axis_index("opt")
+
+
+def peer(r, c):
+    return {"dp": 2 * r + c}
+
+
+def enter(pn):
+    r, c, z = place()
+    bar = pltpu.get_barrier_semaphore()
+    pl.semaphore_signal(bar, inc=1, device_id=peer(r, 1 - c), device_id_type=MESH)
+    for j in range(1, pn.rest):
+        pl.semaphore_signal(bar, inc=1, device_id=peer(lax.rem(r + j, pn.rest), c), device_id_type=MESH)
+    for j in range(1, pn.ns):
+        pl.semaphore_signal(bar, inc=1, device_id={"opt": lax.rem(z + j, pn.ns)}, device_id_type=MESH)
+    pl.semaphore_wait(bar, pn.rest + pn.ns - 1)
+
+
+def remote(src, dst, sems, n, where):
+    return pltpu.make_async_remote_copy(src_ref=src, dst_ref=dst, send_sem=sems.at[0, n], recv_sem=sems.at[1, n], device_id=where, device_id_type=MESH)
+
+
+class Chunk:
+    def __init__(self, pn, n, scattered, last, src, r1, s1, r2, r3, ag, sems, lsem):
+        self.pn, self.n, self.scattered, self.last = pn, n, scattered, last
+        self.m = n // pn.nk if scattered else n
+        self.src, self.r1, self.s1, self.r2, self.r3, self.ag, self.sems, self.lsem = src, r1, s1, r2, r3, ag, sems, lsem
+        self.k2 = 1
+        self.k3 = self.k2 + pn.rest - 1
+        self.k4 = self.k3 + pn.ns - 1
+        self.k5 = self.k4 + pn.rest - 1
+
+    @staticmethod
+    def nsems(pn):
+        return 2 * pn.rest + pn.ns - 1
+
+    def here(self, z):
+        return z >= self.pn.ka if self.scattered else z <= self.last
+
+    def c1(self):
+        r, c, z = place()
+        return remote(self.src.at[1 - c], self.r1, self.sems, 0, peer(r, 1 - c))
+
+    def local(self):
+        r, c, z = place()
+        return pltpu.make_async_copy(self.src.at[c], self.s1, self.lsem)
+
+    def start1(self):
+        self.c1().start()
+        self.local().start()
+
+    def c2(self, j):
+        r, c, z = place()
+        to = lax.rem(r + j, self.pn.rest)
+        return remote(self.s1.at[to], self.r2.at[j - 1], self.sems, self.k2 + j - 1, peer(to, c))
+
+    def start2(self):
+        r, c, z = place()
+        self.local().wait()
+        self.c1().wait()
+        step = self.m
+        for j in list(range(1, self.pn.rest)) + [0]:
+            to = lax.rem(r + j, self.pn.rest)
+
+            def add(t, _):
+                u = pl.ds(t * step, step)
+                self.s1[to, u] = (self.s1[to, u].astype(F32) + self.r1[to, u].astype(F32)).astype(BF16)
+                return 0
+            lax.fori_loop(0, self.n // step, add, 0)
+            if j:
+                self.c2(j).start()
+
+    def c3(self, j):
+        r, c, z = place()
+        to = lax.rem(z + j, self.pn.ns)
+        if self.scattered:
+            src = self.s1.at[r, pl.ds(lax.max(to - self.pn.ka, 0) * self.m, self.m)]
+        else:
+            src = self.s1.at[r]
+        return to, remote(src, self.r3.at[j - 1], self.sems, self.k3 + j - 1, {"opt": to})
+
+    def start3(self):
+        r, c, z = place()
+        for j in range(1, self.pn.rest):
+            self.c2(j).wait()
+        step = self.m
+
+        def add(t, _):
+            u = pl.ds(t * step, step)
+            v = self.s1[r, u].astype(F32)
+            for j in range(1, self.pn.rest):
+                v = v + self.r2[j - 1, u].astype(F32)
+            self.s1[r, u] = v.astype(BF16)
+            return 0
+        lax.fori_loop(0, self.n // step, add, 0)
+        for j in range(1, self.pn.ns):
+            to, cp = self.c3(j)
+
+            @pl.when(self.here(to))
+            def _():
+                cp.start()
+
+    def c4(self, j):
+        r, c, z = place()
+        return remote(self.ag.at[c, r], self.ag.at[c, r], self.sems, self.k4 + j - 1, peer(lax.rem(r + j, self.pn.rest), c))
+
+    def start4(self):
+        r, c, z = place()
+        for j in range(1, self.pn.ns):
+            to, cp = self.c3(j)
+
+            @pl.when(self.here(to))
+            def _():
+                cp.wait_send()
+
+        @pl.when(self.here(z))
+        def _():
+            for j in range(1, self.pn.ns):
+                self.c3(j)[1].wait_recv()
+            if self.scattered:
+                own = self.s1[r, pl.ds((z - self.pn.ka) * self.m, self.m)]
+            else:
+                own = self.s1[r]
+            v = own.astype(F32)
+            for j in range(1, self.pn.ns):
+                v = v + self.r3[j - 1].astype(F32)
+            self.ag[c, r] = v.astype(BF16)
+            for j in range(1, self.pn.rest):
+                self.c4(j).start()
+
+    def c5(self):
+        r, c, z = place()
+        return remote(self.ag.at[c], self.ag.at[c], self.sems, self.k5, peer(r, 1 - c))
+
+    def start5(self):
+        r, c, z = place()
+
+        @pl.when(self.here(z))
+        def _():
+            for j in range(1, self.pn.rest):
+                self.c4(j).wait()
+            self.c5().start()
+
+    def finish(self):
+        r, c, z = place()
+
+        @pl.when(self.here(z))
+        def _():
+            self.c5().wait()
+
+
+def chunk_scratch(pn, n, m):
+    return [pltpu.VMEM((pn.rest, n, 8, 128), BF16), pltpu.VMEM((pn.rest, n, 8, 128), BF16), pltpu.VMEM((pn.rest - 1, n, 8, 128), BF16),
+            pltpu.VMEM((pn.ns - 1, m, 8, 128), BF16), pltpu.VMEM((2, pn.rest, m, 8, 128), BF16),
+            pltpu.SemaphoreType.DMA((2, Chunk.nsems(pn))), pltpu.SemaphoreType.DMA]
+
+
+GROUP_ROWS = [R_G1, R_B1, R_QKV, R_BQ, R_BV, R_TAB]
+STEP = 2
+DECAYED = (2, 6, 10, 12)
+LENGTHS = [D, D, 3 * D * D, D, D, TAB * HEADS, D * D, D, D, D, D * HID, HID, HID * D, D]
+
+
+def adam_units(pn, rates, g, p_v, m_v, w_v, g_v, goff, first, u0, n):
+    sl = pl.ds(u0, n)
+    grad = g[pl.ds((goff + u0) * 8, n * 8), :].reshape(n, 8, 128)
+    shape = (n, 8, 128)
+    index = ((first + u0 + lax.broadcasted_iota(jnp.int32, shape, 0)) * 8 + lax.broadcasted_iota(jnp.int32, shape, 1)) * 128 + lax.broadcasted_iota(jnp.int32, shape, 2)
+    rate = jnp.zeros(shape, F32) + rates[0]
+    decay = jnp.zeros(shape, F32)
+    at = 0
+    for n_, length in enumerate(LENGTHS):
+        at += length
+        after = index >= at
+        rate = jnp.where(after, rates[n_ + 1], rate)
+        if n_ in DECAYED or n_ + 1 in DECAYED:
+            decay = jnp.where(after, 0.05 if n_ + 1 in DECAYED else 0.0, decay)
+    w = p_v[sl]
+    m = 0.9 * m_v[sl] + 0.1 * grad
+    s = 0.999 * w_v[sl] + 0.001 * grad * grad
+    mh = m / (1.0 - 0.9 ** STEP)
+    sh = s / (1.0 - 0.999 ** STEP)
+    p_v[sl] = w - rate * (mh / (jnp.sqrt(sh) + 1e-08) + decay * w)
+    m_v[sl] = m
+    w_v[sl] = s
+    g_v[sl] = grad
+
+
+def spread_grad(pn, g, agb, agm, ags):
+    r, c, z = place()
+
+    @pl.when(z >= pn.ka)
+    def _():
+        def piece(p, _):
+            g[pl.ds(p * pn.pc * 8, pn.pc * 8), :] = agb[p & 1, lax.shift_right_arithmetic(p, 1)].astype(F32).reshape(pn.pc * 8, 128)
+            return 0
+        lax.fori_loop(0, pn.ndp, piece, 0)
+
+    @pl.when(z < pn.ka)
+    def _():
+        def piece(p, _):
+            for col in range(12):
+                v = agm[p & 1, lax.shift_right_arithmetic(p, 1), col * (pn.mrow // 8):(col + 1) * (pn.mrow // 8)].astype(F32).reshape(pn.mrow, 128)
+                g[pl.ds(R_QKV + p * pn.mrow * 12 + col, pn.mrow, stride=12), :] = v
+            return 0
+        lax.fori_loop(0, pn.ndp, piece, 0)
+        for n, u in enumerate((0, 769, 770, 771, 772)):
+            g[u * 8:u * 8 + 8, :] = ags[n & 1, n >> 1, 0].astype(F32)
+
+    @pl.when(z == pn.ka)
+    def _():
+        for n, u in enumerate((0, 769, 770, 771, 772)):
+            if u >= pn.base:
+                k = (u - pn.base) * 8
+                g[k:k + 8, :] += ags[n & 1, n >> 1, 0].astype(F32)
+
+
+def kernel_d(pn, gb, gm, gs, rates, params, mom1, mom2, *rest):
+    (grad_o, p_o, m_o, w_o, rb1, sb1, rb2, rb3, agb, semb, lb, rm1, sm1, rm2, rm3, agm, semm, lm, rs1, ss1, rs2, rs3, ags, sems, ls,
+     g, g_v, p_v, m_v, w_v, isem, osem) = rest
+    ins = [pltpu.make_async_copy(a, b, isem.at[n]) for n, (a, b) in enumerate([(params, p_v), (mom1, m_v), (mom2, w_v)])]
+    for cp in ins:
+        cp.start()
+    enter(pn)
+    chunks = [Chunk(pn, pn.nk * pn.pc, True, 0, gb, rb1, sb1, rb2, rb3, agb, semb, lb),
+              Chunk(pn, 12 * pn.mrow // 8, False, pn.ka - 1, gm, rm1, sm1, rm2, rm3, agm, semm, lm),
+              Chunk(pn, 1, False, pn.ka, gs, rs1, ss1, rs2, rs3, ags, sems, ls)]
+    for step in ("start1", "start2", "start3", "start4", "start5", "finish"):
+        for ch in chunks:
+            getattr(ch, step)()
+    spread_grad(pn, g, agb, agm, ags)
+    r, c, z = place()
+    goff = lax.select(z < pn.ka, z * pn.units, 0)
+    first = z * pn.units
+    for cp in ins:
+        cp.wait()
+    blk = 32
+    full = pn.units // blk
+
+    def body(t, _):
+        adam_units(pn, rates, g, p_v, m_v, w_v, g_v, goff, first, t * blk, blk)
+        return 0
+    lax.fori_loop(0, full, body, 0)
+    if pn.units % blk:
+        adam_units(pn, rates, g, p_v, m_v, w_v, g_v, goff, first, full * blk, pn.units % blk)
+    outs = [pltpu.make_async_copy(a, b, osem.at[n]) for n, (a, b) in enumerate([(g_v, grad_o), (p_v, p_o), (m_v, m_o), (w_v, w_o)])]
+    for cp in outs:
+        cp.start()
+    for cp in outs:
+        cp.wait()
+
+
+def call_d(pn, gb, gm, gs, rates, params, mom1, mom2):
+    any_ = pl.BlockSpec(memory_space=pl.ANY)
+    shard = jax.ShapeDtypeStruct((pn.units, 8, 128), F32)
+    sv = pltpu.VMEM((pn.units, 8, 128), F32)
+    view = lambda t: t.reshape(pn.units, 8, 128)
+    out = pl.pallas_call(
+        functools.partial(kernel_d, pn),
+        out_shape=[shard] * 4,
+        in_specs=[any_] * 3 + [pl.BlockSpec(memory_space=pltpu.SMEM)] + [any_] * 3,
+        out_specs=[any_] * 4,
+        scratch_shapes=chunk_scratch(pn, pn.nk * pn.pc, pn.pc) + chunk_scratch(pn, 12 * pn.mrow // 8, 12 * pn.mrow // 8) + chunk_scratch(pn, 1, 1)
+        + [pltpu.VMEM((pn.gunits * 8, 128), F32), sv, sv, sv, sv, pltpu.SemaphoreType.DMA((3,)), pltpu.SemaphoreType.DMA((4,))],
+        compiler_params=pltpu.CompilerParams(vmem_limit_bytes=64000000, collective_id=1, has_side_effects=True),
+        name="reduce",
+    )(gb, gm, gs, rates, view(params), view(mom1), view(mom2))
+    return [t.reshape(-1) for t in out]
+
+
+def kernel_g(pn, params, w_o, p_v, wb, sems, isem, osem):
+    r, c, z = place()
+    cp = pltpu.make_async_copy(params, p_v.at[pl.ds(0, pn.units)], isem)
+    cp.start()
+    enter(pn)
+    cp.wait()
+
+    def cast(p, _):
+        wb[z, p & 1, lax.shift_right_arithmetic(p, 1)] = p_v[pl.ds(p * pn.pc, pn.pc)].astype(BF16)
+        return 0
+    lax.fori_loop(0, pn.ndp, cast, 0)
+
+    def o(j):
+        to = lax.rem(z + j, pn.ns)
+        return remote(wb.at[z, c, r], wb.at[z, c, r], sems, j - 1, {"opt": to})
+
+    def x(k, j):
+        to = lax.rem(r + j, pn.rest)
+        src = lax.rem(z - k + pn.ns, pn.ns)
+        return remote(wb.at[src, c, r], wb.at[src, c, r], sems, pn.ns - 1 + (k - 1) * (pn.rest - 1) + j - 1, peer(to, c))
+
+    def y(k):
+        src = lax.rem(z - k + pn.ns, pn.ns)
+        return remote(wb.at[src, c], wb.at[src, c], sems, (pn.ns - 1) * pn.rest + k - 1, peer(r, 1 - c))
+
+    for j in range(1, pn.ns):
+        o(j).start()
+    for k in range(1, pn.ns):
+        o(k).wait()
+        for j in range(1, pn.rest):
+            x(k, j).start()
+    for k in range(1, pn.ns):
+        for j in range(1, pn.rest):
+            x(k, j).wait()
+        y(k).start()
+    for k in range(1, pn.ns):
+        y(k).wait()
+    cp = pltpu.make_async_copy(wb, w_o, osem)
+    cp.start()
+    cp.wait()
+
+
+def call_g(pn, params):
+    any_ = pl.BlockSpec(memory_space=pl.ANY)
+    shape = (pn.ns, 2, pn.rest, pn.pc, 8, 128)
+    nsem = (pn.ns - 1) * (pn.rest + 1)
+    return pl.pallas_call(
+        functools.partial(kernel_g, pn),
+        out_shape=jax.ShapeDtypeStruct(shape, BF16),
+        in_specs=[any_],
+        out_specs=any_,
+        scratch_shapes=[pltpu.VMEM((pn.ndp * pn.pc, 8, 128), F32), pltpu.VMEM(shape, BF16), pltpu.SemaphoreType.DMA((2, nsem)), pltpu.SemaphoreType.DMA, pltpu.SemaphoreType.DMA],
+        compiler_params=pltpu.CompilerParams(vmem_limit_bytes=64000000, collective_id=0, has_side_effects=True),
+        name="gather",
+    )(params.reshape(pn.units, 8, 128))
 
 
 from jax.sharding import PartitionSpec as P
 
-STEP = 2
-HIGH = lax.Precision.HIGHEST
-DECAY = [0.0, 0.0, 0.05, 0.0, 0.0, 0.0, 0.05, 0.0, 0.0, 0.0, 0.05, 0.0, 0.05, 0.0, 0.0]
-
-
-def group_starts():
-    lengths = [D, D, 3 * D * D, D, D, TAB * HEADS, D * D, D, D, D, D * HID, HID, HID * D, D]
-    starts = [0]
-    for length in lengths:
-        starts.append(starts[-1] + length)
-    return starts
-
-
-def adam_update(weights, first, second, grad, rates, start):
-    index = start + lax.iota(jnp.int32, weights.shape[0])
-    starts = group_starts()
-    rate = jnp.zeros_like(weights) + rates[0]
-    decay = jnp.zeros_like(weights)
-    for group in range(1, len(starts)):
-        after = index >= starts[group]
-        rate = jnp.where(after, rates[group], rate)
-        decay = jnp.where(after, DECAY[group], decay)
-    first_new = 0.9 * first + 0.1 * grad
-    second_new = 0.999 * second + 0.001 * grad * grad
-    first_hat = first_new / (1.0 - 0.9**STEP)
-    second_hat = second_new / (1.0 - 0.999**STEP)
-    weights_new = weights - rate * (first_hat / (jnp.sqrt(second_hat) + 1e-08) + decay * weights)
-    return (weights_new, first_new, second_new)
-
-
-def local(images, cotangent, counts, rel_index, params, moment1, moment2, rates):
-    shard_len = params.shape[0]
-    total_len = shard_len * lax.axis_size("opt")
-    working = lax.all_gather(params.astype(BF16), "opt", axis=0, tiled=True)
-    starts = group_starts()
-    xt = images.transpose(1, 2, 0, 3)
-    ct = cotangent.transpose(1, 2, 0, 3)
-    flat = working.reshape(-1, 8, 128)
-    wqkv, wp, w1, w2, vec, hw, ob, qkv, p = call_a(xt, flat, rel_lanes(rel_index))
-    y, dx1, dwp, dw1, dw2, vgb = call_b(xt, ct, ob, wp, w1, w2, vec, counts)
-    dx, dwq, vga, dtab = call_c(xt, dx1, hw, qkv, p, wqkv, wp, vec)
-    score = dtab.reshape(4, 64, 4, 64)[:, :SPAN, :, :SPAN].transpose(0, 2, 3, 1).reshape(HEADS, SPAN * SPAN)
-    onehot = rel_index.reshape(-1)[:, None] == lax.iota(jnp.int32, TAB)[None, :]
-    grad_table = jnp.dot(score, onehot.astype(F32), precision=HIGH).T.reshape(-1)
-    local_grad = jnp.concatenate([
-        vga[0], vga[1], dwq.reshape(-1), vga[2], vga[3], grad_table, dwp.reshape(-1), vgb[3], vgb[1], vgb[2],
-        dw1.reshape(-1), vgb[4:8].reshape(-1), dw2.reshape(-1), vgb[0], jnp.zeros((total_len - starts[-1],), F32)])
-    summed = lax.psum(local_grad.astype(BF16), "dp")
-    grad_shard = lax.psum_scatter(summed, "opt", scatter_dimension=0, tiled=True).astype(F32)
-    start = lax.axis_index("opt") * shard_len
-    new_params, new_first, new_second = adam_update(params, moment1, moment2, grad_shard, rates, start)
-    return (y.transpose(2, 0, 1, 3), dx.transpose(2, 0, 1, 3), grad_shard, new_params, new_first, new_second)
-
 
 def solution(mesh):
+    def local(images, cotangent, counts, rel_index, params, moment1, moment2, rates):
+        pn = Plan(mesh, params.shape[0])
+        xt = images.transpose(1, 2, 0, 3)
+        ct = cotangent.transpose(1, 2, 0, 3)
+        rel = rel_lanes(rel_index)
+        flat = call_g(pn, params)
+        wqkv, wp, w1, w2, vec, hw, ob, qkv, p = call_a(pn, xt, flat, rel)
+        y, dx1, gb = call_b(pn, xt, ct, ob, wp, w1, w2, vec, counts)
+        dx, gm, gs = call_c(pn, xt, dx1, hw, qkv, p, wqkv, wp, vec, rel)
+        grad, new_params, new_first, new_second = call_d(pn, gb, gm, gs, rates, params, moment1, moment2)
+        return (y.transpose(2, 0, 1, 3), dx.transpose(2, 0, 1, 3), grad, new_params, new_first, new_second)
+
     split = P(("dp", "opt"), None, None, None)
     return jax.shard_map(
         local, mesh=mesh,

time: 705 us -> 298 us (0.42)
  waiting for transfers between devices: 396 us -> 0 us
  Pallas kernels: 149 us -> 283 us
  local copies, waits for them, and re-layouts: 107 us -> 13.4 us
  other arithmetic: 30.2 us -> 0 us
  between operations: 15.3 us -> 1.33 us
    unnamed x4 -> x0, waiting for transfers between devices: 220 us -> none
    pallas_call x3 -> x5, Pallas kernels: 149 us -> 283 us  [the longest x1 85.9 us: call_d(): pl.pallas_call(functools.partial(kernel_d, pn), out_shape=[shard] * 4, in...]
    all_gather x1 -> x0, waiting for transfers between devices: 117 us -> none  [local(): working = lax.all_gather(params.astype(BF16), 'opt', axis=0, tiled=True)]
    concatenate x1 -> x0, local copies, waits for them, and re-layouts: 93.4 us -> none  [local(): jnp.concatenate([vga[0], vga[1], dwq.reshape(-1), vga[2], vga[3], grad_ta...]
    psum x1 -> x0, waiting for transfers between devices: 58.4 us -> none  [local(): summed = lax.psum(local_grad.astype(BF16), 'dp')]
    sub x1 -> x0, other arithmetic: 21.1 us -> none  [adam_update(): weights - rate * (first_hat / (jnp.sqrt(second_hat) + 1e-08) + decay * we...]
  transfers between devices with their start and end apart: 3 -> 0, of which waited for: 3 -> 0; matrix products, arithmetic and copies ran while one was open for 0% -> 0% of each run, Pallas kernels for 0% -> 0%
where the time goes in v2:
time: 298 us
  Pallas kernels  283 us (95%)
  local copies, waits for them, and re-layouts  13.4 us (4%)
    pallas_call x1, Pallas kernels, call_d(): pl.pallas_call(functools.partial(kernel_d, pn), out_shape=[shard] * 4, in...  85.9 us
    pallas_call x1, Pallas kernels, call_b(): pl.pallas_call(functools.partial(kernel_b, pn), out_shape=outs, in_specs=...  57.6 us
    pallas_call x1, Pallas kernels, call_c(): pl.pallas_call(functools.partial(kernel_c, pn), out_shape=outs, in_specs=...  50.5 us
    pallas_call x1, Pallas kernels, call_a(): pl.pallas_call(functools.partial(kernel_a, pn), out_shape=outs, in_specs=...  45 us
    pallas_call x1, Pallas kernels, call_g(): pl.pallas_call(functools.partial(kernel_g, pn), out_shape=jax.ShapeDtypeS...  44.3 us
    unnamed x11, local copies, waits for them, and re-layouts  12.7 us

profile of v2, /device:TPU:0, one launch (start us, length us, event | category | flops | bytes accessed | tf_op | source)
XLA Modules:
  0.0 298.0 jit_solution(4241451594644855324)
XLA Ops:
  1.3 0.8 copy.15
  2.1 0.7 reshape.69.rel_ref
  2.8 44.3 %gather.1.flat_hbm = bf16[4,2,4,97,8,128]{5,4,3,2,1,0:T(8,128)(2,1)} custom-call(f32[771,8,128]{2,1,0:T(8,128)} %bitcast.15), custom_call_target="tpu_custom_call" | custom-call | tf_op jit(solution)/shard_map/gather/pallas_call | solution.py:952
  47.1 45.0 %attend.1 = (bf16[512,1536]{1,0:T(8,128)(2,1)}, bf16[512,512]{1,0:T(8,128)(2,1)}, bf16[512,2048]{1,0:T(8,128)(2,1)}, bf16[2048,512]{1,0:T(8,128)(2,1)}, f32[16,5...) custom-call(bf16[14,14,8,512]{3,2,1,0:T(8,128)(2,1)} %bitcast.12, ...), custom_call_target="tpu_custom_call" | custom-call | tf_op jit(solution)/shard_map/attend/pallas_call | solution.py:282
  92.2 57.6 %mlp.1 = (bf16[14,14,8,512]{3,2,1,0:T(8,128)(2,1)}, f32[1568,512]{1,0:T(8,128)}, bf16[2,4,291,8,128]{4,3,2,1,0:T(8,128)(2,1)}) custom-call(bf16[14,14,8,512]{3,2,1,0:T(8,128)(2,1)} %bitcast.13, bf16[14,14,8,512]{3,2,1,0:T(8,128)(2,1)} %bitcast.23, bf16[1568,512]{1,0:T(8,128)(2,1)} %get-tuple-element.37.ob_hbm, bf16[512,512]{1,0:T(8,128)(2,1)} %get-tuple-element.38.wp, ...), custom_call_target="tpu_custom_call" | custom-call | tf_op jit(solution)/shard_map/mlp/pallas_call | solution.py:451
  149.8 50.5 %attend_back.1 = (f32[14,14,8,512]{3,2,1,0:T(8,128)}, bf16[2,4,96,8,128]{4,3,2,1,0:T(8,128)(2,1)}, bf16[2,4,1,8,128]{4,3,2,1,0:T(8,128)(2,1)}) custom-call(bf16[14,14,8,512]{3,2,1,0:T(8,128)(2,1)} %bitcast.14, f32[1568,512]{1,0:T(8,128)} %get-tuple-element.43.dx1_hbm, bf16[1568,512]{1,0:T(8,128)(2,1)} %get-tuple-element.44.hw_hbm, ...), custom_call_target="tpu_custom_call" | custom-call | tf_op jit(solution)/shard_map/attend_back/pallas_call | solution.py:597
  200.2 85.9 %reduce.3 = (f32[771,8,128]{2,1,0:T(8,128)}, f32[771,8,128]{2,1,0:T(8,128)}, f32[771,8,128]{2,1,0:T(8,128)}, f32[771,8,128]{2,1,0:T(8,128)}) custom-call(bf16[2,4,291,8,128]{4,3,2,1,0:T(8,128)(2,1)} %get-tuple-element.49.gb, bf16[2,4,96,8,128]{4,3,2,1,0:T(8,128)(2,1)} %get-tuple-element.50.gm, bf16[2,4,1,8,128]{4,3,2,1,0:T(8,128)(2,1)} %get-tuple-element.51.gs, ...), custom_call_target="tpu_custom_call" | custom-call | tf_op jit(solution)/shard_map/reduce/pallas_call | solution.py:893
  286.2 0.0 copy-start.2
  286.2 3.9 %copy.21 = f32[789504]{0:T(1024)} copy(f32[789504]{0:T(1024)} %bitcast.20) | data formatting | bytes 6316032
  290.1 0.0 copy-done.2
  290.1 0.0 copy-start.1
  290.1 1.9 copy.22
  292.0 1.2 copy-done.1
  293.1 0.0 copy-start
  293.1 1.9 copy.23
  295.0 1.2 copy-done
  296.2 1.9 copy.24
  (1 shorter events, 0.0 us)
Async XLA Ops:
  286.2 3.9 %copy-start.2 = (f32[771,8,128]{2,1,0:T(8,128)S(1)}, f32[771,8,128]{2,1,0:T(8,128)}, u32[]{:S(2)}) copy-start(f32[771,8,128]{2,1,0:T(8,128)} %get-tuple-element.53) | copy-start | bytes 9474052
  290.1 3.0 %copy-start.1 = (f32[771,8,128]{2,1,0:T(8,128)S(1)}, f32[771,8,128]{2,1,0:T(8,128)}, u32[]{:S(2)}) copy-start(f32[771,8,128]{2,1,0:T(8,128)} %get-tuple-element.54) | copy-start | bytes 9474052
  293.1 3.0 %copy-start = (f32[771,8,128]{2,1,0:T(8,128)S(1)}, f32[771,8,128]{2,1,0:T(8,128)}, u32[]{:S(2)}) copy-start(f32[771,8,128]{2,1,0:T(8,128)} %get-tuple-element.55) | copy-start | bytes 9474052

commit v3 on v2

v3 whole, which is shorter than its diff:
```python
import functools
import jax
import jax.numpy as jnp
from jax import lax
from jax.experimental import pallas as pl
from jax.experimental.pallas import tpu as pltpu

D = 512
HEADS = 16
HEAD_DIM = 32
HID = 2048
SIDE = 14
WIN = 7
SHIFT = 3
TAB = 169
F32 = jnp.float32
BF16 = jnp.bfloat16

IMGS = 8
SPAN = WIN * WIN
WROWS = SPAN * IMGS
ROWS = 4 * WROWS
RS = ROWS + 64
BLK = 224
NBLK = ROWS // BLK
WB = 4 * IMGS
SCALE = HEAD_DIM ** -0.5

R_G1, R_B1, R_QKV, R_BQ, R_BV, R_TAB = 0, 4, 8, 6152, 6156, 6160
R_PROJ, R_BP, R_G2, R_B2, R_W1, R_C1, R_W2, R_C2, R_END = 6181, 8229, 8233, 8237, 8241, 16433, 16449, 24641, 24645
LANE = 16
BROW = 6176


def segments(w):
    if w == 0:
        return [(SHIFT, WIN, 0)]
    return [(WIN + SHIFT, WIN - SHIFT, 0), (0, SHIFT, WIN - SHIFT)]


def window_copies(hbm, vmem, sem, inward):
    out = []
    n = 0
    for wy in range(2):
        for wx in range(2):
            for ys, yl, yo in segments(wy):
                for xs, xl, xo in segments(wx):
                    a = hbm.at[pl.ds(ys, yl), pl.ds(xs, xl)]
                    b = vmem.at[pl.ds((2 * wy + wx) * WIN + yo, yl), pl.ds(xo, xl)]
                    out.append(pltpu.make_async_copy(a, b, sem.at[n]) if inward else pltpu.make_async_copy(b, a, sem.at[n]))
                    n += 1
    return out


NSEG = 9


def dot(a, b):
    return lax.dot_general(a, b, (((1,), (0,)), ((), ())), preferred_element_type=F32)


def dot_nt(a, b):
    return lax.dot_general(a, b, (((1,), (1,)), ((), ())), preferred_element_type=F32)


def dot_tn(a, b):
    return lax.dot_general(a, b, (((0,), (0,)), ((), ())), preferred_element_type=F32)


def norm_stats(x):
    mean = jnp.mean(x, -1, keepdims=True)
    dev = x - mean
    var = jnp.mean(dev * dev, -1, keepdims=True)
    r = lax.rsqrt(var + 1e-05)
    return dev * r, r


def pieces_to_rows(pn, wb, fs, shard, count, base):
    def body(p, _):
        row = pl.multiple_of((shard * pn.units - base + p * pn.pc) * 8, 8)
        fs[pl.ds(row, pn.pc * 8), :] = wb[shard, p & 1, lax.shift_right_arithmetic(p, 1)].astype(F32).reshape(pn.pc * 8, 128)
        return 0
    lax.fori_loop(0, count, body, 0)


def vec_from(fs, row, width, shift):
    parts = []
    lane = lax.broadcasted_iota(jnp.int32, (1, 128), 1)
    for c in range(width // 128):
        a = fs[pl.ds(row + c, 1), :]
        if shift:
            b = fs[pl.ds(row + c + 1, 1), :]
            a = jnp.where(lane < 128 - LANE, pltpu.roll(a, 128 - LANE, 1), pltpu.roll(b, 128 - LANE, 1))
        parts.append(a)
    return jnp.concatenate(parts, 1)


def take_matrix(fs, row, dst, nrows, ncb, shift, step=128):
    lane = lax.broadcasted_iota(jnp.int32, (step, 128), 1)

    def body(t, _):
        base = row + t * (step * ncb)
        r0 = pl.multiple_of(t * step, step)
        for c in range(ncb):
            a = fs[pl.ds(base + c, step, stride=ncb), :]
            if shift:
                b = fs[pl.ds(base + c + 1, step, stride=ncb), :]
                a = jnp.where(lane < 128 - LANE, pltpu.roll(a, 128 - LANE, 1), pltpu.roll(b, 128 - LANE, 1))
            dst[pl.ds(r0, step), c * 128:(c + 1) * 128] = a.astype(BF16)
        return 0

    lax.fori_loop(0, nrows // step, body, 0)


def transpose_rows(src, dst):
    full = ROWS // 128

    def body(t, _):
        r0 = pl.multiple_of(t * 128, 128)
        dst[:, pl.ds(r0, 128)] = src[pl.ds(r0, 128), :].T
        return 0
    lax.fori_loop(0, full, body, 0)
    if ROWS % 128:
        dst[:, full * 128:ROWS] = src[full * 128:ROWS, :].T


def lane_head():
    return lax.broadcasted_iota(jnp.int32, (64, 128), 1) // HEAD_DIM


def block_diag(v, heads):
    zero = jnp.zeros_like(v)
    return jnp.concatenate([jnp.where(heads == h, v, zero) for h in range(4)], 0)


def diag_sum(r, heads):
    out = r[0:64]
    for h in range(1, 4):
        out = jnp.where(heads == h, r[64 * h:64 * h + 64], out)
    return out


def take_rows(fs, start):
    v = fs[pl.ds(start, 56, stride=IMGS), :]
    v = jnp.where(lax.broadcasted_iota(jnp.int32, (56, 128), 0) < SPAN, v, 0.0)
    return jnp.concatenate([v, jnp.zeros((8, 128), F32)], 0)


def put_rows(fs, start, v):
    fs[pl.ds(start, 48, stride=IMGS), :] = v[0:48]
    fs[pl.ds(start + 48 * IMGS, 1), :] = v[48:49]


def build_bias(tab3, rel_ref, big, bias):
    rel = rel_ref[...]
    row = lax.shift_right_arithmetic(rel, 3)
    low = rel & 7
    oh = (lax.broadcasted_iota(jnp.int32, (32, 4096), 0) == row).astype(F32).astype(BF16)
    tab = jnp.concatenate([tab3, jnp.zeros((8, 128), F32)], 0).astype(BF16)
    r = dot_tn(tab, oh)
    acc = jnp.zeros((16, 4096), F32)
    for j in range(8):
        acc = acc + jnp.where(low == j, r[16 * j:16 * j + 16], 0.0)
    for kk in range(32):
        big[kk * 16:kk * 16 + 16, :] = acc[:, kk * 128:kk * 128 + 128]
    k = lax.broadcasted_iota(jnp.int32, (64, 256), 0)
    q = lax.broadcasted_iota(jnp.int32, (64, 256), 1) & 63
    ki = lax.shift_right_arithmetic(k * 37, 8)
    kj = k - ki * 7
    qi = lax.shift_right_arithmetic(q * 37, 8)
    qj = q - qi * 7
    cut = WIN - SHIFT
    same_y = (ki < cut) == (qi < cut)
    same_x = (kj < cut) == (qj < cut)
    lane = lax.broadcasted_iota(jnp.int32, (32, 128), 1)
    for g in range(4):
        for pair in range(2):
            h = 4 * g + 2 * pair
            a = big[pl.ds(h, 32, stride=16), :]
            b = big[pl.ds(h + 1, 32, stride=16), :]
            even = jnp.where(lane < 64, a, pltpu.roll(b, 64, 1))
            odd = jnp.where(lane < 64, pltpu.roll(a, 64, 1), b)
            big[pl.ds(1024 + g * 256 + pair * 128, 32, stride=2), :] = even
            big[pl.ds(1024 + g * 256 + pair * 128 + 1, 32, stride=2), :] = odd
    for g in range(4):
        pos = jnp.concatenate([big[1024 + g * 256:1024 + g * 256 + 64, :], big[1024 + g * 256 + 128:1024 + g * 256 + 192, :]], 1)
        for w in range(4):
            keep = None
            if w == 1:
                keep = same_x
            elif w == 2:
                keep = same_y
            elif w == 3:
                keep = same_y & same_x
            val = pos if keep is None else pos + jnp.where(keep, 0.0, -100.0)
            bias[w * 4 + g] = jnp.where(k < SPAN, val, -1e30)


def kernel_a(pn, x_hbm, flat_hbm, rel_ref,
             wqkv_o, wp_o, w1_o, w2_o, vec_o, hw_o, ob_o, qkv_o, p_o,
             x_v, flat_v, fs, os_, bias, wqkv, wp, w1, w2, vec, hw, hwt, ob, qkvb, pb, xsem, fsem, osem, wsem):
    cps = window_copies(x_hbm, x_v, xsem, True)
    for c in cps:
        c.start()
    fcp = pltpu.make_async_copy(flat_hbm, flat_v, fsem)
    fcp.start()
    fcp.wait()
    for k in range(pn.ka):
        pieces_to_rows(pn, flat_v, fs, k, pn.ndp, 0)
    pieces_to_rows(pn, flat_v, fs, pn.ka, 1, 0)
    take_matrix(fs, R_QKV, wqkv, D, 12, False)
    vec[0:1, :] = vec_from(fs, R_G1, D, False)
    vec[1:2, :] = vec_from(fs, R_B1, D, False)
    vec[2:3, :] = vec_from(fs, R_BQ, D, False)
    vec[3:4, :] = vec_from(fs, R_BV, D, False)
    build_bias(fs[R_TAB:R_TAB + 24, :], rel_ref, os_, bias)
    for c in cps:
        c.wait()
    gain = vec[0:1, :]
    shift = vec[1:2, :]
    bq = vec[2:3, :]
    bv = vec[3:4, :]

    def rows(t, _):
        r0 = pl.multiple_of(t * BLK, BLK)
        x = x_v[pl.ds(4 * t, 4)].reshape(BLK, D).astype(F32)
        xhat, _r = norm_stats(x)
        h = (xhat * gain + shift).astype(BF16)
        hw[pl.ds(r0, BLK), :] = h
        for c in range(12):
            y = dot(h, wqkv[:, c * 128:(c + 1) * 128])
            if c < 4:
                y = (y + bq[:, c * 128:(c + 1) * 128]) * SCALE
            if c >= 8:
                y = y + bv[:, (c - 8) * 128:(c - 7) * 128]
            fs[pl.ds(c * RS + r0, BLK), :] = y
        return 0
    lax.fori_loop(0, NBLK, rows, 0)

    heads = lane_head()

    def attend(i, _):
        w = lax.shift_right_arithmetic(i, 3)
        b = i & 7
        base = w * WROWS + b
        for g in range(4):
            q = take_rows(fs, g * RS + base).astype(BF16)
            k = take_rows(fs, (4 + g) * RS + base).astype(BF16)
            v = take_rows(fs, (8 + g) * RS + base).astype(BF16)
            qkvb[i, g] = q
            qkvb[i, 4 + g] = k
            qkvb[i, 8 + g] = v
            s = dot_nt(k, block_diag(q, heads)) + bias[w * 4 + g]
            m = jnp.max(s, 0, keepdims=True)
            e = jnp.exp(s - m)
            p = (e * (1.0 / jnp.sum(e, 0, keepdims=True))).astype(BF16)
            pb[i, g] = p
            o = diag_sum(dot_tn(p, v), heads)
            put_rows(os_, g * RS + base, o)
        return 0
    lax.fori_loop(0, WB, attend, 0)

    def outs(t, _):
        r0 = pl.multiple_of(t * BLK, BLK)
        for g in range(4):
            ob[pl.ds(r0, BLK), g * 128:(g + 1) * 128] = os_[pl.ds(g * RS + r0, BLK), :].astype(BF16)
        return 0
    lax.fori_loop(0, NBLK, outs, 0)
    transpose_rows(hw, hwt)
    cos = [pltpu.make_async_copy(a, b, osem.at[n]) for n, (a, b) in enumerate([(hwt, hw_o), (ob, ob_o), (qkvb, qkv_o), (pb, p_o)])]
    for c in cos:
        c.start()
    for k in range(pn.ka, pn.ns):
        pieces_to_rows(pn, flat_v, fs, k, pn.ndp, pn.base)
    first = pn.base * 8
    take_matrix(fs, R_PROJ - first, wp, D, 4, True)
    take_matrix(fs, R_W1 - first, w1, D, 16, True)
    take_matrix(fs, R_W2 - first, w2, HID, 4, True)
    for n, r in enumerate((R_BP, R_G2, R_B2, R_C2)):
        vec[4 + n:5 + n, :] = vec_from(fs, r - first, D, True)
    for n in range(4):
        vec[8 + n:9 + n, :] = vec_from(fs, R_C1 - first + 4 * n, D, True)
    wos = [pltpu.make_async_copy(a, b, wsem.at[n]) for n, (a, b) in enumerate([(wqkv, wqkv_o), (wp, wp_o), (w1, w1_o), (w2, w2_o), (vec, vec_o)])]
    for c in wos:
        c.start()
    for c in cos + wos:
        c.wait()


def call_a(pn, x, flat, rel):
    any_ = pl.BlockSpec(memory_space=pl.ANY)
    sds = jax.ShapeDtypeStruct
    outs = [sds((D, 3 * D), BF16), sds((D, D), BF16), sds((D, HID), BF16), sds((HID, D), BF16), sds((16, D), F32),
            sds((D, ROWS), BF16), sds((ROWS, D), BF16), sds((WB, 12, 64, 128), BF16), sds((WB, 4, 64, 256), BF16)]
    return pl.pallas_call(
        functools.partial(kernel_a, pn),
        out_shape=outs,
        in_specs=[any_, any_, pl.BlockSpec(memory_space=pltpu.VMEM)],
        out_specs=[any_] * len(outs),
        scratch_shapes=[
            pltpu.VMEM((28, 7, 8, D), BF16), pltpu.VMEM(flat.shape, BF16), pltpu.VMEM((12 * RS, 128), F32), pltpu.VMEM((4 * RS, 128), F32),
            pltpu.VMEM((16, 64, 256), F32), pltpu.VMEM((D, 3 * D), BF16), pltpu.VMEM((D, D), BF16), pltpu.VMEM((D, HID), BF16), pltpu.VMEM((HID, D), BF16),
            pltpu.VMEM((16, D), F32), pltpu.VMEM((ROWS, D), BF16), pltpu.VMEM((D, ROWS), BF16), pltpu.VMEM((ROWS, D), BF16), pltpu.VMEM((WB, 12, 64, 128), BF16), pltpu.VMEM((WB, 4, 64, 256), BF16),
            pltpu.SemaphoreType.DMA((NSEG,)), pltpu.SemaphoreType.DMA, pltpu.SemaphoreType.DMA((4,)), pltpu.SemaphoreType.DMA((5,)),
        ],
        compiler_params=pltpu.CompilerParams(vmem_limit_bytes=64000000),
        name="attend",
    )(x, flat, rel)


def rel_lanes(rel_index):
    t = jnp.full((64, 64), -1, jnp.int32).at[:SPAN, :SPAN].set(rel_index.T)
    return t.reshape(1, 4096)


CH = 512
INV_SQRT2 = 0.7071067811865476
INV_SQRT2PI = 0.3989422804014327


def gelu_parts(u):
    e = jnp.exp(u * u * -0.5)
    t = 1.0 / (1.0 + jnp.abs(u) * (0.3275911 * INV_SQRT2))
    half = t * (0.127414796 + t * (-0.142248368 + t * (0.7107068705 + t * (-0.7265760135 + t * 0.5307027145)))) * e
    cdf = jnp.where(u >= 0, 1.0 - half, half)
    return cdf, e * INV_SQRT2PI


def put_block(fs, start, stride, v):
    n = v.shape[0]
    lane = lax.broadcasted_iota(jnp.int32, (n, 128), 1)
    v = pltpu.roll(v, LANE, 1)
    here = pl.ds(start, n, stride=stride) if n > 1 else pl.ds(start, 1)
    fs[here, :] = jnp.where(lane >= LANE, v, fs[here, :])
    here = pl.ds(start + 1, n, stride=stride) if n > 1 else pl.ds(start + 1, 1)
    fs[here, :] = jnp.where(lane < LANE, v, fs[here, :])


def put_vec(fs, row, v):
    for c in range(v.shape[1] // 128):
        put_block(fs, row + c, 1, v[:, c * 128:(c + 1) * 128])


def acc_rows(ref, i, v):
    ref[8 * i:8 * i + 8, 0:v.shape[1]] += jnp.sum(v.reshape(v.shape[0] // 8, 8, v.shape[1]), 0)


def table_grad(rel_ref, big, dtab):
    lane = lax.broadcasted_iota(jnp.int32, (32, 128), 1)
    for g in range(4):
        for pair in range(2):
            at = 1024 + g * 256 + pair * 128
            big[at:at + 64, :] = dtab[g, :, pair * 128:pair * 128 + 128]
    for g in range(4):
        for pair in range(2):
            at = 1024 + g * 256 + pair * 128
            even = big[pl.ds(at, 32, stride=2), :]
            odd = big[pl.ds(at + 1, 32, stride=2), :]
            h = 4 * g + 2 * pair
            big[pl.ds(h, 32, stride=16), :] = jnp.where(lane < 64, even, pltpu.roll(odd, 64, 1))
            big[pl.ds(h + 1, 32, stride=16), :] = jnp.where(lane < 64, pltpu.roll(even, 64, 1), odd)
    rel = rel_ref[...]
    row = lax.shift_right_arithmetic(rel, 3)
    low = rel & 7
    oh = (lax.broadcasted_iota(jnp.int32, (32, 4096), 0) == row).astype(F32).astype(BF16)
    grad = jnp.concatenate([big[kk * 16:kk * 16 + 16, :] for kk in range(32)], 1)
    out = jnp.zeros((32, 128), F32)
    high = grad.astype(BF16).astype(F32)
    for part in (high, grad - high):
        m = jnp.concatenate([jnp.where(low == j, part, 0.0) for j in range(8)], 0).astype(BF16)
        out = out + dot_nt(oh, m)
    return out


MESH = pl.DeviceIdType.MESH
NMAT = 768


class Plan:
    def __init__(self, mesh, shard_len):
        self.ndp = mesh.shape["dp"]
        self.ns = mesh.shape["opt"]
        self.rest = self.ndp // 2
        self.units = shard_len // 1024
        self.pc = -(-self.units // self.ndp)
        self.ka = (BROW // 8) // self.units
        self.base = self.ka * self.units
        self.bunits = (self.ns - self.ka - 1) * self.units + self.ndp * self.pc
        self.kh = -(-(R_W2 // 8 + 1) // self.units)
        self.mrow = D // self.ndp
        self.gunits = max(BROW // 8 + 1, self.ndp * self.pc)


def place():
    me = lax.axis_index("dp")
    return lax.shift_right_arithmetic(me, 1), me & 1, lax.axis_index("opt")


def peer(r, c):
    return {"dp": 2 * r + c}


def enter(pn, all_dp=False):
    r, c, z = place()
    bar = pltpu.get_barrier_semaphore()
    pl.semaphore_signal(bar, inc=1, device_id=peer(r, 1 - c), device_id_type=MESH)
    for j in range(1, pn.rest):
        for to in ((c, 1 - c) if all_dp else (c,)):
            pl.semaphore_signal(bar, inc=1, device_id=peer(lax.rem(r + j, pn.rest), to), device_id_type=MESH)
    for j in range(1, pn.ns):
        pl.semaphore_signal(bar, inc=1, device_id={"opt": lax.rem(z + j, pn.ns)}, device_id_type=MESH)
    pl.semaphore_wait(bar, (pn.ndp - 1 if all_dp else pn.rest) + pn.ns - 1)


def remote(src, dst, sems, n, where):
    return pltpu.make_async_remote_copy(src_ref=src, dst_ref=dst, send_sem=sems.at[0, n], recv_sem=sems.at[1, n], device_id=where, device_id_type=MESH)


class Chunk:
    def __init__(self, pn, k0, k1, scatter, m, src, r1, r2, r3, sems, ag):
        self.pn, self.k0, self.k1, self.scatter, self.m = pn, k0, k1, scatter, m
        self.n = m * (k1 - k0) if scatter else m
        self.src, self.r1, self.r2, self.r3, self.ag, self.sems = src, r1, r2, r3, ag, sems
        self.k2 = 1
        self.k3 = self.k2 + pn.rest - 1
        self.k4 = self.k3 + pn.ns - 1
        self.k5 = self.k4 + pn.rest - 1

    @staticmethod
    def scratch(pn, m, count, shared):
        n = m * count
        return [pltpu.VMEM((2, pn.rest, n, 8, 128), BF16), pltpu.VMEM((pn.rest, n, 8, 128), BF16), pltpu.VMEM((pn.rest - 1, n, 8, 128), BF16),
                pltpu.VMEM((pn.ns - 1, m, 8, 128), BF16),
                pltpu.SemaphoreType.DMA((2, 2 * pn.rest + pn.ns - 1))] + [pltpu.VMEM((2, pn.rest, m, 8, 128), BF16)] * (not shared)

    def here(self, z):
        return (z >= self.k0) & (z < self.k1)

    def c1(self):
        r, c, z = place()
        return remote(self.src.at[1 - c], self.r1, self.sems, 0, peer(r, 1 - c))

    def start1(self):
        self.c1().start()

    def c2(self, j):
        r, c, z = place()
        to = lax.rem(r + j, self.pn.rest)
        return remote(self.src.at[c, to], self.r2.at[j - 1], self.sems, self.k2 + j - 1, peer(to, c))

    def start2(self):
        r, c, z = place()
        self.c1().wait()
        step = self.m
        for j in list(range(1, self.pn.rest)) + [0]:
            to = lax.rem(r + j, self.pn.rest)

            def add(t, _):
                u = pl.ds(t * step, step)
                self.src[c, to, u] = (self.src[c, to, u].astype(F32) + self.r1[to, u].astype(F32)).astype(BF16)
                return 0
            lax.fori_loop(0, self.n // step, add, 0)
            if j:
                self.c2(j).start()

    def c3(self, j):
        r, c, z = place()
        to = lax.rem(z + j, self.pn.ns)
        src = self.src.at[c, r]
        if self.scatter:
            src = src.at[pl.ds(lax.clamp(0, to - self.k0, self.k1 - self.k0 - 1) * self.m, self.m)]
        return to, remote(src, self.r3.at[j - 1], self.sems, self.k3 + j - 1, {"opt": to})

    def start3(self):
        r, c, z = place()
        for j in range(1, self.pn.rest):
            self.c2(j).wait()
        step = self.m

        def add(t, _):
            u = pl.ds(t * step, step)
            v = self.src[c, r, u].astype(F32)
            for j in range(1, self.pn.rest):
                v = v + self.r2[j - 1, u].astype(F32)
            self.src[c, r, u] = v.astype(BF16)
            return 0
        lax.fori_loop(0, self.n // step, add, 0)
        for j in range(1, self.pn.ns):
            to, cp = self.c3(j)

            @pl.when(self.here(to))
            def _():
                cp.start()

    def c4(self, j):
        r, c, z = place()
        return remote(self.ag.at[c, r], self.ag.at[c, r], self.sems, self.k4 + j - 1, peer(lax.rem(r + j, self.pn.rest), c))

    def start4(self):
        r, c, z = place()
        for j in range(1, self.pn.ns):
            to, cp = self.c3(j)

            @pl.when(self.here(to))
            def _():
                cp.wait_send()

        @pl.when(self.here(z))
        def _():
            for j in range(1, self.pn.ns):
                self.c3(j)[1].wait_recv()
            at = lax.clamp(0, z - self.k0, self.k1 - self.k0 - 1) * self.m if self.scatter else 0
            v = self.src[c, r, pl.ds(at, self.m)].astype(F32)
            for j in range(1, self.pn.ns):
                v = v + self.r3[j - 1].astype(F32)
            self.ag[c, r] = v.astype(BF16)
            for j in range(1, self.pn.rest):
                self.c4(j).start()

    def c5(self):
        r, c, z = place()
        return remote(self.ag.at[c], self.ag.at[c], self.sems, self.k5, peer(r, 1 - c))

    def start5(self):
        r, c, z = place()

        @pl.when(self.here(z))
        def _():
            for j in range(1, self.pn.rest):
                self.c4(j).wait()
            self.c5().start()

    def finish(self):
        r, c, z = place()

        @pl.when(self.here(z))
        def _():
            self.c5().wait()


SMALL = (0, 769, 770, 771, 772)


class Small:
    def __init__(self, pn, own, r1, mid, r2, sems):
        self.pn, self.own, self.r1, self.mid, self.r2, self.sems = pn, own, r1, mid, r2, sems

    @staticmethod
    def scratch(pn):
        u = len(SMALL)
        return [pltpu.VMEM((u, 8, 128), BF16), pltpu.VMEM((pn.ndp, u, 8, 128), BF16), pltpu.VMEM((u, 8, 128), BF16), pltpu.VMEM((pn.ns, u, 8, 128), BF16),
                pltpu.SemaphoreType.DMA((2, pn.ndp + pn.ns - 2))]

    def c1(self, j):
        me = lax.axis_index("dp")
        return remote(self.own, self.r1.at[me], self.sems, j - 1, {"dp": lax.rem(me + j, self.pn.ndp)})

    def w1(self, j):
        me = lax.axis_index("dp")
        return remote(self.own, self.r1.at[lax.rem(me - j + self.pn.ndp, self.pn.ndp)], self.sems, j - 1, {"dp": lax.rem(me + j, self.pn.ndp)})

    def start1(self):
        me = lax.axis_index("dp")
        for j in range(1, self.pn.ndp):
            self.c1(j).start()
        self.r1[me] = self.own[...]

    def c2(self, j):
        z = lax.axis_index("opt")
        to = lax.rem(z + j, self.pn.ns)
        return to, remote(self.mid, self.r2.at[z], self.sems, self.pn.ndp - 2 + j, {"opt": to})

    def w2(self, j):
        z = lax.axis_index("opt")
        return remote(self.mid, self.r2.at[lax.rem(z - j + self.pn.ns, self.pn.ns)], self.sems, self.pn.ndp - 2 + j, {"opt": lax.rem(z + j, self.pn.ns)})

    def start2(self):
        z = lax.axis_index("opt")
        for j in range(1, self.pn.ndp):
            self.c1(j).wait_send()
            self.w1(j).wait_recv()
        v = self.r1[0].astype(F32)
        for n in range(1, self.pn.ndp):
            v = v + self.r1[n].astype(F32)
        self.mid[...] = v.astype(BF16)
        for j in range(1, self.pn.ns):
            to, cp = self.c2(j)

            @pl.when(to <= self.pn.ka)
            def _():
                cp.start()
        self.r2[z] = v.astype(BF16)

    def finish(self):
        z = lax.axis_index("opt")
        for j in range(1, self.pn.ns):
            to, cp = self.c2(j)

            @pl.when(to <= self.pn.ka)
            def _():
                cp.wait_send()

            @pl.when(z <= self.pn.ka)
            def _():
                self.w2(j).wait_recv()

    def total(self, n):
        v = self.r2[0, n].astype(F32)
        for k in range(1, self.pn.ns):
            v = v + self.r2[k, n].astype(F32)
        return v.astype(BF16).astype(F32)


BM = 784
NSEMS = 32


def put_rows_grad(fs, start, v):
    put_rows(fs, start, v)


def kernel_bc(pn, x_hbm, cot_hbm, ob_hbm, wp_hbm, w1_hbm, w2_hbm, hwt_hbm, qkv_hbm, p_hbm, wqkv_hbm, vec, rel_ref, counts,
              y_hbm, dx_hbm, g_hbm, *refs):
    refs = list(refs)
    dx1, wp, acc, dsem = refs[:4]
    refs = refs[4:]
    chunks = []
    for n, (k0, k1, scatter, m) in enumerate(part_list(pn)):
        if n == 1:
            refs.insert(5, chunks[0].ag)
        chunks.append(Chunk(pn, k0, k1, scatter, m, *refs[:6]))
        refs = refs[6:]
    hi, lo = chunks[:2]
    ac = chunks[2:]
    small = Small(pn, *refs)
    count = counts[0]

    def local(n, src, dst):
        return pltpu.make_async_copy(src, dst, dsem.at[n])

    def mlp(x_v, dy_v, ob, a, du, h2, w1, w2, fs, xsem, csem):
        ins = [local(n, s, d) for n, (s, d) in enumerate([(ob_hbm, ob), (wp_hbm, wp), (w1_hbm, w1), (w2_hbm, w2)])]
        cps = window_copies(x_hbm, x_v, xsem, True) + window_copies(cot_hbm, dy_v, csem, True)
        for cp in cps + ins:
            cp.start()
        acc[...] = jnp.zeros_like(acc)
        bp, g2, b2, c2 = (vec[n:n + 1, :] for n in range(4, 8))
        enter(pn, True)
        for cp in cps + ins:
            cp.wait()
        nb = BM // 56

        def rows(t, _):
            r0 = pl.multiple_of(t * BM, BM)
            x = x_v[pl.ds(nb * t, nb)].reshape(BM, D).astype(F32)
            alive = lax.broadcasted_iota(jnp.int32, (nb, 7, 8, D), 2) < count
            dy = jnp.where(alive, dy_v[pl.ds(nb * t, nb)].astype(F32), 0.0)
            dyb = dy.astype(BF16)
            dy_v[pl.ds(nb * t, nb)] = dyb
            dy = dy.reshape(BM, D)
            dyb = dyb.reshape(BM, D)
            x1 = x + dot(ob[pl.ds(r0, BM), :], wp[...]) + bp
            xhat, r = norm_stats(x1)
            h = (xhat * g2 + b2).astype(BF16)
            h2[pl.ds(r0, BM), :] = h
            y = x1 + c2
            dh = jnp.zeros((BM, D), F32)
            for j in range(HID // CH):
                cs = slice(j * CH, (j + 1) * CH)
                u = dot(h, w1[:, cs]) + vec[8 + j:9 + j, :]
                cdf, pdf = gelu_parts(u)
                av = (u * cdf).astype(BF16)
                a[pl.ds(r0, BM), cs] = av
                y = y + dot(av, w2[cs, :])
                da = dot_nt(dyb, w2[cs, :])
                duv = da * (cdf + u * pdf)
                acc_rows(acc, 4 + j, duv)
                dub = duv.astype(BF16)
                du[pl.ds(r0, BM), cs] = dub
                dh = dh + dot_nt(dub, w1[:, cs])
            x_v[pl.ds(nb * t, nb)] = y.reshape(nb, 7, 8, D).astype(BF16)
            acc_rows(acc, 0, dy)
            acc_rows(acc, 1, dh * xhat)
            acc_rows(acc, 2, dh)
            dg = dh * g2
            dt = r * (dg - jnp.mean(dg, -1, keepdims=True) - xhat * jnp.mean(dg * xhat, -1, keepdims=True))
            dxv = dy + dt
            acc_rows(acc, 3, dxv)
            dx1[pl.ds(nb * t, nb)] = dxv.reshape(nb, 7, 8, D)
            return 0
        lax.fori_loop(0, ROWS // BM, rows, 0)
        ycs = window_copies(y_hbm, x_v, xsem, False)
        for cp in ycs:
            cp.start()
        vg = jnp.sum(acc[...].reshape(8, 8, D), 1)
        first = pn.base * 8
        nrow = pn.bunits * 8
        lo_row = (R_PROJ // 8 + 1) * 8 - first
        hi_row = R_END // 8 * 8 - first
        fs[0:lo_row, :] = jnp.zeros((lo_row, 128), F32)
        fs[hi_row:nrow, :] = jnp.zeros((nrow - hi_row, 128), F32)
        dyf = dy_v[...].reshape(ROWS, D)

        def w2rows(t, _):
            r0 = pl.multiple_of(t * 512, 512)
            v = dot_tn(a[:, pl.ds(r0, 512)], dyf)
            for c in range(4):
                put_block(fs, R_W2 - first + r0 * 4 + c, 4, v[:, c * 128:(c + 1) * 128])
            return 0
        lax.fori_loop(0, HID // 512, w2rows, 0)
        put_vec(fs, R_C2 - first, vg[0:1])

        def fill(ch):
            for k in range(ch.k0, ch.k1):
                def piece(p, _):
                    row = pl.multiple_of(((k - pn.ka) * pn.units + p * pn.pc) * 8, 8)
                    ch.src[p & 1, lax.shift_right_arithmetic(p, 1), (k - ch.k0) * pn.pc:(k - ch.k0 + 1) * pn.pc] = fs[pl.ds(row, pn.pc * 8), :].reshape(pn.pc, 8, 128).astype(BF16)
                    return 0
                lax.fori_loop(0, pn.ndp, piece, 0)
        fill(hi)
        hi.start1()
        h2t = a.at[0:D, 0:1664]
        transpose_rows(h2, h2t)

        def w1rows(t, _):
            r0 = pl.multiple_of(t * 256, 256)
            v = dot(h2t[:, 0:ROWS], du[:, pl.ds(r0, 256)])
            for c in range(2):
                put_block(fs, R_W1 - first + 2 * t + c, 16, v[:, c * 128:(c + 1) * 128])
            return 0
        lax.fori_loop(0, HID // 256, w1rows, 0)
        hi.start2()
        v = dot_tn(ob[...], dx1[...].reshape(ROWS, D).astype(BF16))
        for c in range(4):
            put_block(fs, R_PROJ - first + c, 4, v[:, c * 128:(c + 1) * 128])
        for row, n in ((R_BP, 3), (R_G2, 1), (R_B2, 2)):
            put_vec(fs, row - first, vg[n:n + 1])
        for j in range(4):
            put_vec(fs, R_C1 - first + 4 * j, vg[4 + j:5 + j])
        fill(lo)
        lo.start1()
        for cp in ycs:
            cp.wait()

    big = pltpu.VMEM((28, 7, 8, D), BF16)
    pl.run_scoped(mlp, big, big, pltpu.VMEM((ROWS, D), BF16), pltpu.VMEM((ROWS, HID), BF16), pltpu.VMEM((ROWS, HID), BF16), pltpu.VMEM((ROWS, D), BF16),
                  pltpu.VMEM((D, HID), BF16), pltpu.VMEM((HID, D), BF16), pltpu.VMEM((pn.bunits * 8, 128), F32),
                  pltpu.SemaphoreType.DMA((NSEG,)), pltpu.SemaphoreType.DMA((NSEG,)))

    def attention(x_v, qkvb, pb, hwt, wqkv, fs, os_, dq, dtab, xsem):
        ins = [local(n, s, d) for n, (s, d) in enumerate([(qkv_hbm, qkvb), (p_hbm, pb), (hwt_hbm, hwt), (wqkv_hbm, wqkv)])]
        for cp in ins:
            cp.start()
        cps = window_copies(x_hbm, x_v, xsem, True)
        for cp in cps:
            cp.start()
        acc[...] = jnp.zeros_like(acc)
        dtab[...] = jnp.zeros_like(dtab)

        def rows0(t, _):
            r0 = pl.multiple_of(t * 392, 8)
            ev = dx1[pl.ds(7 * t, 7)].reshape(392, D).astype(BF16)
            v = dot_nt(ev, wp[...])
            for g in range(4):
                os_[pl.ds(g * RS + r0, 392), :] = v[:, g * 128:(g + 1) * 128]
            return 0
        lax.fori_loop(0, 4, rows0, 0)
        ins[0].wait()
        ins[1].wait()
        lo.start2()
        heads = lane_head()

        def one(g, i):
            base = lax.shift_right_arithmetic(i, 3) * WROWS + (i & 7)
            do = take_rows(os_, g * RS + base).astype(BF16)
            q = qkvb[i, g]
            k = qkvb[i, 4 + g]
            v = qkvb[i, 8 + g]
            pbv = pb[i, g]
            p = pbv.astype(F32)
            dobd = block_diag(do, heads)
            dp = dot_nt(v, dobd)
            t = p * dp
            ds = t - p * jnp.sum(t, 0, keepdims=True)
            dsb = ds.astype(BF16)
            put_rows(fs, 2 * RS + base, dot(pbv, dobd))
            put_rows(fs, RS + base, dot(dsb, block_diag(q, heads)))
            put_rows(fs, base, diag_sum(dot_tn(dsb, k), heads) * SCALE)
            return ds

        mid = {0: (hi.start3,), 1: (ac[0].start2, hi.start4), 2: (hi.start5, ac[1].start2, ac[0].start3), 3: (ac[2].start2, ac[1].start3, ac[0].start4)}
        end = {0: (), 1: (lo.start3,), 2: (lo.start4,), 3: (lo.start5,)}
        for g in range(4):
            def attend(t, _):
                @pl.when(t == 4)
                def _():
                    for f in mid[g]:
                        f()
                total = dtab[g]
                for n in range(4):
                    total = total + one(g, 4 * t + n)
                dtab[g] = total
                return 0
            lax.fori_loop(0, WB // 4, attend, 0)
            for f in end[g]:
                f()
            parts = []
            for n in range(3):
                v = fs[n * RS:n * RS + ROWS, :]
                if n != 1:
                    acc[8 * (2 + n // 2):8 * (3 + n // 2), g * 128:(g + 1) * 128] = jnp.sum(v.reshape(ROWS // 8, 8, 128), 0)
                v = v.astype(BF16)
                dq[:, n * D + g * 128:n * D + (g + 1) * 128] = v
                parts.append(v)
            if g == 0:
                ins[2].wait()
                ins[3].wait()
            v = dot(hwt[...], jnp.concatenate(parts, 1))
            mu = pn.mrow // 8
            for n in range(3):
                u = v[:, n * 128:(n + 1) * 128].reshape(D // 8, 8, 128).astype(BF16)
                for p in range(pn.ndp):
                    ac[g].src[p & 1, p >> 1, n * mu:(n + 1) * mu] = u[p * mu:(p + 1) * mu]
            ac[g].start1()
        for cp in cps:
            cp.wait()
        gain = vec[0:1, :]
        tab = table_grad(rel_ref, os_, dtab)
        for n in range(3):
            small.own[2 + n] = tab[8 * n:8 * n + 8].astype(BF16)
        late = {1: (ac[3].start2, ac[2].start3, ac[1].start4, ac[0].start5), 3: (ac[3].start3, ac[2].start4, ac[1].start5), 5: (ac[3].start4, ac[2].start5)}

        def rows1(t, _):
            for k, fns in late.items():
                @pl.when(t == k)
                def _():
                    for f in fns:
                        f()
            r0 = pl.multiple_of(t * BLK, BLK)
            dn = dot_nt(dq[pl.ds(r0, BLK), :], wqkv[...])
            x = x_v[pl.ds(4 * t, 4)].reshape(BLK, D).astype(F32)
            xhat, r = norm_stats(x)
            acc_rows(acc, 0, dn * xhat)
            acc_rows(acc, 1, dn)
            dg = dn * gain
            dt = r * (dg - jnp.mean(dg, -1, keepdims=True) - xhat * jnp.mean(dg * xhat, -1, keepdims=True))
            dx1[pl.ds(4 * t, 4)] += dt.reshape(4, 7, 8, D)
            return 0
        lax.fori_loop(0, NBLK, rows1, 0)
        vg = jnp.sum(acc[...].reshape(8, 8, D), 1)
        flat = [vg[n:n + 1, c * 128:(c + 1) * 128] for n in range(4) for c in range(4)]
        small.own[0] = jnp.concatenate(flat[:8], 0).astype(BF16)
        small.own[1] = jnp.concatenate(flat[8:], 0).astype(BF16)
        small.start1()
        ycs = window_copies(dx_hbm, dx1, xsem, False)
        for cp in ycs:
            cp.start()
        ac[3].start5()
        for ch in chunks:
            ch.finish()
        small.start2()
        r, c, z = place()
        g = os_

        def scattered(ch):
            @pl.when(ch.here(z))
            def _():
                def piece(p, _):
                    g[pl.ds(pl.multiple_of(p * pn.pc * 8, 8), pn.pc * 8), :] = ch.ag[p & 1, lax.shift_right_arithmetic(p, 1)].astype(F32).reshape(pn.pc * 8, 128)
                    return 0
                lax.fori_loop(0, pn.ndp, piece, 0)
        scattered(hi)
        scattered(lo)
        mu = pn.mrow // 8

        @pl.when(z < pn.ka)
        def _():
            def piece(p, _):
                for h in range(4):
                    for n in range(3):
                        v = ac[h].ag[p & 1, lax.shift_right_arithmetic(p, 1), n * mu:(n + 1) * mu].astype(F32).reshape(pn.mrow, 128)
                        g[pl.ds(R_QKV + p * pn.mrow * 12 + n * 4 + h, pn.mrow, stride=12), :] = v
                return 0
            lax.fori_loop(0, pn.ndp, piece, 0)
        small.finish()

        @pl.when(z < pn.ka)
        def _():
            for n, u in enumerate(SMALL):
                g[u * 8:u * 8 + 8, :] = small.total(n)

        @pl.when(z == pn.ka)
        def _():
            for n, u in enumerate(SMALL):
                if u >= pn.base:
                    k = (u - pn.base) * 8
                    g[k:k + 8, :] += small.total(n)
        out = local(0, g.at[pl.ds(pl.multiple_of(lax.select(z < pn.ka, z * (pn.units * 8), 0), 8), pn.units * 8)], g_hbm)
        out.start()
        out.wait()
        for cp in ycs:
            cp.wait()

    pl.run_scoped(attention, big, pltpu.VMEM((WB, 12, 64, 128), BF16), pltpu.VMEM((WB, 4, 64, 256), BF16), pltpu.VMEM((D, ROWS), BF16), pltpu.VMEM((D, 3 * D), BF16),
                  pltpu.VMEM((3 * RS, 128), F32), pltpu.VMEM((max(4 * RS, pn.gunits * 8), 128), F32), pltpu.VMEM((ROWS, 3 * D), BF16), pltpu.VMEM((4, 64, 256), F32), pltpu.SemaphoreType.DMA((NSEG,)))


def part_list(pn):
    mu = 3 * pn.mrow // 8
    return [(pn.kh, pn.ns, True, pn.pc), (pn.ka, pn.kh, True, pn.pc)] + [(0, pn.ka, False, mu)] * 4


def call_bc(pn, x, cot, ob, wp, w1, w2, hwt, qkv, p, wqkv, vec, rel, counts):
    any_ = pl.BlockSpec(memory_space=pl.ANY)
    vm = pl.BlockSpec(memory_space=pltpu.VMEM)
    sds = jax.ShapeDtypeStruct
    outs = [sds((14, 14, 8, D), BF16), sds((14, 14, 8, D), F32), sds((pn.units * 8, 128), F32)]
    scratch = [pltpu.VMEM((28, 7, 8, D), F32), pltpu.VMEM((D, D), BF16), pltpu.VMEM((64, D), F32), pltpu.SemaphoreType.DMA((4,))]
    for n, (k0, k1, scatter, m) in enumerate(part_list(pn)):
        scratch += Chunk.scratch(pn, m, k1 - k0 if scatter else 1, n == 1)
    scratch += Small.scratch(pn)
    return pl.pallas_call(
        functools.partial(kernel_bc, pn),
        out_shape=outs,
        in_specs=[any_] * 10 + [vm, vm, pl.BlockSpec(memory_space=pltpu.SMEM)],
        out_specs=[any_] * 3,
        scratch_shapes=scratch,
        compiler_params=pltpu.CompilerParams(vmem_limit_bytes=67000000, collective_id=1, has_side_effects=True),
        name="back",
    )(x, cot, ob, wp, w1, w2, hwt, qkv, p, wqkv, vec, rel, counts)


STEP = 2
DECAYED = (2, 6, 10, 12)
LENGTHS = [D, D, 3 * D * D, D, D, TAB * HEADS, D * D, D, D, D, D * HID, HID, HID * D, D]
AU = 64


def kernel_adam(rates, first, g, p, m1, m2, g_o, p_o, m_o, v_o):
    shape = (AU, 8, 128)
    u0 = first[0] + pl.program_id(0) * AU
    index = ((u0 + lax.broadcasted_iota(jnp.int32, shape, 0)) * 8 + lax.broadcasted_iota(jnp.int32, shape, 1)) * 128 + lax.broadcasted_iota(jnp.int32, shape, 2)
    rate = jnp.zeros(shape, F32) + rates[0]
    decay = jnp.zeros(shape, F32)
    at = 0
    for n, length in enumerate(LENGTHS):
        at += length
        after = index >= at
        rate = jnp.where(after, rates[n + 1], rate)
        if n in DECAYED or n + 1 in DECAYED:
            decay = jnp.where(after, 0.05 if n + 1 in DECAYED else 0.0, decay)
    grad = g[...]
    w = p[...]
    m = 0.9 * m1[...] + 0.1 * grad
    v = 0.999 * m2[...] + 0.001 * grad * grad
    mh = m / (1.0 - 0.9 ** STEP)
    vh = v / (1.0 - 0.999 ** STEP)
    p_o[...] = w - rate * (mh / (jnp.sqrt(vh) + 1e-08) + decay * w)
    m_o[...] = m
    v_o[...] = v
    g_o[...] = grad


def call_adam(pn, rates, g, params, mom1, mom2):
    view = lambda t: t.reshape(pn.units, 8, 128)
    spec = pl.BlockSpec((AU, 8, 128), lambda i: (i, 0, 0))
    sm = pl.BlockSpec(memory_space=pltpu.SMEM)
    first = (lax.axis_index("opt") * pn.units).astype(jnp.int32).reshape(1)
    out = pl.pallas_call(
        kernel_adam,
        grid=(pl.cdiv(pn.units, AU),),
        out_shape=[jax.ShapeDtypeStruct((pn.units, 8, 128), F32)] * 4,
        in_specs=[sm, sm] + [spec] * 4,
        out_specs=[spec] * 4,
        compiler_params=pltpu.CompilerParams(vmem_limit_bytes=67043328),
        name="adamw",
    )(rates, first, view(g), view(params), view(mom1), view(mom2))
    return [t.reshape(-1) for t in out]


def kernel_g(pn, params, w_o, p_v, wb, sems, isem, osem):
    r, c, z = place()
    cp = pltpu.make_async_copy(params, p_v.at[pl.ds(0, pn.units)], isem)
    cp.start()
    enter(pn)
    cp.wait()

    def cast(p, _):
        wb[z, p & 1, lax.shift_right_arithmetic(p, 1)] = p_v[pl.ds(p * pn.pc, pn.pc)].astype(BF16)
        return 0
    lax.fori_loop(0, pn.ndp, cast, 0)

    def o(j):
        to = lax.rem(z + j, pn.ns)
        return remote(wb.at[z, c, r], wb.at[z, c, r], sems, j - 1, {"opt": to})

    def x(k, j):
        to = lax.rem(r + j, pn.rest)
        src = lax.rem(z - k + pn.ns, pn.ns)
        return remote(wb.at[src, c, r], wb.at[src, c, r], sems, pn.ns - 1 + (k - 1) * (pn.rest - 1) + j - 1, peer(to, c))

    def y(k):
        src = lax.rem(z - k + pn.ns, pn.ns)
        return remote(wb.at[src, c], wb.at[src, c], sems, (pn.ns - 1) * pn.rest + k - 1, peer(r, 1 - c))

    for j in range(1, pn.ns):
        o(j).start()
    for k in range(1, pn.ns):
        o(k).wait()
        for j in range(1, pn.rest):
            x(k, j).start()
    for k in range(1, pn.ns):
        for j in range(1, pn.rest):
            x(k, j).wait()
        y(k).start()
    for k in range(1, pn.ns):
        y(k).wait()
    cp = pltpu.make_async_copy(wb, w_o, osem)
    cp.start()
    cp.wait()


def call_g(pn, params):
    any_ = pl.BlockSpec(memory_space=pl.ANY)
    shape = (pn.ns, 2, pn.rest, pn.pc, 8, 128)
    nsem = (pn.ns - 1) * (pn.rest + 1)
    return pl.pallas_call(
        functools.partial(kernel_g, pn),
        out_shape=jax.ShapeDtypeStruct(shape, BF16),
        in_specs=[any_],
        out_specs=any_,
        scratch_shapes=[pltpu.VMEM((pn.ndp * pn.pc, 8, 128), F32), pltpu.VMEM(shape, BF16), pltpu.SemaphoreType.DMA((2, nsem)), pltpu.SemaphoreType.DMA, pltpu.SemaphoreType.DMA],
        compiler_params=pltpu.CompilerParams(vmem_limit_bytes=64000000, collective_id=0, has_side_effects=True),
        name="gather",
    )(params.reshape(pn.units, 8, 128))


from jax.sharding import PartitionSpec as P


def solution(mesh):
    def local(images, cotangent, counts, rel_index, params, moment1, moment2, rates):
        pn = Plan(mesh, params.shape[0])
        xt = images.transpose(1, 2, 0, 3)
        ct = cotangent.transpose(1, 2, 0, 3)
        rel = rel_lanes(rel_index)
        flat = call_g(pn, params)
        wqkv, wp, w1, w2, vec, hwt, ob, qkv, p = call_a(pn, xt, flat, rel)
        y, dx, g = call_bc(pn, xt, ct, ob, wp, w1, w2, hwt, qkv, p, wqkv, vec, rel, counts)
        grad, new_params, new_first, new_second = call_adam(pn, rates, g, params, moment1, moment2)
        return (y.transpose(2, 0, 1, 3), dx.transpose(2, 0, 1, 3), grad, new_params, new_first, new_second)

    split = P(("dp", "opt"), None, None, None)
    return jax.shard_map(
        local, mesh=mesh,
        in_specs=(split, split, P(("dp", "opt")), P(), P("opt"), P("opt"), P("opt"), P()),
        out_specs=(split, split, P("opt"), P("opt"), P("opt"), P("opt")),
        check_vma=False)
```

time: 298 us -> 235 us (0.79)
  Pallas kernels: 283 us -> 228 us
  local copies, waits for them, and re-layouts: 13.4 us -> 5.32 us
    pallas_call x3 -> x2, Pallas kernels: 194 us -> 137 us  [the longest x1 122 us: call_bc(): pl.pallas_call(functools.partial(kernel_bc, pn), out_shape=outs, in_specs...]
    unnamed x11 -> x7, local copies, waits for them, and re-layouts: 12.7 us -> 4.62 us
where the time goes in v3:
time: 235 us; the launch traced here: 234 us
  Pallas kernels  228 us (97%)
  local copies, waits for them, and re-layouts  5.32 us (2%)
    pallas_call x1, Pallas kernels, call_bc(): pl.pallas_call(functools.partial(kernel_bc, pn), out_shape=outs, in_specs...  122 us
    pallas_call x1, Pallas kernels, call_a(): pl.pallas_call(functools.partial(kernel_a, pn), out_shape=outs, in_specs=...  46.1 us
    pallas_call x1, Pallas kernels, call_g(): pl.pallas_call(functools.partial(kernel_g, pn), out_shape=jax.ShapeDtypeS...  44.3 us
    pallas_call x1, Pallas kernels, call_adam(): pl.pallas_call(kernel_adam, grid=(pl.cdiv(pn.units, AU),), out_shape=[jax...  15.3 us

profile of v3, /device:TPU:0, one launch (start us, length us, event | category | flops | bytes accessed | tf_op | source)
XLA Modules:
  0.0 234.2 jit_solution(11565188225729454383)
XLA Ops:
  0.6 0.0 copy-start.1
  0.6 44.3 %gather.1.flat_hbm = bf16[4,2,4,97,8,128]{5,4,3,2,1,0:T(8,128)(2,1)} custom-call(f32[771,8,128]{2,1,0:T(8,128)} %bitcast.14), custom_call_target="tpu_custom_call" | custom-call | tf_op jit(solution)/shard_map/gather/pallas_call | solution.py:1027
  44.9 0.0 copy-done.1
  44.9 0.1 copy.15
  45.0 0.7 reshape.75.rel_ref
  45.7 46.1 %attend.1 = (bf16[512,1536]{1,0:T(8,128)(2,1)}, bf16[512,512]{1,0:T(8,128)(2,1)}, bf16[512,2048]{1,0:T(8,128)(2,1)}, bf16[2048,512]{1,0:T(8,128)(2,1)}, f32[16,5...) custom-call(bf16[14,14,8,512]{3,2,1,0:T(8,128)(2,1)} %bitcast.16, ...), custom_call_target="tpu_custom_call" | custom-call | tf_op jit(solution)/shard_map/attend/pallas_call | solution.py:295
  92.5 121.9 %back.1 = (bf16[14,14,8,512]{3,2,1,0:T(8,128)(2,1)}, f32[14,14,8,512]{3,2,1,0:T(8,128)}, f32[6168,128]{1,0:T(8,128)}) custom-call(bf16[14,14,8,512]{3,2,1,0:T(8,128)(2,1)} %bitcast.17, bf16[14,14,8,512]{3,2,1,0:T(8,128)(2,1)} %bitcast.22, bf16[1568,512]{1,0:T(8,128)(2,1)} %get-tuple-element.34.ob_hbm, bf16[512,512]{1,0:T(8,128)(2,1)} %get-tuple-element.35.wp_hbm, ...), custom_call_target="tpu_custom_call" | custom-call | tf_op jit(solution)/shard_map/back/pallas_call | solution.py:922
  214.4 15.3 %adamw.1 = (f32[771,8,128]{2,1,0:T(8,128)}, f32[771,8,128]{2,1,0:T(8,128)}, f32[771,8,128]{2,1,0:T(8,128)}, f32[771,8,128]{2,1,0:T(8,128)}) custom-call(f32[15]{0:T(128)} %rates.1, s32[1]{0:T(128)} %bitcast.6.first, f32[771,8,128]{2,1,0:T(8,128)} %bitcast.21, f32[771,8,128]{2,1,0:T(8,128)} %bitcast.15, f32[771,8,128]{2,1,0:T(8,128)} %bitcast.19, ...), custom_call_target="tpu_custom_call" | custom-call | tf_op jit(solution)/shard_map/adamw/pallas_call | solution.py:969
  229.7 0.0 copy-start
  229.7 2.8 %copy.19 = bf16[8,14,14,512]{3,0,2,1:T(8,128)(2,1)} copy(bf16[8,14,14,512]{3,0,2,1:T(8,128)(2,1)} %bitcast.23) | data formatting | bytes 3211264
  232.6 0.0 copy-done
  232.6 1.7 copy.20
  (1 shorter events, 0.0 us)
Async XLA Ops:
  0.6 44.3 %copy-start.1 = (s32[49,49]{1,0:T(8,128)S(1)}, s32[49,49]{1,0:T(8,128)}, u32[]{:S(2)}) copy-start(s32[49,49]{1,0:T(8,128)} %param.13) | copy-start | bytes 28816
  229.7 2.8 %copy-start = (f32[14,14,8,512]{3,2,1,0:T(8,128)S(1)}, f32[14,14,8,512]{3,2,1,0:T(8,128)}, u32[]{:S(2)}) copy-start(f32[14,14,8,512]{3,2,1,0:T(8,128)} %get-tuple-element.44) | copy-start | bytes 9633796

commit v4 on v3

--- a/solution.py
+++ b/solution.py
@@ -196,32 +196,172 @@
             bias[w * 4 + g] = jnp.where(k < SPAN, val, -1e30)
 
 
-def kernel_a(pn, x_hbm, flat_hbm, rel_ref,
+MESH = pl.DeviceIdType.MESH
+NMAT = 768
+
+
+class Plan:
+    def __init__(self, mesh, shard_len):
+        self.ndp = mesh.shape["dp"]
+        self.ns = mesh.shape["opt"]
+        self.rest = self.ndp // 2
+        self.units = shard_len // 1024
+        self.pc = -(-self.units // self.ndp)
+        self.ka = (BROW // 8) // self.units
+        self.base = self.ka * self.units
+        self.bunits = (self.ns - self.ka - 1) * self.units + self.ndp * self.pc
+        self.kh = -(-(R_W2 // 8 + 1) // self.units)
+        self.mrow = D // self.ndp
+        self.gunits = max(BROW // 8 + 1, self.ndp * self.pc)
+
+
+def place():
+    me = lax.axis_index("dp")
+    return lax.shift_right_arithmetic(me, 1), me & 1, lax.axis_index("opt")
+
+
+def peer(r, c):
+    return {"dp": 2 * r + c}
+
+
+def enter(pn, all_dp=False):
+    r, c, z = place()
+    bar = pltpu.get_barrier_semaphore()
+    pl.semaphore_signal(bar, inc=1, device_id=peer(r, 1 - c), device_id_type=MESH)
+    for j in range(1, pn.rest):
+        for to in ((c, 1 - c) if all_dp else (c,)):
+            pl.semaphore_signal(bar, inc=1, device_id=peer(lax.rem(r + j, pn.rest), to), device_id_type=MESH)
+    for j in range(1, pn.ns):
+        pl.semaphore_signal(bar, inc=1, device_id={"opt": lax.rem(z + j, pn.ns)}, device_id_type=MESH)
+    pl.semaphore_wait(bar, (pn.ndp - 1 if all_dp else pn.rest) + pn.ns - 1)
+
+
+def remote(src, dst, sems, n, where):
+    return pltpu.make_async_remote_copy(src_ref=src, dst_ref=dst, send_sem=sems.at[0, n], recv_sem=sems.at[1, n], device_id=where, device_id_type=MESH)
+
+
+class Gather:
+    def __init__(self, pn, wb, osend, orecv, xsem, ysem):
+        self.pn, self.wb, self.osend, self.orecv, self.xsem, self.ysem = pn, wb, osend, orecv, xsem, ysem
+
+    @staticmethod
+    def scratch(pn):
+        return [pltpu.VMEM((pn.ns, 2, pn.rest, pn.pc, 8, 128), BF16), pltpu.SemaphoreType.DMA((pn.ns,)), pltpu.SemaphoreType.DMA((pn.ns,)),
+                pltpu.SemaphoreType.DMA((2, pn.ns * pn.rest)), pltpu.SemaphoreType.DMA((2, pn.ns))]
+
+    def o(self, j):
+        r, c, z = place()
+        own = self.wb.at[z, c, r]
+        return pltpu.make_async_remote_copy(src_ref=own, dst_ref=own, send_sem=self.osend.at[j], recv_sem=self.orecv.at[z],
+                                            device_id={"opt": lax.rem(z + j, self.pn.ns)}, device_id_type=MESH)
+
+    def arrived(self, s):
+        r, c, z = place()
+        own = self.wb.at[s, c, r]
+        return pltpu.make_async_remote_copy(src_ref=own, dst_ref=own, send_sem=self.osend.at[0], recv_sem=self.orecv.at[s],
+                                            device_id={"opt": lax.rem(z + 1, self.pn.ns)}, device_id_type=MESH)
+
+    def x(self, s, j):
+        r, c, z = place()
+        own = self.wb.at[s, c, r]
+        return remote(own, own, self.xsem, s * self.pn.rest + j, peer(lax.rem(r + j, self.pn.rest), c))
+
+    def y(self, s):
+        r, c, z = place()
+        return remote(self.wb.at[s, c], self.wb.at[s, c], self.ysem, s, peer(r, 1 - c))
+
+    def start(self):
+        for j in range(1, self.pn.ns):
+            self.o(j).start()
+
+    def spread(self, s):
+        r, c, z = place()
+
+        @pl.when(z != s)
+        def _():
+            self.arrived(s).wait_recv()
+            for j in range(1, self.pn.rest):
+                self.x(s, j).start()
+
+    def pair(self, s):
+        r, c, z = place()
+
+        @pl.when(z != s)
+        def _():
+            for j in range(1, self.pn.rest):
+                self.x(s, j).wait_recv()
+            self.y(s).start()
+
+    def ready(self, s):
+        r, c, z = place()
+
+        @pl.when(z != s)
+        def _():
+            self.y(s).wait_recv()
+
+    def finish(self):
+        r, c, z = place()
+        for j in range(1, self.pn.ns):
+            self.o(j).wait_send()
+        for s in range(self.pn.ns):
+            @pl.when(z != s)
+            def _():
+                for j in range(1, self.pn.rest):
+                    self.x(s, j).wait_send()
+                self.y(s).wait_send()
+
+
+def kernel_a(pn, x_hbm, params, rel_ref,
              wqkv_o, wp_o, w1_o, w2_o, vec_o, hw_o, ob_o, qkv_o, p_o,
-             x_v, flat_v, fs, os_, bias, wqkv, wp, w1, w2, vec, hw, hwt, ob, qkvb, pb, xsem, fsem, osem, wsem):
+             x_v, fs, os_, bias, wqkv, wp, w1, w2, vec, hw, hwt, ob, qkvb, pb, xsem, fsem, osem, wsem, flat_v, *gsems):
     cps = window_copies(x_hbm, x_v, xsem, True)
     for c in cps:
         c.start()
-    fcp = pltpu.make_async_copy(flat_hbm, flat_v, fsem)
+    r, c, z = place()
+    gather = Gather(pn, flat_v, *gsems)
+    fcp = pltpu.make_async_copy(params, fs.at[pl.ds(0, pn.units * 8)], fsem)
     fcp.start()
+    enter(pn)
     fcp.wait()
+
+    def cast(p):
+        flat_v[z, p & 1, lax.shift_right_arithmetic(p, 1)] = fs[pl.ds(pl.multiple_of(p * pn.pc * 8, 8), pn.pc * 8), :].reshape(pn.pc, 8, 128).astype(BF16)
+    me = lax.axis_index("dp")
+    cast(me)
+    gather.start()
+
+    def others(j, _):
+        cast(lax.rem(me + j, pn.ndp))
+        return 0
+    lax.fori_loop(1, pn.ndp, others, 0)
+    for k in range(pn.ka + 1):
+        gather.spread(k)
+    for k in range(pn.ka):
+        gather.pair(k)
+    for k in range(pn.ka):
+        gather.ready(k)
     for k in range(pn.ka):
         pieces_to_rows(pn, flat_v, fs, k, pn.ndp, 0)
-    pieces_to_rows(pn, flat_v, fs, pn.ka, 1, 0)
     take_matrix(fs, R_QKV, wqkv, D, 12, False)
     vec[0:1, :] = vec_from(fs, R_G1, D, False)
     vec[1:2, :] = vec_from(fs, R_B1, D, False)
     vec[2:3, :] = vec_from(fs, R_BQ, D, False)
     vec[3:4, :] = vec_from(fs, R_BV, D, False)
-    build_bias(fs[R_TAB:R_TAB + 24, :], rel_ref, os_, bias)
-    for c in cps:
-        c.wait()
+    wos = [pltpu.make_async_copy(wqkv, wqkv_o, wsem.at[0])]
+    wos[0].start()
+    for cp in cps:
+        cp.wait()
     gain = vec[0:1, :]
     shift = vec[1:2, :]
     bq = vec[2:3, :]
     bv = vec[3:4, :]
 
     def rows(t, _):
+        @pl.when(t == 2)
+        def _():
+            gather.pair(pn.ka)
+            for k in range(pn.ka + 1, pn.ns):
+                gather.spread(k)
         r0 = pl.multiple_of(t * BLK, BLK)
         x = x_v[pl.ds(4 * t, 4)].reshape(BLK, D).astype(F32)
         xhat, _r = norm_stats(x)
@@ -236,29 +376,56 @@
             fs[pl.ds(c * RS + r0, BLK), :] = y
         return 0
     lax.fori_loop(0, NBLK, rows, 0)
-
+    gather.ready(pn.ka)
+    tab = []
+    for u in range(R_TAB // 8, R_TAB // 8 + 3):
+        k, at = (pn.ka, u - pn.base) if u >= pn.base else (pn.ka - 1, u - pn.base + pn.units)
+        p = at // pn.pc
+        tab.append(flat_v[k, p & 1, p >> 1, at - p * pn.pc].astype(F32))
+    build_bias(jnp.concatenate(tab, 0), rel_ref, os_, bias)
     heads = lane_head()
 
-    def attend(i, _):
-        w = lax.shift_right_arithmetic(i, 3)
-        b = i & 7
-        base = w * WROWS + b
-        for g in range(4):
+    def saved(t):
+        four = pl.ds(4 * t, 4)
+        return [pltpu.make_async_copy(qkvb.at[four], qkv_o.at[four], osem.at[2 + t]), pltpu.make_async_copy(pb.at[four], p_o.at[four], osem.at[2 + WB // 4 + t])]
+
+    def attend(t, _):
+        un = 4
+        items = [(un * t + n, g) for n in range(un) for g in range(4)]
+        ss = []
+        vs = []
+        for i, g in items:
+            w = lax.shift_right_arithmetic(i, 3)
+            base = w * WROWS + (i & 7)
             q = take_rows(fs, g * RS + base).astype(BF16)
             k = take_rows(fs, (4 + g) * RS + base).astype(BF16)
             v = take_rows(fs, (8 + g) * RS + base).astype(BF16)
             qkvb[i, g] = q
             qkvb[i, 4 + g] = k
             qkvb[i, 8 + g] = v
-            s = dot_nt(k, block_diag(q, heads)) + bias[w * 4 + g]
+            vs.append(v)
+            ss.append(dot_nt(k, block_diag(q, heads)) + bias[w * 4 + g])
+        ps = []
+        for (i, g), s in zip(items, ss):
             m = jnp.max(s, 0, keepdims=True)
             e = jnp.exp(s - m)
             p = (e * (1.0 / jnp.sum(e, 0, keepdims=True))).astype(BF16)
             pb[i, g] = p
+            ps.append(p)
+        for (i, g), p, v in zip(items, ps, vs):
+            w = lax.shift_right_arithmetic(i, 3)
+            base = w * WROWS + (i & 7)
             o = diag_sum(dot_tn(p, v), heads)
             put_rows(os_, g * RS + base, o)
+        for cp in saved(t):
+            cp.start()
+
+        @pl.when(t == 2)
+        def _():
+            for k in range(pn.ka + 1, pn.ns):
+                gather.pair(k)
         return 0
-    lax.fori_loop(0, WB, attend, 0)
+    lax.fori_loop(0, WB // 4, attend, 0)
 
     def outs(t, _):
         r0 = pl.multiple_of(t * BLK, BLK)
@@ -267,9 +434,11 @@
         return 0
     lax.fori_loop(0, NBLK, outs, 0)
     transpose_rows(hw, hwt)
-    cos = [pltpu.make_async_copy(a, b, osem.at[n]) for n, (a, b) in enumerate([(hwt, hw_o), (ob, ob_o), (qkvb, qkv_o), (pb, p_o)])]
-    for c in cos:
-        c.start()
+    cos = [pltpu.make_async_copy(a, b, osem.at[n]) for n, (a, b) in enumerate([(hwt, hw_o), (ob, ob_o)])]
+    for cp in cos:
+        cp.start()
+    for k in range(pn.ka + 1, pn.ns):
+        gather.ready(k)
     for k in range(pn.ka, pn.ns):
         pieces_to_rows(pn, flat_v, fs, k, pn.ndp, pn.base)
     first = pn.base * 8
@@ -280,14 +449,17 @@
         vec[4 + n:5 + n, :] = vec_from(fs, r - first, D, True)
     for n in range(4):
         vec[8 + n:9 + n, :] = vec_from(fs, R_C1 - first + 4 * n, D, True)
-    wos = [pltpu.make_async_copy(a, b, wsem.at[n]) for n, (a, b) in enumerate([(wqkv, wqkv_o), (wp, wp_o), (w1, w1_o), (w2, w2_o), (vec, vec_o)])]
-    for c in wos:
-        c.start()
-    for c in cos + wos:
-        c.wait()
-
-
-def call_a(pn, x, flat, rel):
+    for n, (a, b) in enumerate([(wp, wp_o), (w1, w1_o), (w2, w2_o), (vec, vec_o)]):
+        wos.append(pltpu.make_async_copy(a, b, wsem.at[n + 1]))
+        wos[-1].start()
+    for t in range(WB // 4):
+        cos += saved(t)
+    for cp in cos + wos:
+        cp.wait()
+    gather.finish()
+
+
+def call_a(pn, x, params, rel):
     any_ = pl.BlockSpec(memory_space=pl.ANY)
     sds = jax.ShapeDtypeStruct
     outs = [sds((D, 3 * D), BF16), sds((D, D), BF16), sds((D, HID), BF16), sds((HID, D), BF16), sds((16, D), F32),
@@ -298,14 +470,14 @@
         in_specs=[any_, any_, pl.BlockSpec(memory_space=pltpu.VMEM)],
         out_specs=[any_] * len(outs),
         scratch_shapes=[
-            pltpu.VMEM((28, 7, 8, D), BF16), pltpu.VMEM(flat.shape, BF16), pltpu.VMEM((12 * RS, 128), F32), pltpu.VMEM((4 * RS, 128), F32),
+            pltpu.VMEM((28, 7, 8, D), BF16), pltpu.VMEM((12 * RS, 128), F32), pltpu.VMEM((4 * RS, 128), F32),
             pltpu.VMEM((16, 64, 256), F32), pltpu.VMEM((D, 3 * D), BF16), pltpu.VMEM((D, D), BF16), pltpu.VMEM((D, HID), BF16), pltpu.VMEM((HID, D), BF16),
             pltpu.VMEM((16, D), F32), pltpu.VMEM((ROWS, D), BF16), pltpu.VMEM((D, ROWS), BF16), pltpu.VMEM((ROWS, D), BF16), pltpu.VMEM((WB, 12, 64, 128), BF16), pltpu.VMEM((WB, 4, 64, 256), BF16),
-            pltpu.SemaphoreType.DMA((NSEG,)), pltpu.SemaphoreType.DMA, pltpu.SemaphoreType.DMA((4,)), pltpu.SemaphoreType.DMA((5,)),
-        ],
-        compiler_params=pltpu.CompilerParams(vmem_limit_bytes=64000000),
+            pltpu.SemaphoreType.DMA((NSEG,)), pltpu.SemaphoreType.DMA, pltpu.SemaphoreType.DMA((2 + WB // 2,)), pltpu.SemaphoreType.DMA((5,)),
+        ] + Gather.scratch(pn),
+        compiler_params=pltpu.CompilerParams(vmem_limit_bytes=64000000, collective_id=0, has_side_effects=True),
         name="attend",
-    )(x, flat, rel)
+    )(x, params.reshape(pn.units * 8, 128), rel)
 
 
 def rel_lanes(rel_index):
@@ -370,50 +542,6 @@
         m = jnp.concatenate([jnp.where(low == j, part, 0.0) for j in range(8)], 0).astype(BF16)
         out = out + dot_nt(oh, m)
     return out
-
-
-MESH = pl.DeviceIdType.MESH
-NMAT = 768
-
-
-class Plan:
-    def __init__(self, mesh, shard_len):
-        self.ndp = mesh.shape["dp"]
-        self.ns = mesh.shape["opt"]
-        self.rest = self.ndp // 2
-        self.units = shard_len // 1024
-        self.pc = -(-self.units // self.ndp)
-        self.ka = (BROW // 8) // self.units
-        self.base = self.ka * self.units
-        self.bunits = (self.ns - self.ka - 1) * self.units + self.ndp * self.pc
-        self.kh = -(-(R_W2 // 8 + 1) // self.units)
-        self.mrow = D // self.ndp
-        self.gunits = max(BROW // 8 + 1, self.ndp * self.pc)
-
-
-def place():
-    me = lax.axis_index("dp")
-    return lax.shift_right_arithmetic(me, 1), me & 1, lax.axis_index("opt")
-
-
-def peer(r, c):
-    return {"dp": 2 * r + c}
-
-
-def enter(pn, all_dp=False):
-    r, c, z = place()
-    bar = pltpu.get_barrier_semaphore()
-    pl.semaphore_signal(bar, inc=1, device_id=peer(r, 1 - c), device_id_type=MESH)
-    for j in range(1, pn.rest):
-        for to in ((c, 1 - c) if all_dp else (c,)):
-            pl.semaphore_signal(bar, inc=1, device_id=peer(lax.rem(r + j, pn.rest), to), device_id_type=MESH)
-    for j in range(1, pn.ns):
-        pl.semaphore_signal(bar, inc=1, device_id={"opt": lax.rem(z + j, pn.ns)}, device_id_type=MESH)
-    pl.semaphore_wait(bar, (pn.ndp - 1 if all_dp else pn.rest) + pn.ns - 1)
-
-
-def remote(src, dst, sems, n, where):
-    return pltpu.make_async_remote_copy(src_ref=src, dst_ref=dst, send_sem=sems.at[0, n], recv_sem=sems.at[1, n], device_id=where, device_id_type=MESH)
 
 
 class Chunk:
@@ -770,40 +898,37 @@
         lo.start2()
         heads = lane_head()
 
-        def one(g, i):
-            base = lax.shift_right_arithmetic(i, 3) * WROWS + (i & 7)
-            do = take_rows(os_, g * RS + base).astype(BF16)
-            q = qkvb[i, g]
-            k = qkvb[i, 4 + g]
-            v = qkvb[i, 8 + g]
-            pbv = pb[i, g]
-            p = pbv.astype(F32)
-            dobd = block_diag(do, heads)
-            dp = dot_nt(v, dobd)
-            t = p * dp
-            ds = t - p * jnp.sum(t, 0, keepdims=True)
-            dsb = ds.astype(BF16)
-            put_rows(fs, 2 * RS + base, dot(pbv, dobd))
-            put_rows(fs, RS + base, dot(dsb, block_diag(q, heads)))
-            put_rows(fs, base, diag_sum(dot_tn(dsb, k), heads) * SCALE)
-            return ds
-
-        mid = {0: (hi.start3,), 1: (ac[0].start2, hi.start4), 2: (hi.start5, ac[1].start2, ac[0].start3), 3: (ac[2].start2, ac[1].start3, ac[0].start4)}
-        end = {0: (), 1: (lo.start3,), 2: (lo.start4,), 3: (lo.start5,)}
+        def several(g, items):
+            bases = [lax.shift_right_arithmetic(i, 3) * WROWS + (i & 7) for i in items]
+            dobds = [block_diag(take_rows(os_, g * RS + base).astype(BF16), heads) for base in bases]
+            dps = [dot_nt(qkvb[i, 8 + g], d) for i, d in zip(items, dobds)]
+            total = dtab[g]
+            dsbs = []
+            for i, dp in zip(items, dps):
+                p = pb[i, g].astype(F32)
+                t = p * dp
+                ds = t - p * jnp.sum(t, 0, keepdims=True)
+                total = total + ds
+                dsbs.append(ds.astype(BF16))
+            dtab[g] = total
+            dvs = [dot(pb[i, g], d) for i, d in zip(items, dobds)]
+            dks = [dot(d, block_diag(qkvb[i, g], heads)) for i, d in zip(items, dsbs)]
+            dqs = [dot_tn(d, qkvb[i, 4 + g]) for i, d in zip(items, dsbs)]
+            for base, dv, dk, dqv in zip(bases, dvs, dks, dqs):
+                put_rows(fs, 2 * RS + base, dv)
+                put_rows(fs, RS + base, dk)
+                put_rows(fs, base, diag_sum(dqv, heads) * SCALE)
+
+        mid = {0: (hi.start3,), 1: (ac[0].start2,), 2: (ac[1].start2, hi.start4), 3: (ac[2].start2,)}
         for g in range(4):
             def attend(t, _):
                 @pl.when(t == 4)
                 def _():
                     for f in mid[g]:
                         f()
-                total = dtab[g]
-                for n in range(4):
-                    total = total + one(g, 4 * t + n)
-                dtab[g] = total
+                several(g, [4 * t + n for n in range(4)])
                 return 0
             lax.fori_loop(0, WB // 4, attend, 0)
-            for f in end[g]:
-                f()
             parts = []
             for n in range(3):
                 v = fs[n * RS:n * RS + ROWS, :]
@@ -828,7 +953,7 @@
         tab = table_grad(rel_ref, os_, dtab)
         for n in range(3):
             small.own[2 + n] = tab[8 * n:8 * n + 8].astype(BF16)
-        late = {1: (ac[3].start2, ac[2].start3, ac[1].start4, ac[0].start5), 3: (ac[3].start3, ac[2].start4, ac[1].start5), 5: (ac[3].start4, ac[2].start5)}
+        late = {1: (lo.start3, ac[3].start2), 2: (ac[0].start3, hi.start5), 3: (ac[1].start3,), 4: (ac[2].start3,), 5: (ac[3].start3, ac[0].start4), 6: (ac[1].start4,)}
 
         def rows1(t, _):
             for k, fns in late.items():
@@ -855,10 +980,10 @@
         ycs = window_copies(dx_hbm, dx1, xsem, False)
         for cp in ycs:
             cp.start()
-        ac[3].start5()
+        for f in (lo.start4, ac[2].start4, ac[3].start4, ac[0].start5, ac[1].start5, small.start2, lo.start5, ac[2].start5, ac[3].start5):
+            f()
         for ch in chunks:
             ch.finish()
-        small.start2()
         r, c, z = place()
         g = os_
 
@@ -939,26 +1064,46 @@
 def kernel_adam(rates, first, g, p, m1, m2, g_o, p_o, m_o, v_o):
     shape = (AU, 8, 128)
     u0 = first[0] + pl.program_id(0) * AU
-    index = ((u0 + lax.broadcasted_iota(jnp.int32, shape, 0)) * 8 + lax.broadcasted_iota(jnp.int32, shape, 1)) * 128 + lax.broadcasted_iota(jnp.int32, shape, 2)
-    rate = jnp.zeros(shape, F32) + rates[0]
-    decay = jnp.zeros(shape, F32)
-    at = 0
-    for n, length in enumerate(LENGTHS):
-        at += length
-        after = index >= at
-        rate = jnp.where(after, rates[n + 1], rate)
-        if n in DECAYED or n + 1 in DECAYED:
-            decay = jnp.where(after, 0.05 if n + 1 in DECAYED else 0.0, decay)
-    grad = g[...]
-    w = p[...]
-    m = 0.9 * m1[...] + 0.1 * grad
-    v = 0.999 * m2[...] + 0.001 * grad * grad
-    mh = m / (1.0 - 0.9 ** STEP)
-    vh = v / (1.0 - 0.999 ** STEP)
-    p_o[...] = w - rate * (mh / (jnp.sqrt(vh) + 1e-08) + decay * w)
-    m_o[...] = m
-    v_o[...] = v
-    g_o[...] = grad
+    starts = [sum(LENGTHS[:n + 1]) for n in range(len(LENGTHS))]
+
+    def group(at):
+        k = jnp.int32(0)
+        for s in starts:
+            k = k + (at >= s).astype(jnp.int32)
+        return k
+
+    def update(rate, decay):
+        grad = g[...]
+        w = p[...]
+        m = 0.9 * m1[...] + 0.1 * grad
+        v = 0.999 * m2[...] + 0.001 * grad * grad
+        mh = m / (1.0 - 0.9 ** STEP)
+        vh = v / (1.0 - 0.999 ** STEP)
+        p_o[...] = w - rate * (mh / (jnp.sqrt(vh) + 1e-08) + decay * w)
+        m_o[...] = m
+        v_o[...] = v
+        g_o[...] = grad
+    k0 = group(u0 * 1024)
+    k1 = group((u0 + AU) * 1024 - 1)
+
+    @pl.when(k0 == k1)
+    def _():
+        decay = jnp.float32(0.0)
+        for n in DECAYED:
+            decay = jnp.where(k0 == n, jnp.float32(0.05), decay)
+        update(rates[k0], decay)
+
+    @pl.when(k0 != k1)
+    def _():
+        index = ((u0 + lax.broadcasted_iota(jnp.int32, shape, 0)) * 8 + lax.broadcasted_iota(jnp.int32, shape, 1)) * 128 + lax.broadcasted_iota(jnp.int32, shape, 2)
+        rate = jnp.zeros(shape, F32) + rates[0]
+        decay = jnp.zeros(shape, F32)
+        for n, s in enumerate(starts):
+            after = index >= s
+            rate = jnp.where(after, rates[n + 1], rate)
+            if n in DECAYED or n + 1 in DECAYED:
+                decay = jnp.where(after, 0.05 if n + 1 in DECAYED else 0.0, decay)
+        update(rate, decay)
 
 
 def call_adam(pn, rates, g, params, mom1, mom2):
@@ -978,63 +1123,6 @@
     return [t.reshape(-1) for t in out]
 
 
-def kernel_g(pn, params, w_o, p_v, wb, sems, isem, osem):
-    r, c, z = place()
-    cp = pltpu.make_async_copy(params, p_v.at[pl.ds(0, pn.units)], isem)
-    cp.start()
-    enter(pn)
-    cp.wait()
-
-    def cast(p, _):
-        wb[z, p & 1, lax.shift_right_arithmetic(p, 1)] = p_v[pl.ds(p * pn.pc, pn.pc)].astype(BF16)
-        return 0
-    lax.fori_loop(0, pn.ndp, cast, 0)
-
-    def o(j):
-        to = lax.rem(z + j, pn.ns)
-        return remote(wb.at[z, c, r], wb.at[z, c, r], sems, j - 1, {"opt": to})
-
-    def x(k, j):
-        to = lax.rem(r + j, pn.rest)
-        src = lax.rem(z - k + pn.ns, pn.ns)
-        return remote(wb.at[src, c, r], wb.at[src, c, r], sems, pn.ns - 1 + (k - 1) * (pn.rest - 1) + j - 1, peer(to, c))
-
-    def y(k):
-        src = lax.rem(z - k + pn.ns, pn.ns)
-        return remote(wb.at[src, c], wb.at[src, c], sems, (pn.ns - 1) * pn.rest + k - 1, peer(r, 1 - c))
-
-    for j in range(1, pn.ns):
-        o(j).start()
-    for k in range(1, pn.ns):
-        o(k).wait()
-        for j in range(1, pn.rest):
-            x(k, j).start()
-    for k in range(1, pn.ns):
-        for j in range(1, pn.rest):
-            x(k, j).wait()
-        y(k).start()
-    for k in range(1, pn.ns):
-        y(k).wait()
-    cp = pltpu.make_async_copy(wb, w_o, osem)
-    cp.start()
-    cp.wait()
-
-
-def call_g(pn, params):
-    any_ = pl.BlockSpec(memory_space=pl.ANY)
-    shape = (pn.ns, 2, pn.rest, pn.pc, 8, 128)
-    nsem = (pn.ns - 1) * (pn.rest + 1)
-    return pl.pallas_call(
-        functools.partial(kernel_g, pn),
-        out_shape=jax.ShapeDtypeStruct(shape, BF16),
-        in_specs=[any_],
-        out_specs=any_,
-        scratch_shapes=[pltpu.VMEM((pn.ndp * pn.pc, 8, 128), F32), pltpu.VMEM(shape, BF16), pltpu.SemaphoreType.DMA((2, nsem)), pltpu.SemaphoreType.DMA, pltpu.SemaphoreType.DMA],
-        compiler_params=pltpu.CompilerParams(vmem_limit_bytes=64000000, collective_id=0, has_side_effects=True),
-        name="gather",
-    )(params.reshape(pn.units, 8, 128))
-
-
 from jax.sharding import PartitionSpec as P
 
 
@@ -1044,8 +1132,7 @@
         xt = images.transpose(1, 2, 0, 3)
         ct = cotangent.transpose(1, 2, 0, 3)
         rel = rel_lanes(rel_index)
-        flat = call_g(pn, params)
-        wqkv, wp, w1, w2, vec, hwt, ob, qkv, p = call_a(pn, xt, flat, rel)
+        wqkv, wp, w1, w2, vec, hwt, ob, qkv, p = call_a(pn, xt, params, rel)
         y, dx, g = call_bc(pn, xt, ct, ob, wp, w1, w2, hwt, qkv, p, wqkv, vec, rel, counts)
         grad, new_params, new_first, new_second = call_adam(pn, rates, g, params, moment1, moment2)
         return (y.transpose(2, 0, 1, 3), dx.transpose(2, 0, 1, 3), grad, new_params, new_first, new_second)

time: 235 us -> 194 us (0.83)
  Pallas kernels: 228 us -> 186 us
    pallas_call x1 -> x0, Pallas kernels: 44.3 us -> none  [call_g(): pl.pallas_call(functools.partial(kernel_g, pn), out_shape=jax.ShapeDtypeS...]
    pallas_call x1, Pallas kernels: 46.1 us -> 59.4 us  [call_a(): pl.pallas_call(functools.partial(kernel_a, pn), out_shape=outs, in_specs=...]
    pallas_call x1, Pallas kernels: 122 us -> 112 us  [call_bc(): pl.pallas_call(functools.partial(kernel_bc, pn), out_shape=outs, in_specs...]
    unnamed x7 -> x5, local copies, waits for them, and re-layouts: 4.62 us -> 5.36 us
where the time goes in v4:
time: 194 us
  Pallas kernels  186 us (96%)
  local copies, waits for them, and re-layouts  6.07 us (3%)
    pallas_call x1, Pallas kernels, call_bc(): pl.pallas_call(functools.partial(kernel_bc, pn), out_shape=outs, in_specs...  112 us
    pallas_call x1, Pallas kernels, call_a(): pl.pallas_call(functools.partial(kernel_a, pn), out_shape=outs, in_specs=...  59.4 us
    pallas_call x1, Pallas kernels, call_adam(): pl.pallas_call(kernel_adam, grid=(pl.cdiv(pn.units, AU),), out_shape=[jax...  15.1 us
    unnamed x5, local copies, waits for them, and re-layouts  5.36 us

profile of v4, /device:TPU:0, one launch (start us, length us, event | category | flops | bytes accessed | tf_op | source)
XLA Modules:
  0.0 193.7 jit_solution(2709200170796316812)
XLA Ops:
  0.6 0.8 copy.15
  1.5 0.7 reshape.77.rel_ref
  2.2 59.4 %attend.1 = (bf16[512,1536]{1,0:T(8,128)(2,1)}, bf16[512,512]{1,0:T(8,128)(2,1)}, bf16[512,2048]{1,0:T(8,128)(2,1)}, bf16[2048,512]{1,0:T(8,128)(2,1)}, f32[16,5...) custom-call(bf16[14,14,8,512]{3,2,1,0:T(8,128)(2,1)} %bitcast.17, ...), custom_call_target="tpu_custom_call" | custom-call | tf_op jit(solution)/shard_map/attend/pallas_call | solution.py:467
  62.3 111.8 %back.1 = (bf16[14,14,8,512]{3,2,1,0:T(8,128)(2,1)}, f32[14,14,8,512]{3,2,1,0:T(8,128)}, f32[6168,128]{1,0:T(8,128)}) custom-call(bf16[14,14,8,512]{3,2,1,0:T(8,128)(2,1)} %bitcast.18, bf16[14,14,8,512]{3,2,1,0:T(8,128)(2,1)} %bitcast.23, bf16[1568,512]{1,0:T(8,128)(2,1)} %get-tuple-element.34.ob_hbm, bf16[512,512]{1,0:T(8,128)(2,1)} %get-tuple-element.35.wp_hbm, ...), custom_call_target="tpu_custom_call" | custom-call | tf_op jit(solution)/shard_map/back/pallas_call | solution.py:1047
  174.0 15.1 %adamw.1 = (f32[771,8,128]{2,1,0:T(8,128)}, f32[771,8,128]{2,1,0:T(8,128)}, f32[771,8,128]{2,1,0:T(8,128)}, f32[771,8,128]{2,1,0:T(8,128)}) custom-call(f32[15]{0:T(128)} %rates.1, s32[1]{0:T(128)} %bitcast.6.first, f32[771,8,128]{2,1,0:T(8,128)} %bitcast.22, f32[771,8,128]{2,1,0:T(8,128)} %bitcast.16, f32[771,8,128]{2,1,0:T(8,128)} %bitcast.20, ...), custom_call_target="tpu_custom_call" | custom-call | tf_op jit(solution)/shard_map/adamw/pallas_call | solution.py:1114
  189.2 0.0 copy-start
  189.2 2.8 %copy.19 = bf16[8,14,14,512]{3,0,2,1:T(8,128)(2,1)} copy(bf16[8,14,14,512]{3,0,2,1:T(8,128)(2,1)} %bitcast.24) | data formatting | bytes 3211264
  192.0 0.0 copy-done
  192.0 1.7 copy.20
  (1 shorter events, 0.0 us)
Async XLA Ops:
  189.2 2.8 %copy-start = (f32[14,14,8,512]{3,2,1,0:T(8,128)S(1)}, f32[14,14,8,512]{3,2,1,0:T(8,128)}, u32[]{:S(2)}) copy-start(f32[14,14,8,512]{3,2,1,0:T(8,128)} %get-tuple-element.44) | copy-start | bytes 9633796

commit v5 on v4

--- a/solution.py
+++ b/solution.py
@@ -241,74 +241,85 @@
 
 
 class Gather:
-    def __init__(self, pn, wb, osend, orecv, xsem, ysem):
-        self.pn, self.wb, self.osend, self.orecv, self.xsem, self.ysem = pn, wb, osend, orecv, xsem, ysem
+    def __init__(self, pn, wb, osem, xsem, ysem):
+        self.pn, self.wb, self.osem, self.xsem, self.ysem = pn, wb, osem, xsem, ysem
+        h = (pn.pc + 1) // 2
+        self.parts = [pl.ds(0, h), pl.ds(h, pn.pc - h)]
 
     @staticmethod
     def scratch(pn):
-        return [pltpu.VMEM((pn.ns, 2, pn.rest, pn.pc, 8, 128), BF16), pltpu.SemaphoreType.DMA((pn.ns,)), pltpu.SemaphoreType.DMA((pn.ns,)),
-                pltpu.SemaphoreType.DMA((2, pn.ns * pn.rest)), pltpu.SemaphoreType.DMA((2, pn.ns))]
-
-    def o(self, j):
-        r, c, z = place()
-        own = self.wb.at[z, c, r]
-        return pltpu.make_async_remote_copy(src_ref=own, dst_ref=own, send_sem=self.osend.at[j], recv_sem=self.orecv.at[z],
+        return [pltpu.VMEM((pn.ns, 2, pn.rest, pn.pc, 8, 128), BF16), pltpu.SemaphoreType.DMA((2, 2 * pn.ns)),
+                pltpu.SemaphoreType.DMA((2, 2 * pn.ns * pn.rest)), pltpu.SemaphoreType.DMA((2, 2 * pn.ns))]
+
+    def o(self, j, h):
+        r, c, z = place()
+        own = self.wb.at[z, c, r, self.parts[h]]
+        return pltpu.make_async_remote_copy(src_ref=own, dst_ref=own, send_sem=self.osem.at[0, 2 * j + h], recv_sem=self.osem.at[1, 2 * z + h],
                                             device_id={"opt": lax.rem(z + j, self.pn.ns)}, device_id_type=MESH)
 
-    def arrived(self, s):
-        r, c, z = place()
-        own = self.wb.at[s, c, r]
-        return pltpu.make_async_remote_copy(src_ref=own, dst_ref=own, send_sem=self.osend.at[0], recv_sem=self.orecv.at[s],
+    def arrived(self, s, h):
+        r, c, z = place()
+        own = self.wb.at[s, c, r, self.parts[h]]
+        return pltpu.make_async_remote_copy(src_ref=own, dst_ref=own, send_sem=self.osem.at[0, h], recv_sem=self.osem.at[1, 2 * s + h],
                                             device_id={"opt": lax.rem(z + 1, self.pn.ns)}, device_id_type=MESH)
 
-    def x(self, s, j):
-        r, c, z = place()
-        own = self.wb.at[s, c, r]
-        return remote(own, own, self.xsem, s * self.pn.rest + j, peer(lax.rem(r + j, self.pn.rest), c))
-
-    def y(self, s):
-        r, c, z = place()
-        return remote(self.wb.at[s, c], self.wb.at[s, c], self.ysem, s, peer(r, 1 - c))
-
-    def start(self):
-        for j in range(1, self.pn.ns):
-            self.o(j).start()
-
-    def spread(self, s):
+    def x(self, s, h, j):
+        r, c, z = place()
+        own = self.wb.at[s, c, r, self.parts[h]]
+        return remote(own, own, self.xsem, (2 * s + h) * self.pn.rest + j, peer(lax.rem(r + j, self.pn.rest), c))
+
+    def y(self, s, h):
+        r, c, z = place()
+        own = self.wb.at[s, c, :, self.parts[h]]
+        return remote(own, own, self.ysem, 2 * s + h, peer(r, 1 - c))
+
+    def start(self, first):
+        r, c, z = place()
+        for h in range(2):
+            for j in range(1, self.pn.ns):
+                soon = (z < self.pn.ka) | (z + j >= self.pn.ns)
+
+                @pl.when(soon if first else jnp.logical_not(soon))
+                def _():
+                    self.o(j, h).start()
+
+    def spread(self, s, h):
         r, c, z = place()
 
         @pl.when(z != s)
         def _():
-            self.arrived(s).wait_recv()
+            self.arrived(s, h).wait_recv()
             for j in range(1, self.pn.rest):
-                self.x(s, j).start()
-
-    def pair(self, s):
+                self.x(s, h, j).start()
+
+    def pair(self, s, h):
         r, c, z = place()
 
         @pl.when(z != s)
         def _():
             for j in range(1, self.pn.rest):
-                self.x(s, j).wait_recv()
-            self.y(s).start()
+                self.x(s, h, j).wait_recv()
+            self.y(s, h).start()
 
     def ready(self, s):
         r, c, z = place()
 
         @pl.when(z != s)
         def _():
-            self.y(s).wait_recv()
+            for h in range(2):
+                self.y(s, h).wait_recv()
 
     def finish(self):
         r, c, z = place()
-        for j in range(1, self.pn.ns):
-            self.o(j).wait_send()
-        for s in range(self.pn.ns):
-            @pl.when(z != s)
-            def _():
-                for j in range(1, self.pn.rest):
-                    self.x(s, j).wait_send()
-                self.y(s).wait_send()
+        for h in range(2):
+            for j in range(1, self.pn.ns):
+                self.o(j, h).wait_send()
+            for s in range(self.pn.ns):
+                @pl.when(z != s)
+                def _():
+                    for j in range(1, self.pn.rest):
+                        self.x(s, h, j).wait_send()
+                    self.y(s, h).wait_send()
 
 
 def kernel_a(pn, x_hbm, params, rel_ref,
@@ -328,16 +339,20 @@
         flat_v[z, p & 1, lax.shift_right_arithmetic(p, 1)] = fs[pl.ds(pl.multiple_of(p * pn.pc * 8, 8), pn.pc * 8), :].reshape(pn.pc, 8, 128).astype(BF16)
     me = lax.axis_index("dp")
     cast(me)
-    gather.start()
+    gather.start(True)
 
     def others(j, _):
         cast(lax.rem(me + j, pn.ndp))
         return 0
     lax.fori_loop(1, pn.ndp, others, 0)
-    for k in range(pn.ka + 1):
-        gather.spread(k)
-    for k in range(pn.ka):
-        gather.pair(k)
+    for h in range(2):
+        for k in range(pn.ka):
+            gather.spread(k, h)
+    gather.start(False)
+    for h in range(2):
+        for k in range(pn.ka):
+            gather.pair(k, h)
+        gather.spread(pn.ka, h)
     for k in range(pn.ka):
         gather.ready(k)
     for k in range(pn.ka):
@@ -359,9 +374,11 @@
     def rows(t, _):
         @pl.when(t == 2)
         def _():
-            gather.pair(pn.ka)
+            for h in range(2):
+                gather.pair(pn.ka, h)
             for k in range(pn.ka + 1, pn.ns):
-                gather.spread(k)
+                for h in range(2):
+                    gather.spread(k, h)
         r0 = pl.multiple_of(t * BLK, BLK)
         x = x_v[pl.ds(4 * t, 4)].reshape(BLK, D).astype(F32)
         xhat, _r = norm_stats(x)
@@ -423,7 +440,8 @@
         @pl.when(t == 2)
         def _():
             for k in range(pn.ka + 1, pn.ns):
-                gather.pair(k)
+                for h in range(2):
+                    gather.pair(k, h)
         return 0
     lax.fori_loop(0, WB // 4, attend, 0)
 
@@ -508,6 +526,24 @@
     fs[here, :] = jnp.where(lane < LANE, v, fs[here, :])
 
 
+def shifted(blocks):
+    return [pltpu.roll(v, LANE, 1) for v in blocks]
+
+
+def put_tile(fs, base, stride, blocks):
+    n = blocks[0].shape[0]
+    lane = lax.broadcasted_iota(jnp.int32, (n, 128), 1)
+    head = lax.broadcasted_iota(jnp.int32, (n, 128), 0) == 0
+    one = lax.broadcasted_iota(jnp.int32, (1, 128), 1)
+    v = shifted(blocks)
+    first = fs[pl.ds(base, 1), :]
+    last = fs[pl.ds(base + n * stride, 1), :]
+    before = jnp.where(head, first, pltpu.roll(v[-1], 1, 0))
+    for c in range(len(blocks)):
+        fs[pl.ds(base + c, n, stride=stride), :] = jnp.where(lane >= LANE, v[c], before if c == 0 else v[c - 1])
+    fs[pl.ds(base + n * stride, 1), :] = jnp.where(one < LANE, v[-1][n - 1:n], last)
+
+
 def put_vec(fs, row, v):
     for c in range(v.shape[1] // 128):
         put_block(fs, row + c, 1, v[:, c * 128:(c + 1) * 128])
@@ -545,9 +581,11 @@
 
 
 class Chunk:
-    def __init__(self, pn, k0, k1, scatter, m, src, r1, r2, r3, sems, ag):
-        self.pn, self.k0, self.k1, self.scatter, self.m = pn, k0, k1, scatter, m
-        self.n = m * (k1 - k0) if scatter else m
+    def __init__(self, pn, k0, k1, n, at, flip, src, r1, r2, sems, r3, ag):
+        self.pn, self.k0, self.k1, self.n, self.at = pn, k0, k1, n, at
+        self.steps = list(range(pn.rest.bit_length() - 1))
+        if flip:
+            self.steps.reverse()
         self.src, self.r1, self.r2, self.r3, self.ag, self.sems = src, r1, r2, r3, ag, sems
         self.k2 = 1
         self.k3 = self.k2 + pn.rest - 1
@@ -555,11 +593,10 @@
         self.k5 = self.k4 + pn.rest - 1
 
     @staticmethod
-    def scratch(pn, m, count, shared):
-        n = m * count
+    def scratch(pn, n, shared):
         return [pltpu.VMEM((2, pn.rest, n, 8, 128), BF16), pltpu.VMEM((pn.rest, n, 8, 128), BF16), pltpu.VMEM((pn.rest - 1, n, 8, 128), BF16),
-                pltpu.VMEM((pn.ns - 1, m, 8, 128), BF16),
-                pltpu.SemaphoreType.DMA((2, 2 * pn.rest + pn.ns - 1))] + [pltpu.VMEM((2, pn.rest, m, 8, 128), BF16)] * (not shared)
+                pltpu.SemaphoreType.DMA((2, 2 * pn.rest + pn.ns - 1))] + (
+            [] if shared else [pltpu.VMEM((pn.ns - 1, n, 8, 128), BF16), pltpu.VMEM((2, pn.rest, n, 8, 128), BF16)])
 
     def here(self, z):
         return (z >= self.k0) & (z < self.k1)
@@ -571,48 +608,57 @@
     def start1(self):
         self.c1().start()
 
-    def c2(self, j):
-        r, c, z = place()
-        to = lax.rem(r + j, self.pn.rest)
-        return remote(self.src.at[c, to], self.r2.at[j - 1], self.sems, self.k2 + j - 1, peer(to, c))
+    def owners(self, i, other):
+        r, c, z = place()
+        bits = [lax.shift_right_arithmetic(r, b) & 1 for b in range(len(self.steps))]
+        done, b, free = self.steps[:i], self.steps[i], self.steps[i + 1:]
+        base = sum((bits[d] * (1 << d) for d in done), jnp.int32(0))
+        base = base + (1 - bits[b] if other else bits[b]) * (1 << b)
+        out = [base + sum(((q >> n) & 1) << f for n, f in enumerate(free)) for q in range(1 << len(free))]
+        slot = sum(self.pn.rest >> (k + 1) for k in range(i))
+        return out, slot
+
+    def c2(self, i, q):
+        r, c, z = place()
+        own, slot = self.owners(i, True)
+        b = self.steps[i]
+        bit = lax.shift_right_arithmetic(r, b) & 1
+        to = r + (1 - 2 * bit) * (1 << b)
+        return remote(self.src.at[c, own[q]], self.r2.at[slot + q], self.sems, self.k2 + slot + q, peer(to, c))
+
+    def add(self, owner, term):
+        r, c, z = place()
+        self.src[c, owner] = (self.src[c, owner].astype(F32) + term.astype(F32)).astype(BF16)
 
     def start2(self):
-        r, c, z = place()
         self.c1().wait()
-        step = self.m
-        for j in list(range(1, self.pn.rest)) + [0]:
-            to = lax.rem(r + j, self.pn.rest)
-
-            def add(t, _):
-                u = pl.ds(t * step, step)
-                self.src[c, to, u] = (self.src[c, to, u].astype(F32) + self.r1[to, u].astype(F32)).astype(BF16)
-                return 0
-            lax.fori_loop(0, self.n // step, add, 0)
-            if j:
-                self.c2(j).start()
+        for q, owner in enumerate(self.owners(0, True)[0]):
+            self.add(owner, self.r1[owner])
+            self.c2(0, q).start()
+        for owner in self.owners(0, False)[0]:
+            self.add(owner, self.r1[owner])
+
+    def landed(self, i):
+        own, slot = self.owners(i, False)
+        for q in range(len(own)):
+            self.c2(i, q).wait()
+        for q, owner in enumerate(own):
+            self.add(owner, self.r2[slot + q])
+
+    def halve(self):
+        for i in range(1, len(self.steps)):
+            self.landed(i - 1)
+            for q in range(len(self.owners(i, True)[0])):
+                self.c2(i, q).start()
 
     def c3(self, j):
         r, c, z = place()
         to = lax.rem(z + j, self.pn.ns)
-        src = self.src.at[c, r]
-        if self.scatter:
-            src = src.at[pl.ds(lax.clamp(0, to - self.k0, self.k1 - self.k0 - 1) * self.m, self.m)]
-        return to, remote(src, self.r3.at[j - 1], self.sems, self.k3 + j - 1, {"opt": to})
+        return to, remote(self.src.at[c, r], self.r3.at[j - 1], self.sems, self.k3 + j - 1, {"opt": to})
 
     def start3(self):
         r, c, z = place()
-        for j in range(1, self.pn.rest):
-            self.c2(j).wait()
-        step = self.m
-
-        def add(t, _):
-            u = pl.ds(t * step, step)
-            v = self.src[c, r, u].astype(F32)
-            for j in range(1, self.pn.rest):
-                v = v + self.r2[j - 1, u].astype(F32)
-            self.src[c, r, u] = v.astype(BF16)
-            return 0
-        lax.fori_loop(0, self.n // step, add, 0)
+        self.landed(len(self.steps) - 1)
         for j in range(1, self.pn.ns):
             to, cp = self.c3(j)
 
@@ -637,8 +683,7 @@
         def _():
             for j in range(1, self.pn.ns):
                 self.c3(j)[1].wait_recv()
-            at = lax.clamp(0, z - self.k0, self.k1 - self.k0 - 1) * self.m if self.scatter else 0
-            v = self.src[c, r, pl.ds(at, self.m)].astype(F32)
+            v = self.src[c, r].astype(F32)
             for j in range(1, self.pn.ns):
                 v = v + self.r3[j - 1].astype(F32)
             self.ag[c, r] = v.astype(BF16)
@@ -753,13 +798,23 @@
     dx1, wp, acc, dsem = refs[:4]
     refs = refs[4:]
     chunks = []
-    for n, (k0, k1, scatter, m) in enumerate(part_list(pn)):
-        if n == 1:
-            refs.insert(5, chunks[0].ag)
-        chunks.append(Chunk(pn, k0, k1, scatter, m, *refs[:6]))
+    nb = 2 * (pn.ns - pn.ka)
+    for n, (k0, k1, m, at, flip) in enumerate(part_list(pn)):
+        if 1 < n < nb:
+            refs[4:4] = [chunks[n % 2].r3, chunks[n % 2].ag]
+        chunks.append(Chunk(pn, k0, k1, m, at, flip, *refs[:6]))
         refs = refs[6:]
-    hi, lo = chunks[:2]
-    ac = chunks[2:]
+    shards, ac = chunks[:nb], chunks[nb:]
+    his = [ch for ch in shards if ch.k0 >= pn.kh]
+    los = [ch for ch in shards if ch.k0 < pn.kh]
+    mids, last = los[:-2], los[-2:]
+
+    def each(chs, name):
+        return tuple(getattr(ch, name) for ch in chs)
+
+    def run(fns):
+        for f in fns:
+            f()
     small = Small(pn, *refs)
     count = counts[0]
 
@@ -832,41 +887,48 @@
         def w2rows(t, _):
             r0 = pl.multiple_of(t * 512, 512)
             v = dot_tn(a[:, pl.ds(r0, 512)], dyf)
-            for c in range(4):
-                put_block(fs, R_W2 - first + r0 * 4 + c, 4, v[:, c * 128:(c + 1) * 128])
+            put_tile(fs, R_W2 - first + r0 * 4, 4, [v[:, c * 128:(c + 1) * 128] for c in range(4)])
             return 0
         lax.fori_loop(0, HID // 512, w2rows, 0)
         put_vec(fs, R_C2 - first, vg[0:1])
 
         def fill(ch):
-            for k in range(ch.k0, ch.k1):
-                def piece(p, _):
-                    row = pl.multiple_of(((k - pn.ka) * pn.units + p * pn.pc) * 8, 8)
-                    ch.src[p & 1, lax.shift_right_arithmetic(p, 1), (k - ch.k0) * pn.pc:(k - ch.k0 + 1) * pn.pc] = fs[pl.ds(row, pn.pc * 8), :].reshape(pn.pc, 8, 128).astype(BF16)
-                    return 0
-                lax.fori_loop(0, pn.ndp, piece, 0)
-        fill(hi)
-        hi.start1()
+            def piece(p, _):
+                row = pl.multiple_of(((ch.k0 - pn.ka) * pn.units + p * pn.pc + ch.at) * 8, 8)
+                ch.src[p & 1, lax.shift_right_arithmetic(p, 1)] = fs[pl.ds(row, ch.n * 8), :].reshape(ch.n, 8, 128).astype(BF16)
+                return 0
+            lax.fori_loop(0, pn.ndp, piece, 0)
+            ch.start1()
+        for ch in his:
+            fill(ch)
         h2t = a.at[0:D, 0:1664]
         transpose_rows(h2, h2t)
 
-        def w1rows(t, _):
-            r0 = pl.multiple_of(t * 256, 256)
-            v = dot(h2t[:, 0:ROWS], du[:, pl.ds(r0, 256)])
-            for c in range(2):
-                put_block(fs, R_W1 - first + 2 * t + c, 16, v[:, c * 128:(c + 1) * 128])
-            return 0
-        lax.fori_loop(0, HID // 256, w1rows, 0)
-        hi.start2()
+        lane = lax.broadcasted_iota(jnp.int32, (D, 128), 1)
+        at = R_W1 - first
+        keep = fs[pl.ds(at, 1), :]
+
+        def w1rows(t, before):
+            r0 = pl.multiple_of(t * 512, 512)
+            u = dot(h2t[:, 0:ROWS], du[:, pl.ds(r0, 512)])
+            v = shifted([u[:, c * 128:(c + 1) * 128] for c in range(4)])
+            for c in range(4):
+                fs[pl.ds(at + 4 * t + c, D, stride=16), :] = jnp.where(lane >= LANE, v[c], before if c == 0 else v[c - 1])
+            return v[3]
+        v = lax.fori_loop(0, HID // 512, w1rows, jnp.zeros((D, 128), F32))
+        one = lax.broadcasted_iota(jnp.int32, (1, 128), 1)
+        v = jnp.where(lax.broadcasted_iota(jnp.int32, (D, 128), 0) == 0, keep, pltpu.roll(v, 1, 0)), v[D - 1:D]
+        fs[pl.ds(at, D, stride=16), :] = jnp.where(lane < LANE, v[0], fs[pl.ds(at, D, stride=16), :])
+        fs[pl.ds(at + D * 16, 1), :] = jnp.where(one < LANE, v[1], fs[pl.ds(at + D * 16, 1), :])
+        run(each(his, 'start2'))
         v = dot_tn(ob[...], dx1[...].reshape(ROWS, D).astype(BF16))
-        for c in range(4):
-            put_block(fs, R_PROJ - first + c, 4, v[:, c * 128:(c + 1) * 128])
+        put_tile(fs, R_PROJ - first, 4, [v[:, c * 128:(c + 1) * 128] for c in range(4)])
         for row, n in ((R_BP, 3), (R_G2, 1), (R_B2, 2)):
             put_vec(fs, row - first, vg[n:n + 1])
         for j in range(4):
             put_vec(fs, R_C1 - first + 4 * j, vg[4 + j:5 + j])
-        fill(lo)
-        lo.start1()
+        for ch in los:
+            fill(ch)
         for cp in ycs:
             cp.wait()
 
@@ -895,7 +957,7 @@
         lax.fori_loop(0, 4, rows0, 0)
         ins[0].wait()
         ins[1].wait()
-        lo.start2()
+        run(each(his, 'halve') + each(los, 'start2'))
         heads = lane_head()
 
         def several(g, items):
@@ -919,16 +981,17 @@
                 put_rows(fs, RS + base, dk)
                 put_rows(fs, base, diag_sum(dqv, heads) * SCALE)
 
-        mid = {0: (hi.start3,), 1: (ac[0].start2,), 2: (ac[1].start2, hi.start4), 3: (ac[2].start2,)}
+        mid = {0: each(his, 'start3'), 1: each(mids, 'halve') + (ac[0].start2,), 2: each(last, 'halve') + (ac[1].start2,) + each(his, 'start4'),
+               3: each(mids, 'start3') + (ac[0].halve, ac[2].start2)}
         for g in range(4):
             def attend(t, _):
-                @pl.when(t == 4)
+                @pl.when(t == 1)
                 def _():
                     for f in mid[g]:
                         f()
-                several(g, [4 * t + n for n in range(4)])
+                several(g, [16 * t + n for n in range(16)])
                 return 0
-            lax.fori_loop(0, WB // 4, attend, 0)
+            lax.fori_loop(0, WB // 16, attend, 0)
             parts = []
             for n in range(3):
                 v = fs[n * RS:n * RS + ROWS, :]
@@ -947,13 +1010,15 @@
                 for p in range(pn.ndp):
                     ac[g].src[p & 1, p >> 1, n * mu:(n + 1) * mu] = u[p * mu:(p + 1) * mu]
             ac[g].start1()
+        run(each(last, 'start3'))
         for cp in cps:
             cp.wait()
         gain = vec[0:1, :]
         tab = table_grad(rel_ref, os_, dtab)
         for n in range(3):
             small.own[2 + n] = tab[8 * n:8 * n + 8].astype(BF16)
-        late = {1: (lo.start3, ac[3].start2), 2: (ac[0].start3, hi.start5), 3: (ac[1].start3,), 4: (ac[2].start3,), 5: (ac[3].start3, ac[0].start4), 6: (ac[1].start4,)}
+        late = {0: (ac[0].start3,), 1: (ac[3].start2, ac[1].halve), 2: (ac[1].start3, ac[2].halve) + each(his, 'start5'), 3: each(mids, 'start4') + (ac[3].halve,),
+                4: (ac[2].start3,), 5: (ac[3].start3, ac[0].start4), 6: (ac[1].start4,) + each(mids, 'start5')}
 
         def rows1(t, _):
             for k, fns in late.items():
@@ -980,22 +1045,19 @@
         ycs = window_copies(dx_hbm, dx1, xsem, False)
         for cp in ycs:
             cp.start()
-        for f in (lo.start4, ac[2].start4, ac[3].start4, ac[0].start5, ac[1].start5, small.start2, lo.start5, ac[2].start5, ac[3].start5):
-            f()
+        run(each(last, 'start4') + (ac[2].start4, ac[3].start4, ac[0].start5, ac[1].start5, small.start2) + each(last, 'start5') + (ac[2].start5, ac[3].start5))
         for ch in chunks:
             ch.finish()
         r, c, z = place()
         g = os_
 
-        def scattered(ch):
-            @pl.when(ch.here(z))
-            def _():
-                def piece(p, _):
-                    g[pl.ds(pl.multiple_of(p * pn.pc * 8, 8), pn.pc * 8), :] = ch.ag[p & 1, lax.shift_right_arithmetic(p, 1)].astype(F32).reshape(pn.pc * 8, 128)
-                    return 0
-                lax.fori_loop(0, pn.ndp, piece, 0)
-        scattered(hi)
-        scattered(lo)
+        @pl.when(z >= pn.ka)
+        def _():
+            def piece(p, _):
+                for ch in shards[:2]:
+                    g[pl.ds(pl.multiple_of((p * pn.pc + ch.at) * 8, 8), ch.n * 8), :] = ch.ag[p & 1, lax.shift_right_arithmetic(p, 1)].astype(F32).reshape(ch.n * 8, 128)
+                return 0
+            lax.fori_loop(0, pn.ndp, piece, 0)
         mu = pn.mrow // 8
 
         @pl.when(z < pn.ka)
@@ -1032,7 +1094,11 @@
 
 def part_list(pn):
     mu = 3 * pn.mrow // 8
-    return [(pn.kh, pn.ns, True, pn.pc), (pn.ka, pn.kh, True, pn.pc)] + [(0, pn.ka, False, mu)] * 4
+    h = (pn.pc + 1) // 2
+    out = []
+    for k in range(pn.ns - 1, pn.ka - 1, -1):
+        out += [(k, k + 1, h, 0, False), (k, k + 1, pn.pc - h, h, True)]
+    return out + [(0, pn.ka, mu, 0, g % 2 == 1) for g in range(4)]
 
 
 def call_bc(pn, x, cot, ob, wp, w1, w2, hwt, qkv, p, wqkv, vec, rel, counts):
@@ -1041,8 +1107,8 @@
     sds = jax.ShapeDtypeStruct
     outs = [sds((14, 14, 8, D), BF16), sds((14, 14, 8, D), F32), sds((pn.units * 8, 128), F32)]
     scratch = [pltpu.VMEM((28, 7, 8, D), F32), pltpu.VMEM((D, D), BF16), pltpu.VMEM((64, D), F32), pltpu.SemaphoreType.DMA((4,))]
-    for n, (k0, k1, scatter, m) in enumerate(part_list(pn)):
-        scratch += Chunk.scratch(pn, m, k1 - k0 if scatter else 1, n == 1)
+    for n, (k0, k1, m, at, flip) in enumerate(part_list(pn)):
+        scratch += Chunk.scratch(pn, m, 1 < n < 2 * (pn.ns - pn.ka))
     scratch += Small.scratch(pn)
     return pl.pallas_call(
         functools.partial(kernel_bc, pn),
@@ -1058,7 +1124,7 @@
 STEP = 2
 DECAYED = (2, 6, 10, 12)
 LENGTHS = [D, D, 3 * D * D, D, D, TAB * HEADS, D * D, D, D, D, D * HID, HID, HID * D, D]
-AU = 64
+AU = 128
 
 
 def kernel_adam(rates, first, g, p, m1, m2, g_o, p_o, m_o, v_o):

time: 194 us -> 180 us (0.928)
  Pallas kernels: 186 us -> 172 us
    pallas_call x1, Pallas kernels: 112 us -> 104 us  [call_bc(): pl.pallas_call(functools.partial(kernel_bc, pn), out_shape=outs, in_specs...]
    pallas_call x1, Pallas kernels: 59.4 us -> 55.2 us  [call_a(): pl.pallas_call(functools.partial(kernel_a, pn), out_shape=outs, in_specs=...]
    pallas_call x1, Pallas kernels: 15.1 us -> 12.8 us  [call_adam(): pl.pallas_call(kernel_adam, grid=(pl.cdiv(pn.units, AU),), out_shape=[jax...]
where the time goes in v5:
time: 180 us; the launch traced here: 179 us
  Pallas kernels  172 us (96%)
  local copies, waits for them, and re-layouts  6.07 us (3%)
    pallas_call x1, Pallas kernels, call_bc(): pl.pallas_call(functools.partial(kernel_bc, pn), out_shape=outs, in_specs...  104 us
    pallas_call x1, Pallas kernels, call_a(): pl.pallas_call(functools.partial(kernel_a, pn), out_shape=outs, in_specs=...  55.2 us
    pallas_call x1, Pallas kernels, call_adam(): pl.pallas_call(kernel_adam, grid=(pl.cdiv(pn.units, AU),), out_shape=[jax...  12.8 us
    unnamed x5, local copies, waits for them, and re-layouts  5.36 us

profile of v5, /device:TPU:0, one launch (start us, length us, event | category | flops | bytes accessed | tf_op | source)
XLA Modules:
  0.0 179.4 jit_solution(10160866720554893418)
XLA Ops:
  0.6 0.8 copy.15
  1.5 0.7 reshape.77.rel_ref
  2.2 55.2 %attend.1 = (bf16[512,1536]{1,0:T(8,128)(2,1)}, bf16[512,512]{1,0:T(8,128)(2,1)}, bf16[512,2048]{1,0:T(8,128)(2,1)}, bf16[2048,512]{1,0:T(8,128)(2,1)}, f32[16,5...) custom-call(bf16[14,14,8,512]{3,2,1,0:T(8,128)(2,1)} %bitcast.17, ...), custom_call_target="tpu_custom_call" | custom-call | tf_op jit(solution)/shard_map/attend/pallas_call | solution.py:485
  58.0 104.0 %back.1 = (bf16[14,14,8,512]{3,2,1,0:T(8,128)(2,1)}, f32[14,14,8,512]{3,2,1,0:T(8,128)}, f32[6168,128]{1,0:T(8,128)}) custom-call(bf16[14,14,8,512]{3,2,1,0:T(8,128)(2,1)} %bitcast.18, bf16[14,14,8,512]{3,2,1,0:T(8,128)(2,1)} %bitcast.23, bf16[1568,512]{1,0:T(8,128)(2,1)} %get-tuple-element.34.ob_hbm, bf16[512,512]{1,0:T(8,128)(2,1)} %get-tuple-element.35.wp_hbm, ...), custom_call_target="tpu_custom_call" | custom-call | tf_op jit(solution)/shard_map/back/pallas_call | solution.py:1113
  162.0 12.8 %adamw.1 = (f32[771,8,128]{2,1,0:T(8,128)}, f32[771,8,128]{2,1,0:T(8,128)}, f32[771,8,128]{2,1,0:T(8,128)}, f32[771,8,128]{2,1,0:T(8,128)}) custom-call(f32[15]{0:T(128)} %rates.1, s32[1]{0:T(128)} %bitcast.6.first, f32[771,8,128]{2,1,0:T(8,128)} %bitcast.22, f32[771,8,128]{2,1,0:T(8,128)} %bitcast.16, f32[771,8,128]{2,1,0:T(8,128)} %bitcast.20, ...), custom_call_target="tpu_custom_call" | custom-call | tf_op jit(solution)/shard_map/adamw/pallas_call | solution.py:1180
  174.8 0.0 copy-start
  174.9 2.8 %copy.19 = bf16[8,14,14,512]{3,0,2,1:T(8,128)(2,1)} copy(bf16[8,14,14,512]{3,0,2,1:T(8,128)(2,1)} %bitcast.24) | data formatting | bytes 3211264
  177.7 0.0 copy-done
  177.7 1.7 copy.20
  (1 shorter events, 0.0 us)
Async XLA Ops:
  174.8 2.8 %copy-start = (f32[14,14,8,512]{3,2,1,0:T(8,128)S(1)}, f32[14,14,8,512]{3,2,1,0:T(8,128)}, u32[]{:S(2)}) copy-start(f32[14,14,8,512]{3,2,1,0:T(8,128)} %get-tuple-element.44) | copy-start | bytes 9633796

commit v6 on v5

--- a/solution.py
+++ b/solution.py
@@ -23,6 +23,7 @@
 RS = ROWS + 64
 BLK = 224
 NBLK = ROWS // BLK
+BM = 784
 WB = 4 * IMGS
 SCALE = HEAD_DIM ** -0.5
 
@@ -273,15 +274,10 @@
         own = self.wb.at[s, c, :, self.parts[h]]
         return remote(own, own, self.ysem, 2 * s + h, peer(r, 1 - c))
 
-    def start(self, first):
-        r, c, z = place()
+    def start(self):
         for h in range(2):
             for j in range(1, self.pn.ns):
-                soon = (z < self.pn.ka) | (z + j >= self.pn.ns)
-
-                @pl.when(soon if first else jnp.logical_not(soon))
-                def _():
-                    self.o(j, h).start()
+                self.o(j, h).start()
 
     def spread(self, s, h):
         r, c, z = place()
@@ -339,7 +335,7 @@
         flat_v[z, p & 1, lax.shift_right_arithmetic(p, 1)] = fs[pl.ds(pl.multiple_of(p * pn.pc * 8, 8), pn.pc * 8), :].reshape(pn.pc, 8, 128).astype(BF16)
     me = lax.axis_index("dp")
     cast(me)
-    gather.start(True)
+    gather.start()
 
     def others(j, _):
         cast(lax.rem(me + j, pn.ndp))
@@ -348,7 +344,6 @@
     for h in range(2):
         for k in range(pn.ka):
             gather.spread(k, h)
-    gather.start(False)
     for h in range(2):
         for k in range(pn.ka):
             gather.pair(k, h)
@@ -372,27 +367,31 @@
     bv = vec[3:4, :]
 
     def rows(t, _):
-        @pl.when(t == 2)
+        @pl.when(t == 0)
+        def _():
+            for k in range(pn.ka + 1, pn.ns):
+                for h in range(2):
+                    gather.spread(k, h)
+
+        @pl.when(t == 1)
         def _():
             for h in range(2):
                 gather.pair(pn.ka, h)
-            for k in range(pn.ka + 1, pn.ns):
-                for h in range(2):
-                    gather.spread(k, h)
-        r0 = pl.multiple_of(t * BLK, BLK)
-        x = x_v[pl.ds(4 * t, 4)].reshape(BLK, D).astype(F32)
+        r0 = pl.multiple_of(t * BM, BM)
+        x = x_v[pl.ds(BM // 56 * t, BM // 56)].reshape(BM, D).astype(F32)
         xhat, _r = norm_stats(x)
         h = (xhat * gain + shift).astype(BF16)
-        hw[pl.ds(r0, BLK), :] = h
-        for c in range(12):
-            y = dot(h, wqkv[:, c * 128:(c + 1) * 128])
-            if c < 4:
-                y = (y + bq[:, c * 128:(c + 1) * 128]) * SCALE
-            if c >= 8:
-                y = y + bv[:, (c - 8) * 128:(c - 7) * 128]
-            fs[pl.ds(c * RS + r0, BLK), :] = y
+        hw[pl.ds(r0, BM), :] = h
+        for n in range(3):
+            y = dot(h, wqkv[:, n * D:(n + 1) * D])
+            if n == 0:
+                y = (y + bq) * SCALE
+            if n == 2:
+                y = y + bv
+            for c in range(4):
+                fs[pl.ds((4 * n + c) * RS + r0, BM), :] = y[:, c * 128:(c + 1) * 128]
         return 0
-    lax.fori_loop(0, NBLK, rows, 0)
+    lax.fori_loop(0, ROWS // BM, rows, 0)
     gather.ready(pn.ka)
     tab = []
     for u in range(R_TAB // 8, R_TAB // 8 + 3):
@@ -784,7 +783,6 @@
         return v.astype(BF16).astype(F32)
 
 
-BM = 784
 NSEMS = 32
 
 
@@ -1010,15 +1008,15 @@
                 for p in range(pn.ndp):
                     ac[g].src[p & 1, p >> 1, n * mu:(n + 1) * mu] = u[p * mu:(p + 1) * mu]
             ac[g].start1()
-        run(each(last, 'start3'))
+        run(each(last, 'start3') + (ac[0].start3, ac[1].halve))
         for cp in cps:
             cp.wait()
         gain = vec[0:1, :]
         tab = table_grad(rel_ref, os_, dtab)
         for n in range(3):
             small.own[2 + n] = tab[8 * n:8 * n + 8].astype(BF16)
-        late = {0: (ac[0].start3,), 1: (ac[3].start2, ac[1].halve), 2: (ac[1].start3, ac[2].halve) + each(his, 'start5'), 3: each(mids, 'start4') + (ac[3].halve,),
-                4: (ac[2].start3,), 5: (ac[3].start3, ac[0].start4), 6: (ac[1].start4,) + each(mids, 'start5')}
+        late = {0: (ac[3].start2,), 1: (ac[1].start3, ac[2].halve), 2: (ac[3].halve,) + each(his, 'start5'), 3: each(mids, 'start4') + (ac[2].start3,),
+                4: (ac[0].start4, ac[3].start3), 5: each(last, 'start4'), 6: (ac[1].start4,) + each(mids, 'start5')}
 
         def rows1(t, _):
             for k, fns in late.items():
@@ -1045,8 +1043,8 @@
         ycs = window_copies(dx_hbm, dx1, xsem, False)
         for cp in ycs:
             cp.start()
-        run(each(last, 'start4') + (ac[2].start4, ac[3].start4, ac[0].start5, ac[1].start5, small.start2) + each(last, 'start5') + (ac[2].start5, ac[3].start5))
-        for ch in chunks:
+        run((ac[2].start4, ac[3].start4, ac[0].start5, ac[1].start5, small.start2) + each(last, 'start5') + (ac[2].start5, ac[3].start5))
+        for ch in shards:
             ch.finish()
         r, c, z = place()
         g = os_
@@ -1060,15 +1058,17 @@
             lax.fori_loop(0, pn.ndp, piece, 0)
         mu = pn.mrow // 8
 
-        @pl.when(z < pn.ka)
-        def _():
-            def piece(p, _):
-                for h in range(4):
+        for h in range(4):
+            ac[h].finish()
+
+            @pl.when(z < pn.ka)
+            def _():
+                def piece(p, _):
                     for n in range(3):
                         v = ac[h].ag[p & 1, lax.shift_right_arithmetic(p, 1), n * mu:(n + 1) * mu].astype(F32).reshape(pn.mrow, 128)
                         g[pl.ds(R_QKV + p * pn.mrow * 12 + n * 4 + h, pn.mrow, stride=12), :] = v
-                return 0
-            lax.fori_loop(0, pn.ndp, piece, 0)
+                    return 0
+                lax.fori_loop(0, pn.ndp, piece, 0)
         small.finish()
 
         @pl.when(z < pn.ka)

time: 180 us -> 177 us (0.983)
  Pallas kernels: 172 us -> 170 us
    pallas_call x1, Pallas kernels: 104 us -> 102 us  [call_bc(): pl.pallas_call(functools.partial(kernel_bc, pn), out_shape=outs, in_specs...]
where the time goes in v6:
time: 177 us
  Pallas kernels  170 us (96%)
  local copies, waits for them, and re-layouts  6.07 us (3%)
    pallas_call x1, Pallas kernels, call_bc(): pl.pallas_call(functools.partial(kernel_bc, pn), out_shape=outs, in_specs...  102 us
    pallas_call x1, Pallas kernels, call_a(): pl.pallas_call(functools.partial(kernel_a, pn), out_shape=outs, in_specs=...  55.3 us
    pallas_call x1, Pallas kernels, call_adam(): pl.pallas_call(kernel_adam, grid=(pl.cdiv(pn.units, AU),), out_shape=[jax...  12.8 us
    unnamed x5, local copies, waits for them, and re-layouts  5.36 us

profile of v6, /device:TPU:0, one launch (start us, length us, event | category | flops | bytes accessed | tf_op | source)
XLA Modules:
  0.0 177.1 jit_solution(7756325247565354424)
XLA Ops:
  0.6 0.8 copy.15
  1.5 0.7 reshape.77.rel_ref
  2.2 55.3 %attend.1 = (bf16[512,1536]{1,0:T(8,128)(2,1)}, bf16[512,512]{1,0:T(8,128)(2,1)}, bf16[512,2048]{1,0:T(8,128)(2,1)}, bf16[2048,512]{1,0:T(8,128)(2,1)}, f32[16,5...) custom-call(bf16[14,14,8,512]{3,2,1,0:T(8,128)(2,1)} %bitcast.17, ...), custom_call_target="tpu_custom_call" | custom-call | tf_op jit(solution)/shard_map/attend/pallas_call | solution.py:484
  58.1 101.6 %back.1 = (bf16[14,14,8,512]{3,2,1,0:T(8,128)(2,1)}, f32[14,14,8,512]{3,2,1,0:T(8,128)}, f32[6168,128]{1,0:T(8,128)}) custom-call(bf16[14,14,8,512]{3,2,1,0:T(8,128)(2,1)} %bitcast.18, bf16[14,14,8,512]{3,2,1,0:T(8,128)(2,1)} %bitcast.23, bf16[1568,512]{1,0:T(8,128)(2,1)} %get-tuple-element.34.ob_hbm, bf16[512,512]{1,0:T(8,128)(2,1)} %get-tuple-element.35.wp_hbm, ...), custom_call_target="tpu_custom_call" | custom-call | tf_op jit(solution)/shard_map/back/pallas_call | solution.py:1113
  159.7 12.8 %adamw.1 = (f32[771,8,128]{2,1,0:T(8,128)}, f32[771,8,128]{2,1,0:T(8,128)}, f32[771,8,128]{2,1,0:T(8,128)}, f32[771,8,128]{2,1,0:T(8,128)}) custom-call(f32[15]{0:T(128)} %rates.1, s32[1]{0:T(128)} %bitcast.6.first, f32[771,8,128]{2,1,0:T(8,128)} %bitcast.22, f32[771,8,128]{2,1,0:T(8,128)} %bitcast.16, f32[771,8,128]{2,1,0:T(8,128)} %bitcast.20, ...), custom_call_target="tpu_custom_call" | custom-call | tf_op jit(solution)/shard_map/adamw/pallas_call | solution.py:1180
  172.5 0.0 copy-start
  172.6 2.8 %copy.19 = bf16[8,14,14,512]{3,0,2,1:T(8,128)(2,1)} copy(bf16[8,14,14,512]{3,0,2,1:T(8,128)(2,1)} %bitcast.24) | data formatting | bytes 3211264
  175.4 0.0 copy-done
  175.4 1.7 copy.20
  (1 shorter events, 0.0 us)
Async XLA Ops:
  172.5 2.8 %copy-start = (f32[14,14,8,512]{3,2,1,0:T(8,128)S(1)}, f32[14,14,8,512]{3,2,1,0:T(8,128)}, u32[]{:S(2)}) copy-start(f32[14,14,8,512]{3,2,1,0:T(8,128)} %get-tuple-element.44) | copy-start | bytes 9633796

commit v7 on v6

--- a/solution.py
+++ b/solution.py
@@ -1124,7 +1124,7 @@
 STEP = 2
 DECAYED = (2, 6, 10, 12)
 LENGTHS = [D, D, 3 * D * D, D, D, TAB * HEADS, D * D, D, D, D, D * HID, HID, HID * D, D]
-AU = 128
+AU = 129
 
 
 def kernel_adam(rates, first, g, p, m1, m2, g_o, p_o, m_o, v_o):

time: 177 us -> 177 us (level)
  no operation moved by 1% of the time
where the time goes in v7:
time: 177 us
  Pallas kernels  169 us (95%)
  local copies, waits for them, and re-layouts  6.07 us (3%)
    pallas_call x1, Pallas kernels, call_bc(): pl.pallas_call(functools.partial(kernel_bc, pn), out_shape=outs, in_specs...  102 us
    pallas_call x1, Pallas kernels, call_a(): pl.pallas_call(functools.partial(kernel_a, pn), out_shape=outs, in_specs=...  55.3 us
    pallas_call x1, Pallas kernels, call_adam(): pl.pallas_call(kernel_adam, grid=(pl.cdiv(pn.units, AU),), out_shape=[jax...  12.4 us
    unnamed x5, local copies, waits for them, and re-layouts  5.36 us

profile of v7, /device:TPU:0, one launch (start us, length us, event | category | flops | bytes accessed | tf_op | source)
XLA Modules:
  0.0 176.7 jit_solution(17519521038399191671)
XLA Ops:
  0.6 0.8 copy.15
  1.5 0.7 reshape.77.rel_ref
  2.2 55.3 %attend.1 = (bf16[512,1536]{1,0:T(8,128)(2,1)}, bf16[512,512]{1,0:T(8,128)(2,1)}, bf16[512,2048]{1,0:T(8,128)(2,1)}, bf16[2048,512]{1,0:T(8,128)(2,1)}, f32[16,5...) custom-call(bf16[14,14,8,512]{3,2,1,0:T(8,128)(2,1)} %bitcast.17, ...), custom_call_target="tpu_custom_call" | custom-call | tf_op jit(solution)/shard_map/attend/pallas_call | solution.py:484
  58.1 101.6 %back.1 = (bf16[14,14,8,512]{3,2,1,0:T(8,128)(2,1)}, f32[14,14,8,512]{3,2,1,0:T(8,128)}, f32[6168,128]{1,0:T(8,128)}) custom-call(bf16[14,14,8,512]{3,2,1,0:T(8,128)(2,1)} %bitcast.18, bf16[14,14,8,512]{3,2,1,0:T(8,128)(2,1)} %bitcast.23, bf16[1568,512]{1,0:T(8,128)(2,1)} %get-tuple-element.34.ob_hbm, bf16[512,512]{1,0:T(8,128)(2,1)} %get-tuple-element.35.wp_hbm, ...), custom_call_target="tpu_custom_call" | custom-call | tf_op jit(solution)/shard_map/back/pallas_call | solution.py:1113
  159.7 12.4 %adamw.1 = (f32[771,8,128]{2,1,0:T(8,128)}, f32[771,8,128]{2,1,0:T(8,128)}, f32[771,8,128]{2,1,0:T(8,128)}, f32[771,8,128]{2,1,0:T(8,128)}) custom-call(f32[15]{0:T(128)} %rates.1, s32[1]{0:T(128)} %bitcast.6.first, f32[771,8,128]{2,1,0:T(8,128)} %bitcast.22, f32[771,8,128]{2,1,0:T(8,128)} %bitcast.16, f32[771,8,128]{2,1,0:T(8,128)} %bitcast.20, ...), custom_call_target="tpu_custom_call" | custom-call | tf_op jit(solution)/shard_map/adamw/pallas_call | solution.py:1180
  172.2 0.0 copy-start
  172.2 2.8 %copy.19 = bf16[8,14,14,512]{3,0,2,1:T(8,128)(2,1)} copy(bf16[8,14,14,512]{3,0,2,1:T(8,128)(2,1)} %bitcast.24) | data formatting | bytes 3211264
  175.0 0.0 copy-done
  175.0 1.7 copy.20
  (1 shorter events, 0.0 us)
Async XLA Ops:
  172.2 2.8 %copy-start = (f32[14,14,8,512]{3,2,1,0:T(8,128)S(1)}, f32[14,14,8,512]{3,2,1,0:T(8,128)}, u32[]{:S(2)}) copy-start(f32[14,14,8,512]{3,2,1,0:T(8,128)} %get-tuple-element.44) | copy-start | bytes 9633796
